TPU v7x, 32 devices: a whole 2x2x4 slice. The times are simulated.
32 devices in a mesh: ctx: 8 (over z, x), fsdp: 4 (over y, core).
Axes of the slice: x: 2, y: 2, z: 4, core: 2. Of those that a mesh axis runs over, the one named last changes fastest.
Arguments:
- tokens: bfloat16 [8, 2, 256, 1536], P('ctx', None, 'fsdp'), may hold values from -6 to 6
- pairing: int32 [8], replicated, may hold values from 0 to 7, each once
- gain_attn: bfloat16 [1536], P('fsdp'), may hold values from 0.099609375 to 1.8984375
- w_qkv: bfloat16 [1536, 2048], P('fsdp'), may hold values from -0.15625 to 0.15625
- b_qkv: bfloat16 [2048], P('fsdp'), may hold values from -10 to 10
- w_out: bfloat16 [1536, 1536], P('fsdp'), may hold values from -0.625 to 0.625
- gain_mlp: bfloat16 [1536], P('fsdp'), may hold values from 0.099609375 to 1.8984375
- w_gate_up: bfloat16 [1536, 2, 4480], P('fsdp'), may hold values from -0.15625 to 0.15625
- w_down: bfloat16 [4480, 1536], P('fsdp'), may hold values from -0.09375 to 0.09375
- cotangent: bfloat16 [8, 2, 256, 1536], P('ctx', None, 'fsdp'), may hold values from -6 to 6
Outputs:
- block_output: bfloat16 [8, 2, 256, 1536], P('ctx', None, 'fsdp')
- d_tokens: float32 [8, 2, 256, 1536], P('ctx', None, 'fsdp')
- d_gain_attn: float32 [1536], P('fsdp')
- d_w_qkv: float32 [1536, 2048], P('fsdp')
- d_b_qkv: float32 [2048], P('fsdp')
- d_w_out: float32 [1536, 1536], P('fsdp')
- d_gain_mlp: float32 [1536], P('fsdp')
- d_w_gate_up: float32 [1536, 2, 4480], P('fsdp')
- d_w_down: float32 [4480, 1536], P('fsdp')
Inputs may be any that keep to these rules, and one draw needn't show every extreme that they name: Each index of ctx holds stretches pairing[c] and 2 * 8 - 1 - pairing[c] of the sequence.
All inputs are finite; a program needn't handle non-finite values.
Results may differ from a plain program's by a relative error of at most 0.02.
The roundings to bfloat16 on the way count: a program that leaves them out, or rounds other values in their place, can miss the bound.
Values may be sent and summed in bfloat16 or wider, within the bound.
A program may use at most 384 MiB of HBM per device.

v0:
```python
import jax
import jax.numpy as jnp
from jax import lax
from jax.sharding import PartitionSpec as P

D = 1536
HEADS = 12
KV_HEADS = 2
HEAD_DIM = 128


eps = 1e-06
rope_base = 1000000.0


def rope_tables(position):
    half = HEAD_DIM // 2
    inverse = rope_base ** (-(jnp.arange(half, dtype=jnp.float32) * 2.0 / HEAD_DIM))
    angle = position.astype(jnp.float32)[:, None] * inverse[None, :]
    return (jnp.cos(angle)[:, None, :], jnp.sin(angle)[:, None, :])


def rotate(vectors, cosines, sines):
    half = HEAD_DIM // 2
    first, second = (vectors[..., :half], vectors[..., half:])
    return jnp.concatenate([first * cosines - second * sines, second * cosines + first * sines], -1)


def unrotate(grads, cosines, sines):
    half = HEAD_DIM // 2
    first, second = (grads[..., :half], grads[..., half:])
    return jnp.concatenate([first * cosines + second * sines, second * cosines - first * sines], -1)


def rms_scale(values):
    return lax.rsqrt(jnp.mean(values * values, -1, keepdims=True) + eps)


def rms_backward(values, scale_rows, gain, d_normed):
    d_gain = jnp.sum(d_normed * values * scale_rows, 0)
    d_inner = d_normed * gain
    d_values = scale_rows * d_inner - values * scale_rows**3 * jnp.mean(
        d_inner * values, -1, keepdims=True
    )
    return (d_values, d_gain)


def contract_rows(left, right):
    return lax.dot_general(
        left, right, (((0,), (0,)), ((), ())), preferred_element_type=jnp.float32
    )


def contract_cols(left, right):
    return lax.dot_general(
        left, right, (((1,), (1,)), ((), ())), preferred_element_type=jnp.float32
    )


def body(tokens, pairing, gain_attn, w_qkv, b_qkv, w_out, gain_mlp, w_gate_up, w_down, cotangent):
    f32 = jnp.float32
    bf16 = jnp.bfloat16
    half_rows = tokens.shape[2]
    n_ctx = lax.axis_size("ctx")
    n_fsdp = lax.axis_size("fsdp")
    ctx_index = lax.axis_index("ctx")
    fsdp_index = lax.axis_index("fsdp")
    stretch_len = half_rows * n_fsdp
    everyone = n_ctx * n_fsdp
    sequence = 2 * n_ctx * stretch_len
    local_count = 2 * half_rows
    q_width = HEADS * HEAD_DIM
    kv_width = KV_HEADS * HEAD_DIM
    per_group = HEADS // KV_HEADS
    softmax_scale = HEAD_DIM ** (-0.5)
    owner_range = jnp.arange(n_ctx, dtype=jnp.int32)
    own_first = jnp.sum(jnp.where(owner_range == ctx_index, pairing, 0))
    own_second = 2 * n_ctx - 1 - own_first
    inverse_pair = jnp.sum(
        owner_range[:, None] * (pairing[:, None] == owner_range[None, :]).astype(jnp.int32), 0
    )
    offsets = fsdp_index * half_rows + jnp.arange(half_rows, dtype=jnp.int32)
    own_pos = jnp.concatenate(
        [own_first * stretch_len + offsets, own_second * stretch_len + offsets]
    )
    gain_one_w, w_qkv_full, b_qkv_full, w_out_full = (
        lax.all_gather(gain_attn, "fsdp", axis=0, tiled=True),
        lax.all_gather(w_qkv, "fsdp", axis=0, tiled=True),
        lax.all_gather(b_qkv, "fsdp", axis=0, tiled=True),
        lax.all_gather(w_out, "fsdp", axis=0, tiled=True),
    )
    gain_one = gain_one_w.astype(f32)
    inputs = tokens.reshape(local_count, D).astype(f32)
    scale_one = rms_scale(inputs)
    normed1 = (inputs * scale_one * gain_one).astype(bf16)
    qkv = jnp.dot(normed1, w_qkv_full, preferred_element_type=f32) + b_qkv_full.astype(f32)
    cosines, sines = rope_tables(own_pos)
    query16 = rotate(qkv[:, :q_width].reshape(local_count, HEADS, HEAD_DIM), cosines, sines).astype(
        bf16
    )
    key16 = rotate(
        qkv[:, q_width : q_width + kv_width].reshape(local_count, KV_HEADS, HEAD_DIM),
        cosines,
        sines,
    ).astype(bf16)
    value16 = qkv[:, q_width + kv_width :].astype(bf16)
    keys_gathered, values_gathered = (
        lax.all_gather(key16.reshape(2, half_rows, kv_width), ("ctx", "fsdp"), axis=1, tiled=True),
        lax.all_gather(
            value16.reshape(2, half_rows, kv_width), ("ctx", "fsdp"), axis=1, tiled=True
        ),
    )

    def by_position(gathered):
        laid = gathered.reshape(2, n_ctx, stretch_len, kv_width)
        ordered = jnp.concatenate(
            [
                jnp.take(laid[0], inverse_pair, axis=0),
                jnp.take(laid[1], inverse_pair[::-1], axis=0),
            ],
            0,
        )
        return ordered.reshape(sequence, KV_HEADS, HEAD_DIM)

    keys_sorted = by_position(keys_gathered)
    values_sorted = by_position(values_gathered)
    query_halves = query16.reshape(2, half_rows, KV_HEADS, per_group, HEAD_DIM)
    pos_halves = own_pos.reshape(2, half_rows)
    stretch_ids = (own_first, own_second)
    key_iota = jnp.arange(stretch_len, dtype=jnp.int32)

    def masked_scores(query_half, pos_half, key_block, start):
        scores = (
            jnp.einsum("tkgd,skd->kgts", query_half, key_block, preferred_element_type=f32)
            * softmax_scale
        )
        visible = (start + key_iota)[None, None, None, :] <= pos_half[None, None, :, None]
        return (jnp.where(visible, scores, -1e30), visible)

    lse_parts = []
    att_parts = []
    for which in range(2):
        forward_query_half = query_halves[which]
        forward_pos_half = pos_halves[which]
        forward_stretch_id = stretch_ids[which]

        def stat_step(block, carry):
            running_max, totals = carry
            start = block * stretch_len
            key_block = lax.dynamic_slice_in_dim(keys_sorted, start, stretch_len, 0)
            scores, visible = masked_scores(forward_query_half, forward_pos_half, key_block, start)
            new_max = jnp.maximum(running_max, jnp.max(scores, -1))
            weights = jnp.where(visible, jnp.exp(scores - new_max[..., None]), 0.0)
            totals = totals * jnp.exp(running_max - new_max) + jnp.sum(weights, -1)
            return (new_max, totals)

        start_max = jnp.full((KV_HEADS, per_group, half_rows), -1e30, f32)
        start_tot = jnp.zeros((KV_HEADS, per_group, half_rows), f32)
        running_max, totals = lax.fori_loop(
            0, forward_stretch_id + 1, stat_step, (start_max, start_tot)
        )
        lse_half = running_max + jnp.log(totals)

        def value_step(block, accumulated):
            start = block * stretch_len
            key_block = lax.dynamic_slice_in_dim(keys_sorted, start, stretch_len, 0)
            value_block = lax.dynamic_slice_in_dim(values_sorted, start, stretch_len, 0)
            scores, visible = masked_scores(forward_query_half, forward_pos_half, key_block, start)
            probs16 = jnp.where(visible, jnp.exp(scores - lse_half[..., None]), 0.0).astype(bf16)
            return accumulated + jnp.einsum(
                "kgts,skd->kgtd", probs16, value_block, preferred_element_type=f32
            )

        start_acc = jnp.zeros((KV_HEADS, per_group, half_rows, HEAD_DIM), f32)
        accumulated = lax.fori_loop(0, forward_stretch_id + 1, value_step, start_acc)
        lse_half, accumulated = (lse_half, accumulated)
        lse_parts.append(lse_half)
        att_parts.append(accumulated)
    attended = jnp.concatenate(att_parts, 2)
    attended16 = attended.transpose(2, 0, 1, 3).reshape(local_count, q_width).astype(bf16)
    hidden = inputs + jnp.dot(attended16, w_out_full, preferred_element_type=f32)
    gain_two_w, w_gu_full, w_down_full = (
        lax.all_gather(gain_mlp, "fsdp", axis=0, tiled=True),
        lax.all_gather(w_gate_up, "fsdp", axis=0, tiled=True),
        lax.all_gather(w_down, "fsdp", axis=0, tiled=True),
    )
    gain_two = gain_two_w.astype(f32)
    scale_two = rms_scale(hidden)
    normed2 = (hidden * scale_two * gain_two).astype(bf16)
    gate_up = jnp.einsum("td,def->tef", normed2, w_gu_full, preferred_element_type=f32)
    gate_val = gate_up[:, 0]
    up_val = gate_up[:, 1]
    act16 = (jax.nn.silu(gate_val) * up_val).astype(bf16)
    result = hidden + jnp.dot(act16, w_down_full, preferred_element_type=f32)
    block_output = result.astype(bf16).reshape(tokens.shape)
    gain_two_back, w_gu_back, w_down_back = (
        lax.all_gather(gain_mlp, "fsdp", axis=0, tiled=True),
        lax.all_gather(w_gate_up, "fsdp", axis=0, tiled=True),
        lax.all_gather(w_down, "fsdp", axis=0, tiled=True),
    )
    cot = cotangent.reshape(local_count, D)
    d_act = contract_cols(cot, w_down_back)
    d_w_down = contract_rows(act16, cot)
    sigmoid_gate = jax.nn.sigmoid(gate_val)
    d_gate = d_act * up_val * sigmoid_gate * (1.0 + gate_val * (1.0 - sigmoid_gate))
    d_up = d_act * gate_val * sigmoid_gate
    d_gu16 = jnp.stack([d_gate, d_up], 1).astype(bf16)
    d_w_gate_up = jnp.einsum("td,tef->def", normed2, d_gu16, preferred_element_type=f32)
    d_normed2 = jnp.einsum("tef,def->td", d_gu16, w_gu_back, preferred_element_type=f32)
    d_hidden_norm, d_gain_two = rms_backward(
        hidden, scale_two, gain_two_back.astype(f32), d_normed2
    )
    mlp_shards = (
        lax.psum_scatter(d_gain_two, "fsdp", scatter_dimension=0, tiled=True),
        lax.psum_scatter(d_w_gate_up, "fsdp", scatter_dimension=0, tiled=True),
        lax.psum_scatter(d_w_down, "fsdp", scatter_dimension=0, tiled=True),
    )
    gain_two_shard, gate_up_shard, down_shard = mlp_shards
    d_gain_mlp, d_w_gate_up_out, d_w_down_out = lax.psum(
        (gain_two_shard, gate_up_shard, down_shard), "ctx"
    )
    d_hidden = cot.astype(f32) + d_hidden_norm
    d_hidden16 = d_hidden.astype(bf16)
    gain_one_back, w_qkv_back, b_unused, w_out_back = (
        lax.all_gather(gain_attn, "fsdp", axis=0, tiled=True),
        lax.all_gather(w_qkv, "fsdp", axis=0, tiled=True),
        lax.all_gather(b_qkv, "fsdp", axis=0, tiled=True),
        lax.all_gather(w_out, "fsdp", axis=0, tiled=True),
    )
    d_w_out = contract_rows(attended16, d_hidden16)
    d_attended16 = contract_cols(d_hidden16, w_out_back).astype(bf16)
    delta = jnp.sum(
        d_attended16.astype(f32).reshape(local_count, HEADS, HEAD_DIM)
        * attended16.astype(f32).reshape(local_count, HEADS, HEAD_DIM),
        -1,
    )
    delta = delta.reshape(local_count, KV_HEADS, per_group).transpose(1, 2, 0)
    d_att_halves = d_attended16.reshape(2, half_rows, KV_HEADS, per_group, HEAD_DIM)
    zero_kv = jnp.zeros((sequence, KV_HEADS, HEAD_DIM), f32)
    buffers = (zero_kv, zero_kv)
    dq_parts = []
    for which in range(2):
        span = slice(which * half_rows, (which + 1) * half_rows)
        backward_query_half = query_halves[which]
        backward_pos_half = pos_halves[which]
        backward_lse_half = lse_parts[which]
        delta_half = delta[:, :, span]
        d_att_half = d_att_halves[which]

        def step(block, carry):
            d_query, d_key_buf, d_value_buf = carry
            start = block * stretch_len
            key_block = lax.dynamic_slice_in_dim(keys_sorted, start, stretch_len, 0)
            value_block = lax.dynamic_slice_in_dim(values_sorted, start, stretch_len, 0)
            scores, visible = masked_scores(
                backward_query_half, backward_pos_half, key_block, start
            )
            probs = jnp.where(visible, jnp.exp(scores - backward_lse_half[..., None]), 0.0)
            probs16 = probs.astype(bf16)
            d_probs = jnp.einsum(
                "tkgd,skd->kgts", d_att_half, value_block, preferred_element_type=f32
            )
            d_scores16 = (probs * (d_probs - delta_half[..., None])).astype(bf16)
            d_query = d_query + softmax_scale * jnp.einsum(
                "kgts,skd->kgtd", d_scores16, key_block, preferred_element_type=f32
            )
            d_key_block = softmax_scale * jnp.einsum(
                "kgts,tkgd->skd", d_scores16, backward_query_half, preferred_element_type=f32
            )
            d_value_block = jnp.einsum(
                "kgts,tkgd->skd", probs16, d_att_half, preferred_element_type=f32
            )
            d_key_buf = lax.dynamic_update_slice_in_dim(
                d_key_buf,
                lax.dynamic_slice_in_dim(d_key_buf, start, stretch_len, 0) + d_key_block,
                start,
                0,
            )
            d_value_buf = lax.dynamic_update_slice_in_dim(
                d_value_buf,
                lax.dynamic_slice_in_dim(d_value_buf, start, stretch_len, 0) + d_value_block,
                start,
                0,
            )
            return (d_query, d_key_buf, d_value_buf)

        zero_query = jnp.zeros((KV_HEADS, per_group, half_rows, HEAD_DIM), f32)
        d_query_half, d_key_buf, d_value_buf = lax.fori_loop(
            0, stretch_ids[which] + 1, step, (zero_query, buffers[0], buffers[1])
        )
        buffers = (d_key_buf, d_value_buf)
        dq_parts.append(d_query_half)
    d_query = jnp.concatenate(dq_parts, 2)

    def by_device(buffer):
        laid = buffer.reshape(2 * n_ctx, stretch_len, kv_width)
        ordered = jnp.stack(
            [jnp.take(laid, pairing, axis=0), jnp.take(laid, 2 * n_ctx - 1 - pairing, axis=0)], 0
        )
        return ordered.reshape(2, everyone * half_rows, kv_width)

    d_keys_own, d_values_own = (
        lax.psum_scatter(by_device(buffers[0]), ("ctx", "fsdp"), scatter_dimension=1, tiled=True),
        lax.psum_scatter(by_device(buffers[1]), ("ctx", "fsdp"), scatter_dimension=1, tiled=True),
    )
    d_query = unrotate(
        d_query.transpose(2, 0, 1, 3).reshape(local_count, HEADS, HEAD_DIM), cosines, sines
    ).reshape(local_count, q_width)
    d_keys = unrotate(d_keys_own.reshape(local_count, KV_HEADS, HEAD_DIM), cosines, sines).reshape(
        local_count, kv_width
    )
    d_qkv = jnp.concatenate([d_query, d_keys, d_values_own.reshape(local_count, kv_width)], 1)
    d_b_qkv = jnp.sum(d_qkv, 0)
    d_qkv16 = d_qkv.astype(bf16)
    d_w_qkv = contract_rows(normed1, d_qkv16)
    d_normed1 = contract_cols(d_qkv16, w_qkv_back)
    d_input_norm, d_gain_one = rms_backward(inputs, scale_one, gain_one_back.astype(f32), d_normed1)
    attn_shards = (
        lax.psum_scatter(d_gain_one, "fsdp", scatter_dimension=0, tiled=True),
        lax.psum_scatter(d_w_qkv, "fsdp", scatter_dimension=0, tiled=True),
        lax.psum_scatter(d_b_qkv, "fsdp", scatter_dimension=0, tiled=True),
        lax.psum_scatter(d_w_out, "fsdp", scatter_dimension=0, tiled=True),
    )
    gain_one_shard, qkv_shard, bias_shard, out_shard = attn_shards
    d_gain_attn, d_w_qkv_out, d_b_qkv_out, d_w_out_out = lax.psum(
        (gain_one_shard, qkv_shard, bias_shard, out_shard), "ctx"
    )
    d_tokens = (d_hidden + d_input_norm).reshape(tokens.shape)
    return (
        block_output,
        d_tokens,
        d_gain_attn,
        d_w_qkv_out,
        d_b_qkv_out,
        d_w_out_out,
        d_gain_mlp,
        d_w_gate_up_out,
        d_w_down_out,
    )


def solution(mesh):
    placed = (
        P("ctx", None, "fsdp", None),
        P(),
        P("fsdp"),
        P("fsdp", None),
        P("fsdp"),
        P("fsdp", None),
        P("fsdp"),
        P("fsdp", None, None),
        P("fsdp", None),
        P("ctx", None, "fsdp", None),
    )
    return jax.shard_map(
        body,
        mesh=mesh,
        in_specs=placed,
        out_specs=(
            P("ctx", None, "fsdp", None),
            P("ctx", None, "fsdp", None),
            P("fsdp"),
            P("fsdp", None),
            P("fsdp"),
            P("fsdp", None),
            P("fsdp"),
            P("fsdp", None, None),
            P("fsdp", None),
        ),
        check_vma=False,
    )
```

profile of v0, /device:TPU:0, one launch (start us, length us, event | category | flops | bytes accessed | tf_op | source)
XLA Modules:
  0.0 2571.6 jit_solution(16829387691928757474)
XLA Ops:
  8.7 6.2 all-gather
  16.8 5.5 all-gather.1
  22.5 36.2 %all-gather.10.cloned.1.call-done = bf16[1536,2048]{1,0:T(8,128)(2,1)} async-done(((bf16[384,2048]{1,0:T(8,128)(2,1)}), bf16[1536,2048]{1,0:T(8,128)(2,1)}) %all-gather.10.cloned.1.call-update) | async-done | bytes 6291472 | tf_op jit(solution)/shard_map/all_gather | solution.py:88
  58.7 3.8 convolution_add_fusion.2
  67.6 6.6 copy.160
  75.7 5.2 all-gather.2
  84.4 35.4 %all-gather.14.cloned.1.call-done = bf16[2,2048,256]{2,1,0:T(8,128)(2,1)} async-done(((bf16[2,64,256]{2,1,0:T(8,128)(2,1)}), bf16[2,2048,256]{2,1,0:T(8,128)(2,1)}) %all-gather.14.cloned.1.call-update) | async-done | bytes 2097168 | tf_op jit(solution)/shard_map/all_gather | solution.py:109
  119.8 2.6 fusion.182
  123.0 55.6 %all-gather.12.cloned.1.call-done = bf16[2,2048,256]{2,1,0:T(8,128)(2,1)} async-done(((bf16[2,64,256]{2,1,0:T(8,128)(2,1)}), bf16[2,2048,256]{2,1,0:T(8,128)(2,1)}) %all-gather.12.cloned.1.call-update) | async-done | bytes 2097168 | tf_op jit(solution)/shard_map/all_gather | solution.py:108
  178.7 2.6 fusion.183
  184.8 2.9 gather_fusion
  187.7 2.8 broadcast_select_fusion.4
  191.9 2.0 reshape.620
  193.9 2.0 copy.150
  197.6 4.0 reshape.621
  201.5 3.2 copy.152
  204.7 13.0 while.80
  217.8 23.5 while.81
  244.0 3.6 while.79
  248.7 2.1 maximum_convert_fusion
  250.8 3.4 multiply_reduce_fusion.2
  254.2 131.5 %all-gather.18.cloned.1.call-done = bf16[1536,2,4480]{2,0,1:T(8,128)(2,1)} async-done(((bf16[384,2,4480]{2,0,1:T(8,128)(2,1)}), bf16[1536,2,4480]{2,0,1:T(8,128)(2,1)}) %all-gather.18.cloned.1.call-update) | async-done | bytes 27525136 | tf_op jit(solution)/shard_map/all_gather | solution.py:184
  385.7 16.4 fusion.167
  402.1 73.8 %all-gather.20.cloned.1.call-done = bf16[4480,1536]{1,0:T(8,128)(2,1)} async-done(((bf16[1120,1536]{1,0:T(8,128)(2,1)}), bf16[4480,1536]{1,0:T(8,128)(2,1)}) %all-gather.20.cloned.1.call-update) | async-done | bytes 13762576 | tf_op jit(solution)/shard_map/all_gather | solution.py:185
  476.0 11.9 fusion.149
  487.8 16.1 multiply_reduce_fusion
  505.3 4.3 convolution_convert_fusion
  512.4 2.3 broadcast_in_dim.144
  514.6 2.3 broadcast_in_dim.144.clone
  516.9 15.5 while.82
  522.7 2.0 fusion.284
  532.7 116.1 %while.83 = (s32[]{:T(128)}, f32[2,6,64,128]{3,2,1,0:T(8,128)S(1)}, f32[4096,2,128]{2,0,1:T(8,128)}, f32[4096,2,128]{2,0,1:T(8,128)}, s32[]{:T(128)}, /*index=5*...) while((s32[]{:T(128)}, f32[2,6,64,128]{3,2,1,0:T(8,128)S(1)}, ...), condition=%wide.region_21.23_spmd.clone, body=%wide.region_20.22_spmd.clone.sunk | while | flops 253641088 | bytes 6595315 | solution.py:288
  538.5 2.0 fusion.299
  631.3 2.0 fusion.299
  639.1 2.0 fusion.299
  648.8 8.9 copy.209
  657.8 6.4 reshape.625
  664.2 8.7 copy.211
  672.9 6.5 reshape.626
  679.4 4.3 gather_fusion.5
  683.7 4.3 gather_fusion.7
  688.0 4.3 gather_fusion.4
  692.3 4.3 gather_fusion.6
  696.6 4.2 broadcast_select_fusion.2
  702.7 2.3 pad_maximum_fusion.1
  705.0 4.5 pad_maximum_fusion
  709.6 5.0 fusion.163
  715.6 132.0 %reduce-scatter.9.cloned.1.call-done = f32[2,64,256]{2,1,0:T(8,128)} async-done(((f32[2,2048,256]{2,1,0:T(8,128)}), f32[2,64,256]{2,1,0:T(8,128)}) %reduce-scatter.9.cloned.1.call-update) | async-done | bytes 131088 | tf_op jit(solution)/shard_map/reduce_scatter | solution.py:304
  848.5 139.7 %reduce-scatter.7.cloned.1.call-done = f32[2,64,256]{2,1,0:T(8,128)} async-done(((f32[2,2048,256]{2,1,0:T(8,128)}), f32[2,64,256]{2,1,0:T(8,128)}) %reduce-scatter.7.cloned.1.call-update) | async-done | bytes 131088 | tf_op jit(solution)/shard_map/reduce_scatter | solution.py:303
  989.8 8.6 fusion.176
  999.5 14.9 fusion.145
  1015.6 23.1 fusion.143
  1038.9 25.8 %reduce-scatter.13.cloned.1.call-done = f32[384,1536]{1,0:T(8,128)} async-done(((f32[1536,1536]{1,0:T(8,128)}), f32[384,1536]{1,0:T(8,128)}) %reduce-scatter.13.cloned.1.call-update) | async-done | bytes 2359312 | tf_op jit(solution)/shard_map/reduce_scatter | solution.py:322
  1064.6 102.7 %reduce-scatter.11.cloned.1.call-done = f32[384,2048]{1,0:T(8,128)} async-done(((f32[1536,2048]{1,0:T(8,128)}), f32[384,2048]{1,0:T(8,128)}) %reduce-scatter.11.cloned.1.call-update) | async-done | bytes 3145744 | tf_op jit(solution)/shard_map/reduce_scatter | solution.py:320
  1167.3 200.3 %reduce-scatter.17.cloned.1.call-done = f32[1120,1536]{1,0:T(8,128)} async-done(((f32[4480,1536]{1,0:T(8,128)}), f32[1120,1536]{1,0:T(8,128)}) %reduce-scatter.17.cloned.1.call-update) | async-done | bytes 6881296 | tf_op jit(solution)/shard_map/reduce_scatter | solution.py:216
  1367.6 380.5 %reduce-scatter.15.cloned.1.call-done = f32[384,2,4480]{2,0,1:T(8,128)} async-done(((f32[1536,2,4480]{2,0,1:T(8,128)}), f32[384,2,4480]{2,0,1:T(8,128)}) %reduce-scatter.15.cloned.1.call-update) | async-done | bytes 13762576 | tf_op jit(solution)/shard_map/reduce_scatter | solution.py:215
  1751.2 9.4 fusion.132
  1761.0 3.7 fusion.159
  1764.8 11.6 all-reduce.5
  1776.6 23.9 all-reduce.3
  1801.1 2.4 fusion.156
  1803.5 720.2 %all-reduce.8.cloned.1.call-done = (f32[384,2048]{1,0:T(8,128)}, f32[384,1536]{1,0:T(8,128)}, f32[384,2,4480]{2,0,1:T(8,128)}, f32[1120,1536]{1,0:T(8,128)}) async-done(((f32[384,2048]{1,0:T(8,128)}, f32[384,1536]{1,0:T(8,128)}, f32[384,2,4480]{2,0,1:T(8,128)}, f32[1120,1536]{1,0:T(8,128)}), (f32[384,2048]{1,0:T(8,128)}, f32[384,1536]{1,0:T(8,128)}, f32[384,2,4480]{2,0,1:T(8,128)}, ...) | async-done | bytes 26148880 | tf_op jit(solution)/shard_map/psum | solution.py:325
  2523.7 33.1 %copy.180 = f32[384,2,4480]{2,1,0:T(2,128)} copy(f32[384,2,4480]{2,0,1:T(8,128)} %get-tuple-element.961) | data formatting | bytes 27525120
  2561.7 2.9 copy.277
  (540 shorter events, 204.0 us)
Async XLA Ops:
  7.2 15.1 copy-start.5
  7.2 51.5 %all-gather.10.cloned.1.call-start = ((), (), s32[]{:S(2)}) async-start(), calls=%async_computation.6 | async-start | bytes 7864320 | tf_op jit(solution)/shard_map/all_gather | solution.py:88
  7.9 111.9 %all-gather.14.cloned.1.call-start = ((), (), s32[]{:S(2)}) async-start(), calls=%async_computation.8 | async-start | bytes 2162688 | tf_op jit(solution)/shard_map/all_gather | solution.py:109
  14.9 43.8 %copy-start.28 = (f32[1536]{0:T(1024)}, f32[1536]{0:T(1024)S(1)}, u32[]{:S(2)}) copy-start(f32[1536]{0:T(1024)S(1)} %reshape.584) | copy-start | bytes 18436
  16.1 42.6 %copy-start.32 = (f32[128]{0:T(128)}, f32[128]{0:T(128)S(1)}, u32[]{:S(2)}) copy-start(f32[128]{0:T(128)S(1)} %rsqrt.26) | copy-start | bytes 1540
  22.5 40.0 %copy-start.11 = (bf16[128,1536]{1,0:T(8,128)(2,1)}, bf16[128,1536]{1,0:T(8,128)(2,1)S(1)}, u32[]{:S(2)}) copy-start(bf16[128,1536]{1,0:T(8,128)(2,1)S(1)} %fusion.153) | copy-start | bytes 1179652
  58.7 4.5 copy-start.37
  63.2 115.5 %all-gather.12.cloned.1.call-start = ((), (), s32[]{:S(2)}) async-start(), calls=%async_computation.7 | async-start | bytes 2162688 | tf_op jit(solution)/shard_map/all_gather | solution.py:108
  65.5 18.3 copy-start.24
  65.5 18.3 copy-start.26
  65.7 8.5 copy-start.22
  67.0 183.8 %all-gather.16.cloned.1.call-start = ((), (), s32[]{:S(2)}) async-start(), calls=%async_computation.9 | async-start | bytes 5898240 | tf_op jit(solution)/shard_map/all_gather | solution.py:90
  67.5 318.2 %all-gather.18.cloned.1.call-start = ((), (), s32[]{:S(2)}) async-start(), calls=%async_computation.10 | async-start | bytes 34406400 | tf_op jit(solution)/shard_map/all_gather | solution.py:184
  74.2 1.4 copy-start.38
  74.2 401.7 %all-gather.20.cloned.1.call-start = ((), (), s32[]{:S(2)}) async-start(), calls=%async_computation.11 | async-start | bytes 17203200 | tf_op jit(solution)/shard_map/all_gather | solution.py:185
  74.8 772.7 %reduce-scatter.9.cloned.1.call-start = ((), (), s32[]{:S(2)}) async-start(), calls=%async_computation.13 | async-start | bytes 4325376 | tf_op jit(solution)/shard_map/reduce_scatter | solution.py:304
  187.7 2.8 copy-start.13
  193.9 2.0 copy-start.14
  193.9 2.2 copy-start.15
  247.6 3.2 copy-start.4
  247.6 6.5 copy-start.30
  385.7 90.2 %copy-start.18 = (bf16[1,2,64,1536]{3,2,1,0:T(8,128)(2,1)S(1)}, bf16[1,2,64,1536]{3,2,1,0:T(8,128)(2,1)}, u32[]{:S(2)}) copy-start(bf16[1,2,64,1536]{3,2,1,0:T(8,128)(2,1)} %param.35) | copy-start | bytes 1179652
  487.8 16.1 copy-start.20
  505.3 204.3 %copy-start.2 = (f32[128,1536]{1,0:T(8,128)}, f32[128,1536]{1,0:T(8,128)S(1)}, u32[]{:S(2)}) copy-start(f32[128,1536]{1,0:T(8,128)S(1)} %subtract_add_fusion) | copy-start | bytes 2359300
  509.6 1.4 copy-start.9
  514.6 2.3 copy-start.31
  692.3 4.3 copy-start.36
  696.6 4.2 copy-start.7
  696.6 4.2 copy-start.8
  696.6 4.2 copy-start.35
  705.0 283.2 %reduce-scatter.7.cloned.1.call-start = ((), (), s32[]{:S(2)}) async-start(), calls=%async_computation.12 | async-start | bytes 4325376 | tf_op jit(solution)/shard_map/reduce_scatter | solution.py:303
  709.5 355.1 %reduce-scatter.13.cloned.1.call-start = ((), (), s32[]{:S(2)}) async-start(), calls=%async_computation.15 | async-start | bytes 11796480 | tf_op jit(solution)/shard_map/reduce_scatter | solution.py:322
  714.6 0.8 copy-start.25
  714.6 0.8 copy-start.27
  714.6 452.7 %reduce-scatter.11.cloned.1.call-start = ((), (), s32[]{:S(2)}) async-start(), calls=%async_computation.14 | async-start | bytes 15728640 | tf_op jit(solution)/shard_map/reduce_scatter | solution.py:320
  714.7 274.4 %copy-start.23 = (f32[128,64]{1,0:T(8,128)S(1)}, f32[128,64]{1,0:T(8,128)}, u32[]{:S(2)}) copy-start(f32[128,64]{1,0:T(8,128)} %copy-done.22) | copy-start | bytes 98308
  715.4 274.4 %copy-start.12 = (bf16[128,1536]{1,0:T(8,128)(2,1)S(1)}, bf16[128,1536]{1,0:T(8,128)(2,1)}, u32[]{:S(2)}) copy-start(bf16[128,1536]{1,0:T(8,128)(2,1)} %copy-done.11) | copy-start | bytes 1179652
  715.6 282.8 %copy-start = (f32[128,12,128]{0,2,1:T(8,128)}, f32[128,12,128]{0,2,1:T(8,128)S(1)}, u32[]{:S(2)}) copy-start(f32[128,12,128]{0,2,1:T(8,128)S(1)} %pad_maximum_fusion.8) | copy-start | bytes 2359300
  998.4 1.1 copy-start.19
  998.4 369.2 %reduce-scatter.17.cloned.1.call-start = ((), (), s32[]{:S(2)}) async-start(), calls=%async_computation.17 | async-start | bytes 34406400 | tf_op jit(solution)/shard_map/reduce_scatter | solution.py:216
  1014.4 1.3 copy-start.21
  1014.4 733.7 %reduce-scatter.15.cloned.1.call-start = ((), (), s32[]{:S(2)}) async-start(), calls=%async_computation.16 | async-start | bytes 68812800 | tf_op jit(solution)/shard_map/reduce_scatter | solution.py:215
  1038.8 1484.9 %all-reduce.8.cloned.1.call-start = ((), (), s32[]{:S(2)}) async-start(), calls=%async_computation.18 | async-start | bytes 52297728 | tf_op jit(solution)/shard_map/psum | solution.py:325
  1748.1 0.7 copy-start.39
  1748.1 2.5 copy-start.33
  1748.1 12.8 slice-start
  1751.2 9.4 copy-start.1
  1751.2 9.8 slice-start.1
  1751.2 9.8 copy-start.6
  1751.2 9.8 copy-start.29
  1751.2 9.8 copy-start.34
  1761.0 40.1 %copy-start.3 = (f32[128,1536]{1,0:T(8,128)S(1)}, f32[128,1536]{1,0:T(8,128)}, u32[]{:S(2)}) copy-start(f32[128,1536]{1,0:T(8,128)} %copy-done.2) | copy-start | bytes 2359300
  2523.7 33.1 %copy-start.16 = (f32[384,2048]{1,0:T(8,128)S(1)}, f32[384,2048]{1,0:T(8,128)}, u32[]{:S(2)}) copy-start(f32[384,2048]{1,0:T(8,128)} %get-tuple-element.1648) | copy-start | bytes 9437188
  2523.7 34.8 %copy-start.17 = (f32[384,1536]{1,0:T(8,128)S(1)}, f32[384,1536]{1,0:T(8,128)}, u32[]{:S(2)}) copy-start(f32[384,1536]{1,0:T(8,128)} %get-tuple-element.1650) | copy-start | bytes 7077892
  2556.8 4.9 copy-start.10
Sparse Core Ops, SparseCore 0:
  9.6 49.0 all-gather.9
  63.3 56.4 all-gather.13
  123.3 55.3 all-gather.11
  180.1 36.3 all-gather.15
  218.4 167.2 all-gather.17
  387.1 88.7 all-gather.19
  705.1 142.3 reduce-scatter.8
  849.8 138.3 reduce-scatter.6
  990.8 73.7 reduce-scatter.12
  1067.7 99.6 reduce-scatter.10
  1169.9 197.6 reduce-scatter.16
  1370.1 377.9 reduce-scatter.14
  1753.0 770.6 all-reduce.7
where the time goes:
time: 2580 us; the launch traced here: 2570 us
  waiting for transfers between devices  2040 us (79%)
  matrix products  280 us (11%)
  local copies, waits for them, and re-layouts  138 us (5%)
  blocking collectives  52.3 us (2%)
  other arithmetic  43.2 us (2%)
    psum x1, waiting for transfers between devices, body(): lax.psum((gain_one_shard, qkv_shard, bias_shard, out_shard), 'ctx')  720 us
    reduce_scatter x1, waiting for transfers between devices, body(): lax.psum_scatter(d_w_gate_up, 'fsdp', scatter_dimension=0, tiled=True)  380 us
    reduce_scatter x1, waiting for transfers between devices, body(): lax.psum_scatter(d_w_down, 'fsdp', scatter_dimension=0, tiled=True)  200 us
    reduce_scatter x1, waiting for transfers between devices, body(): lax.psum_scatter(by_device(buffers[0]), ('ctx', 'fsdp'), scatter_dimensio...  140 us
    reduce_scatter x1, waiting for transfers between devices, body(): lax.psum_scatter(by_device(buffers[1]), ('ctx', 'fsdp'), scatter_dimensio...  132 us
    all_gather x1, waiting for transfers between devices, body(): lax.all_gather(w_gate_up, 'fsdp', axis=0, tiled=True)  132 us
    reduce_scatter x1, waiting for transfers between devices, body(): lax.psum_scatter(d_w_qkv, 'fsdp', scatter_dimension=0, tiled=True)  103 us
    all_gather x1, waiting for transfers between devices, body(): lax.all_gather(w_down, 'fsdp', axis=0, tiled=True)  73.8 us
  transfers between devices with their start and end apart: 13, of which 12 were waited for; matrix products, arithmetic and copies ran while one was open for 7% of the time, Pallas kernels for 0%

commit v1 on v0

v1 whole, which is shorter than its diff:
```python
import functools

import jax
import jax.numpy as jnp
from jax import lax
from jax.experimental import pallas as pl
from jax.experimental.pallas import tpu as pltpu
from jax.sharding import PartitionSpec as P

D = 1536
HEADS = 12
KV_HEADS = 2
HEAD_DIM = 128

eps = 1e-06
rope_base = 1000000.0
F32 = jnp.float32
BF16 = jnp.bfloat16
VMEM_LIMIT = 60 * 1024 * 1024


def rope_tables(position):
    half = HEAD_DIM // 2
    inverse = rope_base ** (-(jnp.arange(half, dtype=F32) * 2.0 / HEAD_DIM))
    angle = position.astype(F32)[:, None] * inverse[None, :]
    return (jnp.cos(angle)[:, None, :], jnp.sin(angle)[:, None, :])


def rotate(vectors, cosines, sines):
    half = HEAD_DIM // 2
    first, second = (vectors[..., :half], vectors[..., half:])
    return jnp.concatenate([first * cosines - second * sines, second * cosines + first * sines], -1)


def unrotate(grads, cosines, sines):
    half = HEAD_DIM // 2
    first, second = (grads[..., :half], grads[..., half:])
    return jnp.concatenate([first * cosines + second * sines, second * cosines - first * sines], -1)


def rms_scale(values):
    return lax.rsqrt(jnp.mean(values * values, -1, keepdims=True) + eps)


def rms_backward(values, scale_rows, gain, d_normed):
    d_gain = jnp.sum(d_normed * values * scale_rows, 0)
    d_inner = d_normed * gain
    d_values = scale_rows * d_inner - values * scale_rows**3 * jnp.mean(
        d_inner * values, -1, keepdims=True
    )
    return (d_values, d_gain)


def dot(left, right, contract):
    return lax.dot_general(left, right, (contract, ((), ())), preferred_element_type=F32)


def contract_rows(left, right):
    return dot(left, right, ((0,), (0,)))


def contract_cols(left, right):
    return dot(left, right, ((1,), (1,)))


def stacked_heads(ref, which, heads):
    return jnp.concatenate(
        [ref[which, :, h * HEAD_DIM : (h + 1) * HEAD_DIM] for h in range(heads)], 0
    )


def causal(block_len, heads):
    keys = lax.broadcasted_iota(jnp.int32, (block_len, block_len), 0)
    queries = lax.broadcasted_iota(jnp.int32, (block_len, block_len), 1)
    return jnp.concatenate([keys <= queries] * heads, 1)


def attend_kernel(heads, table, ids, q_ref, kv_ref, o_ref, lse_ref):
    block_len = q_ref.shape[1]
    cols = heads * block_len
    scale = HEAD_DIM ** (-0.5)
    for which in range(2):
        last = ids[which]
        query = stacked_heads(q_ref, which, heads)

        def step(block, carry, masked=False):
            highest, total, acc = carry
            start = pl.multiple_of(table[block] * block_len, block_len)
            key = kv_ref[pl.ds(start, block_len), :HEAD_DIM]
            value = kv_ref[pl.ds(start, block_len), HEAD_DIM:]
            scores = contract_cols(key, query) * scale
            if masked:
                scores = jnp.where(causal(block_len, heads), scores, -1e30)
            new_high = jnp.maximum(highest, jnp.max(scores, 0, keepdims=True))
            probs = jnp.exp(scores - new_high)
            fade = jnp.exp(highest - new_high)
            total = total * fade + jnp.sum(probs, 0, keepdims=True)
            acc = acc * fade + contract_rows(value, probs.astype(BF16))
            return (new_high, total, acc)

        begin = (
            jnp.full((1, cols), -1e30, F32),
            jnp.zeros((1, cols), F32),
            jnp.zeros((HEAD_DIM, cols), F32),
        )
        carry = lax.fori_loop(0, last, step, begin)
        highest, total, acc = step(last, carry, True)
        lse_ref[which] = highest + jnp.log(total)
        out = (acc / total).T
        for h in range(heads):
            o_ref[which, :, h * HEAD_DIM : (h + 1) * HEAD_DIM] = out[
                h * block_len : (h + 1) * block_len
            ].astype(BF16)


def attend_back_kernel(
    heads, table, ids, q_ref, kv_ref, o_ref, do_ref, lse_ref, dq_ref, dkv_ref, sums
):
    block_len = q_ref.shape[1]
    cols = heads * block_len
    scale = HEAD_DIM ** (-0.5)
    sums[...] = jnp.zeros_like(sums)
    for which in range(2):
        last = ids[which]
        query = stacked_heads(q_ref, which, heads)
        d_out = stacked_heads(do_ref, which, heads)
        out = stacked_heads(o_ref, which, heads)
        delta = jnp.sum((d_out.astype(F32) * out.astype(F32)).T, 0, keepdims=True)
        lse = lse_ref[which]

        def step(block, d_query, masked=False):
            start = pl.multiple_of(table[block] * block_len, block_len)
            key = kv_ref[pl.ds(start, block_len), :HEAD_DIM]
            value = kv_ref[pl.ds(start, block_len), HEAD_DIM:]
            scores = contract_cols(key, query) * scale
            probs = jnp.exp(scores - lse)
            if masked:
                probs = jnp.where(causal(block_len, heads), probs, 0.0)
            d_probs = contract_cols(value, d_out)
            d_scores = (probs * (d_probs - delta)).astype(BF16)
            sums[pl.ds(start, block_len), :HEAD_DIM] += dot(d_scores, query, ((1,), (0,)))
            sums[pl.ds(start, block_len), HEAD_DIM:] += dot(
                probs.astype(BF16), d_out, ((1,), (0,))
            )
            return d_query + contract_rows(key, d_scores)

        d_query = lax.fori_loop(0, last, step, jnp.zeros((HEAD_DIM, cols), F32))
        d_query = step(last, d_query, True)
        d_query = (d_query * scale).T
        for h in range(heads):
            dq_ref[which, :, h * HEAD_DIM : (h + 1) * HEAD_DIM] = d_query[
                h * block_len : (h + 1) * block_len
            ]
    dkv_ref[:, :HEAD_DIM] = (sums[:, :HEAD_DIM] * scale).astype(BF16)
    dkv_ref[:, HEAD_DIM:] = sums[:, HEAD_DIM:].astype(BF16)


def in_vmem(count):
    return [pl.BlockSpec(memory_space=pltpu.VMEM)] * count


def in_smem(count):
    return [pl.BlockSpec(memory_space=pltpu.SMEM)] * count


def attend(table, ids, query, keys_values, heads):
    _, block_len, width = query.shape
    tall = keys_values.shape[0]
    return pl.pallas_call(
        functools.partial(attend_kernel, heads),
        out_shape=(
            jax.ShapeDtypeStruct(query.shape, BF16),
            jax.ShapeDtypeStruct((2, 1, heads * block_len), F32),
        ),
        in_specs=in_smem(2) + in_vmem(2),
        out_specs=tuple(in_vmem(2)),
        compiler_params=pltpu.CompilerParams(vmem_limit_bytes=VMEM_LIMIT),
        cost_estimate=pl.CostEstimate(
            flops=2 * tall * block_len * width * 2,
            bytes_accessed=tall * 512,
            transcendentals=tall * heads * block_len,
        ),
        name="attend",
    )(table, ids, query, keys_values)


def attend_back(table, ids, query, keys_values, out, d_out, lse, heads):
    _, block_len, width = query.shape
    tall = keys_values.shape[0]
    return pl.pallas_call(
        functools.partial(attend_back_kernel, heads),
        out_shape=(
            jax.ShapeDtypeStruct(query.shape, F32),
            jax.ShapeDtypeStruct(keys_values.shape, BF16),
        ),
        in_specs=in_smem(2) + in_vmem(5),
        out_specs=tuple(in_vmem(2)),
        scratch_shapes=[pltpu.VMEM(keys_values.shape, F32)],
        compiler_params=pltpu.CompilerParams(vmem_limit_bytes=VMEM_LIMIT),
        cost_estimate=pl.CostEstimate(
            flops=5 * tall * block_len * width * 2,
            bytes_accessed=tall * 1024,
            transcendentals=tall * heads * block_len,
        ),
        name="attend_back",
    )(table, ids, query, keys_values, out, d_out, lse)


def exchange(pieces, axis):
    return lax.all_to_all(pieces, axis, split_axis=0, concat_axis=0, tiled=True)


def exchange_async(pieces, axis):
    n = pieces.shape[0]
    me = lax.axis_index(axis)
    own = lax.dynamic_index_in_dim(pieces, me, 0, keepdims=True)
    arrived = lax.dynamic_update_slice_in_dim(jnp.zeros_like(pieces), own, me, 0)
    for shift in range(1, n):
        piece = lax.dynamic_index_in_dim(pieces, (me + shift) % n, 0, keepdims=True)
        piece = lax.ppermute(piece, axis, [(i, (i + shift) % n) for i in range(n)])
        arrived = lax.dynamic_update_slice_in_dim(arrived, piece, (me + n - shift) % n, 0)
    return arrived


def body(tokens, pairing, gain_attn, w_qkv, b_qkv, w_out, gain_mlp, w_gate_up, w_down, cotangent):
    half_rows = tokens.shape[2]
    n_ctx = lax.axis_size("ctx")
    n_fsdp = lax.axis_size("fsdp")
    ctx_index = lax.axis_index("ctx")
    fsdp_index = lax.axis_index("fsdp")
    stretch_len = half_rows * n_fsdp
    rows = 2 * stretch_len
    local_count = 2 * half_rows
    q_width = HEADS * HEAD_DIM
    kv_width = KV_HEADS * HEAD_DIM
    heads = HEADS // n_fsdp
    q_cols = heads * HEAD_DIM
    d_shard = w_qkv.shape[0]
    ff_shard = w_down.shape[0]

    owner_range = jnp.arange(n_ctx, dtype=jnp.int32)
    own_first = jnp.sum(jnp.where(owner_range == ctx_index, pairing, 0))
    ids = jnp.stack([own_first, 2 * n_ctx - 1 - own_first])
    inverse_pair = jnp.sum(
        owner_range[:, None] * (pairing[:, None] == owner_range[None, :]).astype(jnp.int32), 0
    )
    table = jnp.concatenate([2 * inverse_pair, 2 * inverse_pair[::-1] + 1])
    position = (
        ids[:, None] * stretch_len + jnp.arange(stretch_len, dtype=jnp.int32)[None, :]
    ).reshape(rows)
    kv_of = [f * KV_HEADS // n_fsdp for f in range(n_fsdp)]
    my_kv = fsdp_index * KV_HEADS // n_fsdp

    small = lax.all_gather(jnp.concatenate([gain_attn, gain_mlp, b_qkv]), "fsdp", axis=0)
    gain_one = small[:, :d_shard].reshape(D).astype(F32)
    gain_two = small[:, d_shard : 2 * d_shard].reshape(D).astype(F32)
    bias = small[:, 2 * d_shard :].reshape(-1).astype(F32)
    x_all = lax.all_gather(tokens[0], "fsdp", axis=1, tiled=True).reshape(rows, D)
    qkv_pieces = jnp.stack(
        [
            jnp.concatenate(
                [
                    w_qkv[:, f * q_cols : (f + 1) * q_cols],
                    w_qkv[:, q_width + kv_of[f] * HEAD_DIM : q_width + (kv_of[f] + 1) * HEAD_DIM],
                    w_qkv[
                        :,
                        q_width + kv_width + kv_of[f] * HEAD_DIM : q_width
                        + kv_width
                        + (kv_of[f] + 1) * HEAD_DIM,
                    ],
                ],
                1,
            )
            for f in range(n_fsdp)
        ]
    )
    w_qkv_cols = exchange(qkv_pieces, "fsdp").reshape(D, -1)
    bias_cols = jnp.concatenate(
        [
            lax.dynamic_slice_in_dim(bias, fsdp_index * q_cols, q_cols),
            lax.dynamic_slice_in_dim(bias, q_width + my_kv * HEAD_DIM, HEAD_DIM),
            lax.dynamic_slice_in_dim(bias, q_width + kv_width + my_kv * HEAD_DIM, HEAD_DIM),
        ]
    )
    w_gate_cols, w_up_cols = (
        exchange_async(
            w_gate_up[:, e].reshape(d_shard, n_fsdp, ff_shard).transpose(1, 0, 2), "fsdp"
        ).reshape(D, ff_shard)
        for e in range(2)
    )
    cot_all = lax.all_gather(cotangent[0], "fsdp", axis=1, tiled=True).reshape(rows, D)

    x32 = x_all.astype(F32)
    normed1 = (x32 * rms_scale(x32) * gain_one).astype(BF16)
    qkv = jnp.dot(normed1, w_qkv_cols, preferred_element_type=F32) + bias_cols
    cosines, sines = rope_tables(position)
    rotated = rotate(
        qkv[:, : q_cols + HEAD_DIM].reshape(rows, heads + 1, HEAD_DIM), cosines, sines
    ).astype(BF16)
    query = rotated[:, :heads].reshape(2, stretch_len, q_cols)
    own_kv = jnp.concatenate([rotated[:, heads], qkv[:, q_cols + HEAD_DIM :].astype(BF16)], 1)
    keys_values = lax.all_gather(own_kv, "ctx", axis=0, tiled=True)
    attended, lse = attend(table, ids, query, keys_values, heads)
    attended16 = attended.reshape(rows, q_cols)

    def scatter(partial):
        return lax.psum_scatter(
            partial.astype(BF16).reshape(2, stretch_len, D), "fsdp", scatter_dimension=1, tiled=True
        ).astype(F32).reshape(local_count, D)

    def gather(own):
        return lax.all_gather(
            own.reshape(2, half_rows, D), "fsdp", axis=1, tiled=True
        ).reshape(rows, D)

    inputs = tokens.reshape(local_count, D).astype(F32)
    scale_one = rms_scale(inputs)
    hidden = inputs + scatter(jnp.dot(attended16, w_out, preferred_element_type=F32))
    scale_two = rms_scale(hidden)
    normed2 = gather((hidden * scale_two * gain_two).astype(BF16))
    gate_val = jnp.dot(normed2, w_gate_cols, preferred_element_type=F32)
    up_val = jnp.dot(normed2, w_up_cols, preferred_element_type=F32)
    sigmoid_gate = jax.nn.sigmoid(gate_val)
    act16 = (jax.nn.silu(gate_val) * up_val).astype(BF16)
    result = hidden + scatter(jnp.dot(act16, w_down, preferred_element_type=F32))
    block_output = result.astype(BF16).reshape(tokens.shape)

    d_act = contract_cols(cot_all, w_down)
    d_gate16 = (d_act * up_val * sigmoid_gate * (1.0 + gate_val * (1.0 - sigmoid_gate))).astype(BF16)
    d_up16 = (d_act * gate_val * sigmoid_gate).astype(BF16)
    d_normed2 = scatter(contract_cols(d_gate16, w_gate_cols) + contract_cols(d_up16, w_up_cols))
    cot = cotangent.reshape(local_count, D).astype(F32)
    d_hidden_norm, d_gain_two = rms_backward(hidden, scale_two, gain_two, d_normed2)
    d_hidden = cot + d_hidden_norm
    dh_all = gather(d_hidden.astype(BF16))
    d_attended16 = contract_cols(dh_all, w_out).astype(BF16).reshape(2, stretch_len, q_cols)
    d_query, d_kv = attend_back(
        table, ids, query, keys_values, attended, d_attended16, lse, heads
    )
    d_kv_own = lax.psum_scatter(d_kv, "ctx", scatter_dimension=0, tiled=True).astype(F32)

    d_w_down = contract_rows(act16, cot_all).astype(BF16)
    d_w_gate, d_w_up = (
        exchange(contract_rows(normed2, piece).astype(BF16).reshape(n_fsdp, d_shard, ff_shard), "fsdp")
        for piece in (d_gate16, d_up16)
    )
    d_w_gate_up = jnp.stack(
        [piece.transpose(1, 0, 2).reshape(d_shard, n_fsdp * ff_shard) for piece in (d_w_gate, d_w_up)], 1
    )
    d_w_out = contract_rows(attended16, dh_all).astype(BF16)

    d_rotated = jnp.concatenate([d_query.reshape(rows, q_cols), d_kv_own[:, :HEAD_DIM]], 1)
    d_rotated = unrotate(
        d_rotated.reshape(rows, heads + 1, HEAD_DIM), cosines, sines
    ).reshape(rows, q_cols + HEAD_DIM)
    d_qkv = jnp.concatenate([d_rotated, d_kv_own[:, HEAD_DIM:]], 1)
    d_bias = jnp.sum(d_qkv, 0)
    d_qkv16 = d_qkv.astype(BF16)
    d_normed1 = scatter(contract_cols(d_qkv16, w_qkv_cols))
    d_input_norm, d_gain_one = rms_backward(inputs, scale_one, gain_one, d_normed1)
    d_tokens = (d_hidden + d_input_norm).reshape(tokens.shape)

    d_w_pieces = exchange(
        contract_rows(normed1, d_qkv16).astype(BF16).reshape(n_fsdp, d_shard, -1), "fsdp"
    )

    def by_columns(pieces):
        queries = [pieces[f][..., :q_cols] for f in range(n_fsdp)]
        rest = []
        for part in range(2):
            lo = q_cols + part * HEAD_DIM
            for g in range(KV_HEADS):
                rest.append(
                    sum(
                        pieces[f][..., lo : lo + HEAD_DIM].astype(F32)
                        for f in range(n_fsdp)
                        if kv_of[f] == g
                    ).astype(pieces[0].dtype)
                )
        return jnp.concatenate(queries + rest, -1)

    d_w_qkv = by_columns([d_w_pieces[f] for f in range(n_fsdp)])

    zeros = jnp.zeros_like(d_bias)
    d_bias_full = by_columns([jnp.where(fsdp_index == f, d_bias, zeros) for f in range(n_fsdp)])
    vector = lax.psum(
        jnp.concatenate([d_gain_one, d_gain_two, d_bias_full]), ("ctx", "fsdp")
    )
    d_gain_attn = lax.dynamic_slice_in_dim(vector[:D], fsdp_index * d_shard, d_shard)
    d_gain_mlp = lax.dynamic_slice_in_dim(vector[D : 2 * D], fsdp_index * d_shard, d_shard)
    b_shard = b_qkv.shape[0]
    d_b_qkv = lax.dynamic_slice_in_dim(vector[2 * D :], fsdp_index * b_shard, b_shard)

    def total(partial):
        return lax.psum(partial, "ctx").astype(F32)

    return (
        block_output,
        d_tokens,
        d_gain_attn,
        total(d_w_qkv),
        d_b_qkv,
        total(d_w_out),
        d_gain_mlp,
        total(d_w_gate_up),
        total(d_w_down),
    )


def solution(mesh):
    placed = (
        P("ctx", None, "fsdp", None),
        P(),
        P("fsdp"),
        P("fsdp", None),
        P("fsdp"),
        P("fsdp", None),
        P("fsdp"),
        P("fsdp", None, None),
        P("fsdp", None),
        P("ctx", None, "fsdp", None),
    )
    return jax.shard_map(
        body,
        mesh=mesh,
        in_specs=placed,
        out_specs=(
            P("ctx", None, "fsdp", None),
            P("ctx", None, "fsdp", None),
            P("fsdp"),
            P("fsdp", None),
            P("fsdp"),
            P("fsdp", None),
            P("fsdp"),
            P("fsdp", None, None),
            P("fsdp", None),
        ),
        check_vma=False,
    )
```

time: 2580 us -> 1010 us (0.39)
  waiting for transfers between devices: 2040 us -> 600 us
  matrix products: 280 us -> 63.6 us
  Pallas kernels: 0 us -> 29.2 us
    reduce_scatter x6 -> x5, waiting for transfers between devices: 981 us -> 84.4 us  [the longest x1 55.6 us: body(): lax.psum_scatter(d_kv, 'ctx', scatter_dimension=0, tiled=True).astype(F32)]
    psum x1, waiting for transfers between devices: 720 us -> 355 us  [total(): return lax.psum(partial, 'ctx').astype(F32)]
    all_gather x6 -> x5, waiting for transfers between devices: 333 us -> 64.5 us  [the longest x1 45 us: body(): keys_values = lax.all_gather(own_kv, 'ctx', axis=0, tiled=True)]
    dot_general x131 -> x15, matrix products: 280 us -> 63.6 us  [the longest x10 42.6 us: dot(): lax.dot_general(left, right, (contract, ((), ())), preferred_element_type...]
    all_to_all x0 -> x4, waiting for transfers between devices: none -> 50.4 us  [exchange(): return lax.all_to_all(pieces, axis, split_axis=0, concat_axis=0, tiled=True)]
    ppermute x0 -> x6, waiting for transfers between devices: none -> 44.5 us  [exchange_async(): piece = lax.ppermute(piece, axis, [(i, (i + shift) % n) for i in range(n)])]
    pallas_call x0 -> x2, Pallas kernels: none -> 29.2 us  [the longest x1 16.1 us: attend_back(): pl.pallas_call(functools.partial(attend_back_kernel, heads), out_shape=(j...]
    reshape x11 -> x6, local copies, waits for them, and re-layouts: 39.6 us -> 12.2 us  [the longest x2 4.21 us: body(): contract_rows(normed2, piece).astype(BF16)]
  transfers between devices with their start and end apart: 13 -> 21, of which waited for: 12 -> 10; matrix products, arithmetic and copies ran while one was open for 7% -> 19% of each run, Pallas kernels for 0% -> 0%
where the time goes in v1:
time: 1010 us; the launch traced here: 1000 us
  waiting for transfers between devices  600 us (59%)
  local copies, waits for them, and re-layouts  141 us (14%)
  blocking collectives  75.7 us (7%)
  matrix products  63.6 us (6%)
  other arithmetic  53.9 us (5%)
  Pallas kernels  29.2 us (3%)
  starting transfers between devices  24.6 us (2%)
  between operations  15.3 us (2%)
    psum x1, waiting for transfers between devices, total(): return lax.psum(partial, 'ctx').astype(F32)  355 us
    unnamed x74, local copies, waits for them, and re-layouts  55.7 us
    reduce_scatter x1, waiting for transfers between devices, body(): lax.psum_scatter(d_kv, 'ctx', scatter_dimension=0, tiled=True).astype(F32)  55.6 us
    all_to_all x4, waiting for transfers between devices, exchange(): return lax.all_to_all(pieces, axis, split_axis=0, concat_axis=0, tiled=True)  50.4 us
    all_gather x1, waiting for transfers between devices, body(): keys_values = lax.all_gather(own_kv, 'ctx', axis=0, tiled=True)  45 us
    ppermute x6, waiting for transfers between devices, exchange_async(): piece = lax.ppermute(piece, axis, [(i, (i + shift) % n) for i in range(n)])  44.5 us
    dot_general x10, matrix products, dot(): lax.dot_general(left, right, (contract, ((), ())), preferred_element_type...  42.6 us
    psum x1, blocking collectives, body(): lax.psum(jnp.concatenate([d_gain_one, d_gain_two, d_bias_full]), ('ctx',...  41.4 us
  transfers between devices with their start and end apart: 21, of which 10 were waited for; matrix products, arithmetic and copies ran while one was open for 19% of the time, Pallas kernels for 0%

profile of v1, /device:TPU:0, one launch (start us, length us, event | category | flops | bytes accessed | tf_op | source)
XLA Modules:
  0.0 1003.2 jit_solution(14890050069471079778)
XLA Ops:
  12.4 4.6 all-to-all-start
  17.1 34.3 %all-gather.3 = bf16[4,1,1280]{2,1,0:T(2,128)(2,1)S(1)} all-gather(bf16[1,1,1280]{2,1,0:T(2,128)(2,1)S(1)} %reshape.448), channel_id=3, replica_groups=mesh['ctx'=8,'fsdp'=4] {'fsdp'}, dimensions={0}, use_global_device_ids=true | all-gather | bytes 12800 | tf_op jit(solution)/shard_map/all_gather | solution.py:254
  59.6 3.4 convolution_add_fusion.1
  64.8 2.5 reshape.411
  67.3 2.3 fusion.52
  75.0 2.0 reshape.452.q_ref
  77.0 45.0 %all-gather.10.cloned.1.call-done.kv_ref = bf16[4096,256]{1,0:T(8,128)(2,1)} async-done(((bf16[512,256]{1,0:T(8,128)(2,1)}), bf16[4096,256]{1,0:T(8,128)(2,1)}) %all-gather.10.cloned.1.call-update) | async-done | bytes 2097168 | tf_op jit(solution)/shard_map/all_gather | solution.py:302
  122.0 13.1 %attend.1 = (bf16[2,256,384]{2,1,0:T(8,128)(2,1)}, f32[2,1,768]{2,1,0:T(1,128)}) custom-call(s32[16]{0:T(128)} %pad_add_fusion.table, s32[2]{0:T(128)} %get-tuple-element.62.ids, bf16[2,256,384]{2,1,0:T(8,128)(2,1)} %reshape.452.q_ref, bf16[4096,256]{1,0:T(8,128)(2,1)} %all-gather.10.cloned.1.call-done.kv_ref), custom_call_target="tpu_custom_call" | custom-call | flops 1610612736 | bytes 2097152 | tf_op jit(solution)/shard_map/attend/pallas_call | solution.py:169
  135.1 3.5 convolution_convert_fusion.6
  139.3 14.7 %fusion.48 = (bf16[384,1,4480]{2,1,0:T(2,128)(2,1)}, bf16[384,1,4480]{2,1,0:T(2,128)(2,1)}) fusion(bf16[384,2,4480]{2,1,0:T(2,128)(2,1)} %param.17), kind=kLoop, calls=%fused_computation.168 | loop fusion | bytes 13762560 | tf_op jit(solution)/shard_map/slice | solution.py:287
  154.0 14.3 %copy.122 = bf16[384,1,4480]{0,2,1:T(8,128)(2,1)} copy(bf16[384,1,4480]{2,1,0:T(2,128)(2,1)} %get-tuple-element.63) | data formatting | bytes 6881280
  168.3 3.8 dynamic-slice_bitcast_fusion.4
  175.0 14.1 %copy.123 = bf16[384,1,4480]{0,2,1:T(8,128)(2,1)} copy(bf16[384,1,4480]{2,1,0:T(2,128)(2,1)} %get-tuple-element.64) | data formatting | bytes 6881280
  189.1 3.8 dynamic-slice_bitcast_fusion
  193.9 2.2 copy.96
  196.1 2.2 copy.101
  198.3 2.0 broadcast.214.clone.1
  206.2 2.1 broadcast.214.clone
  209.2 2.2 copy.97
  211.5 2.3 copy.98
  213.8 13.2 %collective-permute-done.2 = bf16[1,384,1120]{1,2,0:T(8,128)(2,1)} collective-permute-done((bf16[1,384,1120]{1,2,0:T(8,128)(2,1)}, bf16[1,384,1120]{1,2,0:T(8,128)(2,1)}, u32[]{:S(2)}, u32[]{:S(2)}) %collective-permute-start.2) | collective-permute-done | bytes 860192 | tf_op jit(solution)/shard_map/ppermute | solution.py:220
  227.0 2.2 copy.99
  229.2 17.7 %collective-permute-done.3 = bf16[1,384,1120]{1,2,0:T(8,128)(2,1)} collective-permute-done((bf16[1,384,1120]{1,2,0:T(8,128)(2,1)}, bf16[1,384,1120]{1,2,0:T(8,128)(2,1)}, u32[]{:S(2)}, u32[]{:S(2)}) %collective-permute-start.3) | collective-permute-done | bytes 860192 | tf_op jit(solution)/shard_map/ppermute | solution.py:220
  246.9 2.2 copy.102
  249.1 2.2 copy.103
  251.4 13.6 %collective-permute-done.5 = bf16[1,384,1120]{1,2,0:T(8,128)(2,1)} collective-permute-done((bf16[1,384,1120]{1,2,0:T(8,128)(2,1)}, bf16[1,384,1120]{1,2,0:T(8,128)(2,1)}, u32[]{:S(2)}, u32[]{:S(2)}) %collective-permute-start.5) | collective-permute-done | bytes 860192 | tf_op jit(solution)/shard_map/ppermute | solution.py:220
  264.9 2.2 copy.104
  267.2 2.3 constant_dynamic-update-slice_fusion.16
  274.4 4.8 fusion.57
  279.2 4.6 fusion.56
  283.8 6.1 multiply_convert_fusion.1
  289.9 5.1 fusion.58
  295.0 5.5 fusion.5
  300.6 28.8 %reduce-scatter.10.cloned.1.call-done = bf16[2,64,1536]{2,1,0:T(8,128)(2,1)} async-done(((bf16[2,256,1536]{2,1,0:T(8,128)(2,1)}), bf16[2,64,1536]{2,1,0:T(8,128)(2,1)}) %reduce-scatter.10.cloned.1.call-update) | async-done | bytes 393232 | tf_op jit(solution)/shard_map/reduce_scatter | solution.py:307
  330.9 2.5 fusion.19
  333.6 19.6 %all-gather.14.cloned.1.call-done = bf16[2,256,1536]{2,1,0:T(8,128)(2,1)} async-done(((bf16[2,64,1536]{2,1,0:T(8,128)(2,1)}), bf16[2,256,1536]{2,1,0:T(8,128)(2,1)}) %all-gather.14.cloned.1.call-update) | async-done | bytes 1572880 | tf_op jit(solution)/shard_map/all_gather | solution.py:312
  353.1 3.5 convolution_convert_fusion.7
  356.6 16.1 %attend_back.1 = (f32[2,256,384]{2,1,0:T(8,128)}, bf16[4096,256]{1,0:T(8,128)(2,1)}) custom-call(s32[16]{0:T(128)} %pad_add_fusion.table, s32[2]{0:T(128)} %get-tuple-element.62.ids, bf16[2,256,384]{2,1,0:T(8,128)(2,1)} %reshape.452.q_ref, bf16[4096,256]{1,0:T(8,128)(2,1)} %all-gather.10.cloned.1.call-done.kv_ref, ...), custom_call_target="tpu_custom_call" | custom-call | flops 4026531840 | bytes 4194304 | tf_op jit(solution)/shard_map/attend_back/pallas_call | solution.py:190
  372.7 3.7 convolution_convert_fusion.1
  376.4 2.1 copy.139
  378.5 4.7 all-to-all-start.2
  383.3 2.3 copy.106
  385.6 55.6 %reduce-scatter.12.cloned.1.call-done = bf16[512,256]{1,0:T(8,128)(2,1)} async-done(((bf16[4096,256]{1,0:T(8,128)(2,1)}), bf16[512,256]{1,0:T(8,128)(2,1)}) %reduce-scatter.12.cloned.1.call-update) | async-done | bytes 262160 | tf_op jit(solution)/shard_map/reduce_scatter | solution.py:340
  447.2 2.4 copy.124
  449.5 2.4 copy.125
  455.1 2.5 copy.110
  459.4 4.5 convolution_convert_fusion.4
  464.0 3.7 convolution_convert_fusion
  467.7 2.1 copy.138
  469.8 4.7 all-to-all-start.3
  474.8 3.1 fusion.1
  477.9 3.4 convolution_convert_fusion.5
  481.3 4.5 convolution_convert_fusion.3
  485.8 40.2 %all-to-all-done.3 = bf16[4,384,1120]{1,2,0:T(8,128)(2,1)} async-done(((bf16[4,384,1120]{1,2,0:T(8,128)(2,1)}), bf16[4,384,1120]{1,2,0:T(8,128)(2,1)}, u32[]{:S(2)}, u32[]{:S(2)}) %all-to-all-start.3) | async-done | bytes 3440672 | tf_op jit(solution)/shard_map/all_to_all | solution.py:210
  526.1 4.4 all-to-all-start.1
  530.5 5.5 convolution_convert_fusion.2
  536.0 6.8 pad_maximum_fusion
  544.7 10.1 %all-to-all-done.1 = bf16[4,384,640]{2,1,0:T(8,128)(2,1)} async-done(((bf16[4,384,640]{2,1,0:T(8,128)(2,1)}), bf16[4,384,640]{2,1,0:T(8,128)(2,1)}, u32[]{:S(2)}, u32[]{:S(2)}) %all-to-all-start.1) | async-done | bytes 1966112 | tf_op jit(solution)/shard_map/all_to_all | solution.py:210
  566.6 41.4 %psum.35 = f32[5120]{0:T(1024)S(1)} all-reduce(f32[5120]{0:T(1024)S(1)} %constant_dynamic-update-slice_fusion.2), channel_id=1, replica_groups=mesh['ctx'=8,'fsdp'=4] {'ctx','fsdp'}, use_global_device_ids=true, to_apply=%region_15.16 | all-reduce | flops 5120 | bytes 40960 | tf_op jit(solution)/shard_map/psum | solution.py:386
  610.0 3.3 fusion.22
  613.3 354.7 %all-reduce.3.cloned.1.call-done = (bf16[384,2,4480]{0,2,1:T(8,128)(2,1)}, bf16[384,2048]{1,0:T(8,128)(2,1)}, bf16[384,1536]{1,0:T(8,128)(2,1)}, bf16[1120,1536]{1,0:T(8,128)(2,1)}) async-done(((bf16[384,2,4480]{0,2,1:T(8,128)(2,1)}, bf16[384,2048]{1,0:T(8,128)(2,1)}, bf16[384,1536]{1,0:T(8,128)(2,1)}, bf16[1120,1536]{1,0:T(8,128)(2,1)}), (bf16[384,2,4480]{0,2,1:T(8,128)(2,1)}, bf16[384,2048]{1,0:T(8,128)(2,1)}, ...) | async-done | bytes 13074448 | tf_op jit(solution)/shard_map/psum | solution.py:395
  968.0 18.7 %copy.115 = f32[384,2,4480]{2,1,0:T(2,128)} copy(bf16[384,2,4480]{0,2,1:T(8,128)(2,1)} %get-tuple-element.57) | data formatting | bytes 20643840
  986.7 5.9 convert_element_type.248
  992.7 2.0 convert_element_type.241
  (181 shorter events, 66.4 us)
Async XLA Ops:
  7.2 267.2 %copy-start = (bf16[1120,1536]{1,0:T(8,128)(2,1)S(1)}, bf16[1120,1536]{1,0:T(8,128)(2,1)}, u32[]{:S(2)}) copy-start(bf16[1120,1536]{1,0:T(8,128)(2,1)} %param.18) | copy-start | bytes 10321924
  7.2 48.9 %all-gather.16.cloned.1.call-start = ((), (), s32[]{:S(2)}) async-start(), calls=%async_computation.17 | async-start | bytes 1966080 | tf_op jit(solution)/shard_map/all_gather | solution.py:258
  12.4 4.7 copy-start.17
  12.4 4.7 copy-start.18
  12.4 4.7 copy-start.19
  12.4 39.0 %copy-start.22 = (s32[8]{0:T(128)S(1)}, s32[8]{0:T(128)}, u32[]{:S(2)}) copy-start(s32[8]{0:T(128)} %param.11) | copy-start | bytes 100
  12.4 47.2 %all-to-all-start = ((bf16[4,384,640]{2,1,0:T(8,128)(2,1)}), bf16[4,384,640]{2,1,0:T(8,128)(2,1)}, u32[]{:S(2)}, u32[]{:S(2)}) async-start(bf16[4,384,640]{2,1,0:T(8,128)(2,1)} %pad_maximum_fusion.1), calls=%async_computation | async-start | bytes 3932160 | tf_op jit(solution)/shard_map/all_to_all | solution.py:210
  17.0 105.0 %all-gather.10.cloned.1.call-start = ((), (), s32[]{:S(2)}) async-start(), calls=%async_computation.9 | async-start | bytes 2359296 | tf_op jit(solution)/shard_map/all_gather | solution.py:302
  56.1 1.9 copy-start.1
  67.3 2.3 copy-start.11
  67.3 2.3 copy-start.12
  69.6 1.3 copy-start.15
  69.9 0.8 copy-start.2
  69.9 1.0 copy-start.3
  71.7 129.7 %reduce-scatter.6.cloned.1.call-start = ((), (), s32[]{:S(2)}) async-start(), calls=%async_computation.10 | async-start | bytes 1966080 | tf_op jit(solution)/shard_map/reduce_scatter | solution.py:307
  138.7 135.7 %all-gather.18.cloned.1.call-start = ((), (), s32[]{:S(2)}) async-start(), calls=%async_computation.18 | async-start | bytes 1966080 | tf_op jit(solution)/shard_map/all_gather | solution.py:291
  139.2 139.9 %all-gather.12.cloned.1.call-start = ((), (), s32[]{:S(2)}) async-start(), calls=%async_computation.11 | async-start | bytes 1966080 | tf_op jit(solution)/shard_map/all_gather | solution.py:312
  172.1 30.6 %collective-permute-start = (bf16[1,384,1120]{1,2,0:T(8,128)(2,1)}, bf16[1,384,1120]{1,2,0:T(8,128)(2,1)}, u32[]{:S(2)}, u32[]{:S(2)}) collective-permute-start(bf16[1,384,1120]{1,2,0:T(8,128)(2,1)} %get-tuple-element.70), channel_id=1, source_target_pairs={{0,1},{1,2},{2,3},{3,0},{4,5},{5,6},{6,7},{7,4},{8,9},{9,10},{10,1... | collective-permute-start | bytes 2580488 | tf_op jit(solution)/shard_map/ppermute | solution.py:220
  172.1 39.4 %collective-permute-start.1 = (bf16[1,384,1120]{1,2,0:T(8,128)(2,1)}, bf16[1,384,1120]{1,2,0:T(8,128)(2,1)}, u32[]{:S(2)}, u32[]{:S(2)}) collective-permute-start(bf16[1,384,1120]{1,2,0:T(8,128)(2,1)} %get-tuple-element.69), channel_id=1, source_target_pairs={{0,2},{1,3},{2,0},{3,1},{4,6},{5,7},{6,4},{7,5},{8,10},{9,11},{10,... | collective-permute-start | bytes 2580488 | tf_op jit(solution)/shard_map/ppermute | solution.py:220
  173.5 53.4 %collective-permute-start.2 = (bf16[1,384,1120]{1,2,0:T(8,128)(2,1)}, bf16[1,384,1120]{1,2,0:T(8,128)(2,1)}, u32[]{:S(2)}, u32[]{:S(2)}) collective-permute-start(bf16[1,384,1120]{1,2,0:T(8,128)(2,1)} %get-tuple-element.68), channel_id=1, source_target_pairs={{0,3},{1,0},{2,1},{3,2},{4,7},{5,4},{6,5},{7,6},{8,11},{9,8},{10,9... | collective-permute-start | bytes 2580488 | tf_op jit(solution)/shard_map/ppermute | solution.py:220
  192.9 54.0 %collective-permute-start.3 = (bf16[1,384,1120]{1,2,0:T(8,128)(2,1)}, bf16[1,384,1120]{1,2,0:T(8,128)(2,1)}, u32[]{:S(2)}, u32[]{:S(2)}) collective-permute-start(bf16[1,384,1120]{1,2,0:T(8,128)(2,1)} %get-tuple-element.74), channel_id=1, source_target_pairs={{0,1},{1,2},{2,3},{3,0},{4,5},{5,6},{6,7},{7,4},{8,9},{9,10},{10,1... | collective-permute-start | bytes 2580488 | tf_op jit(solution)/shard_map/ppermute | solution.py:220
  193.2 55.9 %collective-permute-start.4 = (bf16[1,384,1120]{1,2,0:T(8,128)(2,1)}, bf16[1,384,1120]{1,2,0:T(8,128)(2,1)}, u32[]{:S(2)}, u32[]{:S(2)}) collective-permute-start(bf16[1,384,1120]{1,2,0:T(8,128)(2,1)} %get-tuple-element.73), channel_id=1, source_target_pairs={{0,2},{1,3},{2,0},{3,1},{4,6},{5,7},{6,4},{7,5},{8,10},{9,11},{10,... | collective-permute-start | bytes 2580488 | tf_op jit(solution)/shard_map/ppermute | solution.py:220
  198.3 2.1 copy-start.10
  202.7 62.3 %collective-permute-start.5 = (bf16[1,384,1120]{1,2,0:T(8,128)(2,1)}, bf16[1,384,1120]{1,2,0:T(8,128)(2,1)}, u32[]{:S(2)}, u32[]{:S(2)}) collective-permute-start(bf16[1,384,1120]{1,2,0:T(8,128)(2,1)} %get-tuple-element.72), channel_id=1, source_target_pairs={{0,3},{1,0},{2,1},{3,2},{4,7},{5,4},{6,5},{7,6},{8,11},{9,8},{10,9... | collective-permute-start | bytes 2580488 | tf_op jit(solution)/shard_map/ppermute | solution.py:220
  206.2 123.2 %reduce-scatter.10.cloned.1.call-start = ((), (), s32[]{:S(2)}) async-start(), calls=%async_computation.13 | async-start | bytes 1966080 | tf_op jit(solution)/shard_map/reduce_scatter | solution.py:307
  206.2 2.1 copy-start.4
  267.2 2.3 copy-start.5
  267.2 3.3 copy-start.6
  269.5 2.0 copy-start.7
  270.4 2.0 copy-start.8
  271.4 2.0 copy-start.9
  279.1 4.6 copy-start.20
  279.1 4.6 copy-start.26
  289.9 5.1 copy-start.24
  289.9 5.1 copy-start.23
  300.5 52.6 %all-gather.14.cloned.1.call-start = ((), (), s32[]{:S(2)}) async-start(), calls=%async_computation.14 | async-start | bytes 1966080 | tf_op jit(solution)/shard_map/all_gather | solution.py:312
  333.4 107.9 %reduce-scatter.12.cloned.1.call-start = ((), (), s32[]{:S(2)}) async-start(), calls=%async_computation.15 | async-start | bytes 2359296 | tf_op jit(solution)/shard_map/reduce_scatter | solution.py:340
  378.5 91.3 %all-to-all-start.2 = ((bf16[4,384,1120]{1,2,0:T(8,128)(2,1)}), bf16[4,384,1120]{1,2,0:T(8,128)(2,1)}, u32[]{:S(2)}, u32[]{:S(2)}) async-start(bf16[4,384,1120]{1,2,0:T(8,128)(2,1)} %bitcast.183), calls=%async_computation.7 | async-start | bytes 6881280 | tf_op jit(solution)/shard_map/all_to_all | solution.py:210
  383.3 181.6 %reduce-scatter.14.cloned.1.call-start = ((), (), s32[]{:S(2)}) async-start(), calls=%async_computation.16 | async-start | bytes 1966080 | tf_op jit(solution)/shard_map/reduce_scatter | solution.py:307
  469.8 56.3 %all-to-all-start.3 = ((bf16[4,384,1120]{1,2,0:T(8,128)(2,1)}), bf16[4,384,1120]{1,2,0:T(8,128)(2,1)}, u32[]{:S(2)}, u32[]{:S(2)}) async-start(bf16[4,384,1120]{1,2,0:T(8,128)(2,1)} %bitcast.184), calls=%async_computation.8 | async-start | bytes 6881280 | tf_op jit(solution)/shard_map/all_to_all | solution.py:210
  474.5 135.4 %reduce-scatter.8.cloned.1.call-start = ((), (), s32[]{:S(2)}) async-start(), calls=%async_computation.12 | async-start | bytes 1966080 | tf_op jit(solution)/shard_map/reduce_scatter | solution.py:307
  474.8 3.1 copy-start.25
  526.1 28.8 %all-to-all-start.1 = ((bf16[4,384,640]{2,1,0:T(8,128)(2,1)}), bf16[4,384,640]{2,1,0:T(8,128)(2,1)}, u32[]{:S(2)}, u32[]{:S(2)}) async-start(bf16[4,384,640]{2,1,0:T(8,128)(2,1)} %bitcast.192), calls=%async_computation.6 | async-start | bytes 3932160 | tf_op jit(solution)/shard_map/all_to_all | solution.py:210
  530.5 437.5 %all-reduce.3.cloned.1.call-start = ((), (), s32[]{:S(2)}) async-start(), calls=%async_computation.19 | async-start | bytes 26148864 | tf_op jit(solution)/shard_map/psum | solution.py:395
  536.0 6.8 copy-start.16
  536.0 6.8 copy-start.21
  986.7 6.0 copy-start.13
  992.7 2.0 copy-start.14
Sparse Core Ops, SparseCore 0:
  9.6 30.8 all-gather.15
  71.8 50.1 all-gather.9
  138.8 26.4 reduce-scatter.5
  166.7 28.1 all-gather.17
  206.3 26.7 all-gather.11
  300.6 28.6 reduce-scatter.9
  333.5 19.6 all-gather.13
  372.8 68.3 reduce-scatter.11
  464.1 35.5 reduce-scatter.13
  502.1 30.4 reduce-scatter.7
  562.3 405.7 all-reduce.2

commit v2 on v1

--- a/solution.py
+++ b/solution.py
@@ -206,20 +206,468 @@
     )(table, ids, query, keys_values, out, d_out, lse)
 
 
+MESH = pl.DeviceIdType.MESH
+
+
+def greet(devices):
+    barrier = pltpu.get_barrier_semaphore()
+    for device in devices:
+        pl.semaphore_signal(barrier, inc=1, device_id=device, device_id_type=MESH)
+    pl.semaphore_wait(barrier, len(devices))
+
+
+def remote(src, dst, send, recv, device):
+    return pltpu.make_async_remote_copy(
+        src_ref=src, dst_ref=dst, send_sem=send, recv_sem=recv, device_id=device, device_id_type=MESH
+    )
+
+
+def group_places(n):
+    ctx = lax.axis_index("ctx")
+    me = lax.axis_index("fsdp")
+    partner = me + 1 - 2 * (me % 2)
+    others = [(me + 2 * k) % n for k in range(1, n // 2)]
+    senders = [(me + n - 2 * k) % n for k in range(1, n // 2)]
+    return ctx, me, partner, others, senders
+
+
+def sum_kernel(mode, n, cuts, *refs):
+    gathers = mode != "input"
+    if mode == "attention":
+        partial, tokens, gain, hidden_out, all_out = refs[:5]
+    elif mode == "mlp":
+        partial, hidden_in, cot, gain, d_out, all_out, d_gain = refs[:7]
+    else:
+        partial, tokens, d_hidden_in, gain, d_out, d_gain = refs[:6]
+    near, summed, far, stage, near_s, near_r, far_s, far_r, own_s, own_r, out_s, out_r, fwd_s, fwd_r = refs[-14:]
+    ctx, me, partner, others, senders = group_places(n)
+    chips = n // 2
+    rows = partial.shape[2]
+    piece = rows // cuts
+    chunks = [(w, i * piece) for w in range(2) for i in range(cuts)]
+    greet([(ctx, partner)] + [(ctx, o) for o in others])
+
+    def part(ref, w, lead, start):
+        return ref.at[w, lead, pl.ds(start, piece)]
+
+    first = []
+    for c, (w, start) in enumerate(chunks):
+        for j in range(chips):
+            target = (partner + 2 * (j + 1)) % n
+            copy = remote(
+                part(partial, w, target, start),
+                part(near, w, j, start),
+                near_s.at[c, j],
+                near_r.at[c, j],
+                (ctx, partner),
+            )
+            copy.start()
+            first.append(copy)
+
+    second = []
+
+    def post(c):
+        w, start = chunks[c]
+        for j in range(chips - 1):
+            copy = remote(
+                part(summed, w, j, start),
+                part(far, w, j, start),
+                far_s.at[c, j],
+                far_r.at[c, j],
+                (ctx, others[j]),
+            )
+            copy.start()
+            second.append(copy)
+
+    for c, (w, start) in enumerate(chunks):
+        span = pl.ds(start, piece)
+        for j in range(chips - 1):
+            first[c * chips + j].wait()
+            target = (me + 2 * (j + 1)) % n
+            summed[w, j, span] = (
+                partial[w, target, span].astype(F32) + near[w, j, span].astype(F32)
+            ).astype(BF16)
+        if c:
+            post(c - 1)
+    post(len(chunks) - 1)
+
+    if mode != "attention":
+        d_gain[...] = jnp.zeros_like(d_gain)
+    third = []
+
+    def spread(c):
+        w, start = chunks[c]
+        src = stage.at[w, pl.ds(start, piece)]
+        for k in range(chips - 1):
+            copy = remote(src, part(all_out, w, me, start), out_s.at[c, k], out_r.at[c, k], (ctx, others[k]))
+            copy.start()
+            third.append(copy)
+        copy = remote(src, part(all_out, w, me, start), own_s.at[c], own_r.at[c], (ctx, partner))
+        copy.start()
+        return copy
+
+    near_copies = []
+    for c, (w, start) in enumerate(chunks):
+        span = pl.ds(start, piece)
+        first[c * chips + chips - 1].wait()
+        total = partial[w, me, span].astype(F32) + near[w, chips - 1, span].astype(F32)
+        for j in range(chips - 1):
+            second[c * (chips - 1) + j].wait()
+            total += far[w, j, span].astype(F32)
+        if mode == "attention":
+            hidden = tokens[w, span].astype(F32) + total
+            hidden_out[w, span] = hidden
+            rounded = (hidden * rms_scale(hidden) * gain[...]).astype(BF16)
+        elif mode == "mlp":
+            hidden = hidden_in[w, span]
+            d_norm, gain_part = rms_backward(hidden, rms_scale(hidden), gain[...], total)
+            d_gain[...] += gain_part[None]
+            d_hidden = cot[w, span].astype(F32) + d_norm
+            d_out[w, span] = d_hidden
+            rounded = d_hidden.astype(BF16)
+        else:
+            values = tokens[w, span].astype(F32)
+            d_norm, gain_part = rms_backward(values, rms_scale(values), gain[...], total)
+            d_gain[...] += gain_part[None]
+            d_out[w, span] = d_hidden_in[w, span] + d_norm
+        if gathers:
+            stage[w, span] = rounded
+            all_out[w, me, span] = rounded
+            if c:
+                near_copies.append(spread(c - 1))
+    if not gathers:
+        return
+    near_copies.append(spread(len(chunks) - 1))
+
+    forwards = []
+    for c, (w, start) in enumerate(chunks):
+        for k in range(chips - 1):
+            third[c * (chips - 1) + k].wait_recv()
+            block = part(all_out, w, senders[k], start)
+            copy = remote(block, block, fwd_s.at[c, k], fwd_r.at[c, k], (ctx, partner))
+            copy.start()
+            forwards.append(copy)
+    for copy in third:
+        copy.wait_send()
+    for copy in near_copies + forwards:
+        copy.wait()
+
+
+def group_sum(mode, partial, *operands, collective):
+    _, n, rows, width = partial.shape
+    cuts = 2
+    chunks = 2 * cuts
+    chips = n // 2
+    row_shape = (2, rows, width)
+    full = jax.ShapeDtypeStruct(row_shape, F32)
+    gathered = jax.ShapeDtypeStruct(partial.shape, BF16)
+    gain_sum = jax.ShapeDtypeStruct((1, width), F32)
+    out_shape = {
+        "attention": (full, gathered),
+        "mlp": (full, gathered, gain_sum),
+        "input": (full, gain_sum),
+    }[mode]
+    dma = pltpu.SemaphoreType.DMA
+    return pl.pallas_call(
+        functools.partial(sum_kernel, mode, n, cuts),
+        out_shape=out_shape,
+        in_specs=in_vmem(1 + len(operands)),
+        out_specs=tuple(in_vmem(len(out_shape))),
+        scratch_shapes=[
+            pltpu.VMEM((2, chips, rows, width), BF16),
+            pltpu.VMEM((2, chips - 1, rows, width), BF16),
+            pltpu.VMEM((2, chips - 1, rows, width), BF16),
+            pltpu.VMEM(row_shape, BF16),
+            dma((chunks, chips)),
+            dma((chunks, chips)),
+            dma((chunks, chips - 1)),
+            dma((chunks, chips - 1)),
+            dma((chunks,)),
+            dma((chunks,)),
+            dma((chunks, chips - 1)),
+            dma((chunks, chips - 1)),
+            dma((chunks, chips - 1)),
+            dma((chunks, chips - 1)),
+        ],
+        compiler_params=pltpu.CompilerParams(
+            vmem_limit_bytes=VMEM_LIMIT, collective_id=collective, has_side_effects=True
+        ),
+        cost_estimate=pl.CostEstimate(
+            flops=20 * rows * width, bytes_accessed=60_000_000, transcendentals=0
+        ),
+        name="group_sum_" + mode,
+    )(partial, *operands)
+
+
+def ring_index(place, n):
+    late = place // (n // 2)
+    return (1 - late) * 2 * place + late * (2 * n - 1 - 2 * place)
+
+
+def ring_place(index, n):
+    odd = index % 2
+    return (1 - odd) * (index // 2) + odd * (n - 1 - index // 2)
+
+
+def share_kernel(n, own, out, right_s, right_r, left_s, left_r, near_s, near_r):
+    ctx = lax.axis_index("ctx")
+    me = lax.axis_index("fsdp")
+    which = me % 2
+    partner = me + 1 - 2 * which
+    place = ring_place(ctx, n)
+    right = (ring_index((place + 1) % n, n), me)
+    left = (ring_index((place + n - 1) % n, n), me)
+    greet([right, left, (ctx, partner)])
+
+    def block(offset):
+        return out.at[ring_index((place + n + offset) % n, n), which]
+
+    def to_right(step):
+        src = own.at[which] if step == 0 else block(-step)
+        return remote(src, block(-step), right_s.at[step], right_r.at[step], right)
+
+    def to_left(step):
+        src = own.at[which] if step == 0 else block(step)
+        return remote(src, block(step), left_s.at[step], left_r.at[step], left)
+
+    rights, lefts = n // 2, n - 1 - n // 2
+    sent = [to_right(0), to_left(0)]
+    for copy in sent:
+        copy.start()
+    out[ctx] = own[...]
+    going = [sent[0], sent[1]]
+    for step in range(1, rights + 1):
+        going[0].wait_recv()
+        if step < rights:
+            going[0] = to_right(step)
+            going[0].start()
+            sent.append(going[0])
+        hand = remote(block(-step), block(-step), near_s.at[step - 1], near_r.at[step - 1], (ctx, partner))
+        hand.start()
+        sent.append(hand)
+        if step <= lefts:
+            going[1].wait_recv()
+            if step < lefts:
+                going[1] = to_left(step)
+                going[1].start()
+                sent.append(going[1])
+            slot = rights + step - 1
+            hand = remote(block(step), block(step), near_s.at[slot], near_r.at[slot], (ctx, partner))
+            hand.start()
+            sent.append(hand)
+    for copy in sent:
+        copy.wait_send()
+    for step in range(1, rights + 1):
+        remote(block(-step), block(-step), near_s.at[step - 1], near_r.at[step - 1], (ctx, partner)).wait_recv()
+    for step in range(1, lefts + 1):
+        slot = rights + step - 1
+        remote(block(step), block(step), near_s.at[slot], near_r.at[slot], (ctx, partner)).wait_recv()
+
+
+def share_keys(own, n, collective):
+    dma = pltpu.SemaphoreType.DMA
+    return pl.pallas_call(
+        functools.partial(share_kernel, n),
+        out_shape=jax.ShapeDtypeStruct((n,) + own.shape, BF16),
+        in_specs=in_vmem(1),
+        out_specs=in_vmem(1)[0],
+        scratch_shapes=[dma((n // 2,))] * 4 + [dma((n - 1,))] * 2,
+        compiler_params=pltpu.CompilerParams(
+            vmem_limit_bytes=VMEM_LIMIT, collective_id=collective, has_side_effects=True
+        ),
+        cost_estimate=pl.CostEstimate(flops=0, bytes_accessed=60_000_000, transcendentals=0),
+        name="share_keys",
+    )(own)
+
+
+def return_kernel(n, partial, out, near, summed, far, near_s, near_r, far_s, far_r):
+    ctx = lax.axis_index("ctx")
+    me = lax.axis_index("fsdp")
+    which = me % 2
+    partner = me + 1 - 2 * which
+    others = [(ctx + k) % n for k in range(1, n)]
+    greet([(ctx, partner)] + [(o, me) for o in others])
+    order = others + [ctx]
+    first = []
+    for k, target in enumerate(order):
+        copy = remote(partial.at[target, 1 - which], near.at[k], near_s.at[k], near_r.at[k], (ctx, partner))
+        copy.start()
+        first.append(copy)
+    second = []
+
+    def post(k):
+        copy = remote(summed.at[k], far.at[k], far_s.at[k], far_r.at[k], (others[k], me))
+        copy.start()
+        second.append(copy)
+
+    for k in range(n - 1):
+        first[k].wait()
+        summed[k] = (partial[others[k], which].astype(F32) + near[k].astype(F32)).astype(BF16)
+        if k:
+            post(k - 1)
+    post(n - 2)
+    out[1 - which] = jnp.zeros(out.shape[1:], F32)
+    first[n - 1].wait()
+    out[which] = partial[ctx, which].astype(F32) + near[n - 1].astype(F32)
+    for k in range(n - 1):
+        second[k].wait()
+        out[which] += far[k].astype(F32)
+
+
+def return_grads(partial, collective):
+    n = partial.shape[0]
+    block = partial.shape[2:]
+    dma = pltpu.SemaphoreType.DMA
+    return pl.pallas_call(
+        functools.partial(return_kernel, n),
+        out_shape=jax.ShapeDtypeStruct(partial.shape[1:], F32),
+        in_specs=in_vmem(1),
+        out_specs=in_vmem(1)[0],
+        scratch_shapes=[
+            pltpu.VMEM((n,) + block, BF16),
+            pltpu.VMEM((n - 1,) + block, BF16),
+            pltpu.VMEM((n - 1,) + block, BF16),
+            dma((n,)),
+            dma((n,)),
+            dma((n - 1,)),
+            dma((n - 1,)),
+        ],
+        compiler_params=pltpu.CompilerParams(
+            vmem_limit_bytes=VMEM_LIMIT, collective_id=collective, has_side_effects=True
+        ),
+        cost_estimate=pl.CostEstimate(flops=0, bytes_accessed=80_000_000, transcendentals=0),
+        name="return_grads",
+    )(partial)
+
+
+def vector_kernel(n_ctx, n, parts, out, near, summed, far, near_s, near_r, far_s, far_r):
+    ctx = lax.axis_index("ctx")
+    me = lax.axis_index("fsdp")
+    members = [(me + k) % n for k in range(1, n)]
+    others = [(ctx + k) % n_ctx for k in range(1, n_ctx)]
+    greet([(ctx, m) for m in members] + [(o, me) for o in others])
+    first = []
+    for k in range(n - 1):
+        copy = remote(parts.at[members[k]], near.at[k], near_s.at[k], near_r.at[k], (ctx, members[k]))
+        copy.start()
+        first.append(copy)
+    total = parts[me]
+    for k in range(n - 1):
+        first[k].wait()
+        total += near[k]
+    summed[...] = total
+    second = []
+    for k in range(n_ctx - 1):
+        copy = remote(summed, far.at[k], far_s.at[k], far_r.at[k], (others[k], me))
+        copy.start()
+        second.append(copy)
+    for k in range(n_ctx - 1):
+        second[k].wait()
+        total += far[k]
+    out[...] = total
+
+
+def vector_sum(parts, n_ctx, collective):
+    n = parts.shape[0]
+    block = parts.shape[1:]
+    dma = pltpu.SemaphoreType.DMA
+    return pl.pallas_call(
+        functools.partial(vector_kernel, n_ctx, n),
+        out_shape=jax.ShapeDtypeStruct(block, F32),
+        in_specs=in_vmem(1),
+        out_specs=in_vmem(1)[0],
+        scratch_shapes=[
+            pltpu.VMEM((n - 1,) + block, F32),
+            pltpu.VMEM(block, F32),
+            pltpu.VMEM((n_ctx - 1,) + block, F32),
+            dma((n - 1,)),
+            dma((n - 1,)),
+            dma((n_ctx - 1,)),
+            dma((n_ctx - 1,)),
+        ],
+        compiler_params=pltpu.CompilerParams(
+            vmem_limit_bytes=VMEM_LIMIT, collective_id=collective, has_side_effects=True
+        ),
+        cost_estimate=pl.CostEstimate(flops=0, bytes_accessed=30_000_000, transcendentals=0),
+        name="vector_sum",
+    )(parts)
+
+
+def ring_pairs(n, step):
+    return [(ring_index(p, n), ring_index((p + step) % n, n)) for p in range(n)]
+
+
+def ring_begin(chunks, take, step):
+    n = lax.axis_size("ctx")
+    place = ring_place(lax.axis_index("ctx"), n)
+    return take(chunks, (place + n - step) % n)
+
+
+def ring_send(held, step):
+    pairs = ring_pairs(lax.axis_size("ctx"), step)
+    return jax.tree.map(lambda a: lax.ppermute(a, "ctx", pairs), held)
+
+
+def ring_add(arrived, chunks, take, step, hop):
+    n = lax.axis_size("ctx")
+    place = ring_place(lax.axis_index("ctx"), n)
+    mine = take(chunks, (place + n * n - step * (hop + 1)) % n)
+    return jax.tree.map(lambda a, b: (a.astype(F32) + b.astype(F32)).astype(BF16), arrived, mine)
+
+
+class RingSum:
+    def __init__(self, right, left, take):
+        self.sides = [(right, 1), (left, -1)]
+        self.take = take
+        self.held = [ring_begin(chunks, take, step) for chunks, step in self.sides]
+        self.hop = 0
+        self.hops = lax.axis_size("ctx") - 1
+
+    def beside(self, *values):
+        if self.hop == self.hops:
+            return values
+        self.hop += 1
+        arrived = [ring_send(h, step) for h, (_, step) in zip(self.held, self.sides)]
+        if values:
+            arrived, *values = together(arrived, *values)
+        self.held = [
+            ring_add(a, chunks, self.take, step, self.hop)
+            for a, (chunks, step) in zip(arrived, self.sides)
+        ]
+        return values
+
+    def finish(self):
+        while self.hop < self.hops:
+            self.beside()
+        return self.held
+
+
+def ring_gather(own, halves, joined):
+    n = lax.axis_size("ctx")
+    place = ring_place(lax.axis_index("ctx"), n)
+    out = jnp.zeros((n,) + own.shape, F32)
+
+    def put(out, block, q):
+        return lax.dynamic_update_index_in_dim(out, block.astype(F32), q % n, 0)
+
+    out = put(out, own, place)
+    right = left = own
+    for hop in range(1, n // 2):
+        right = lax.ppermute(right, "ctx", ring_pairs(n, 1))
+        out = put(out, right, place + n - hop)
+        left = lax.ppermute(left, "ctx", ring_pairs(n, -1))
+        out = put(out, left, place + hop)
+    right = lax.ppermute(halves(right)[0], "ctx", ring_pairs(n, 1))
+    left = lax.ppermute(halves(left)[1], "ctx", ring_pairs(n, -1))
+    return put(out, joined(right, left), place + n // 2)
+
+
 def exchange(pieces, axis):
     return lax.all_to_all(pieces, axis, split_axis=0, concat_axis=0, tiled=True)
 
 
-def exchange_async(pieces, axis):
-    n = pieces.shape[0]
-    me = lax.axis_index(axis)
-    own = lax.dynamic_index_in_dim(pieces, me, 0, keepdims=True)
-    arrived = lax.dynamic_update_slice_in_dim(jnp.zeros_like(pieces), own, me, 0)
-    for shift in range(1, n):
-        piece = lax.dynamic_index_in_dim(pieces, (me + shift) % n, 0, keepdims=True)
-        piece = lax.ppermute(piece, axis, [(i, (i + shift) % n) for i in range(n)])
-        arrived = lax.dynamic_update_slice_in_dim(arrived, piece, (me + n - shift) % n, 0)
-    return arrived
+def together(*values):
+    return lax.optimization_barrier(values)
 
 
 def body(tokens, pairing, gain_attn, w_qkv, b_qkv, w_out, gain_mlp, w_gate_up, w_down, cotangent):
@@ -252,6 +700,7 @@
     my_kv = fsdp_index * KV_HEADS // n_fsdp
 
     small = lax.all_gather(jnp.concatenate([gain_attn, gain_mlp, b_qkv]), "fsdp", axis=0)
+    small, w_qkv, w_gate_up = together(small, w_qkv, w_gate_up)
     gain_one = small[:, :d_shard].reshape(D).astype(F32)
     gain_two = small[:, d_shard : 2 * d_shard].reshape(D).astype(F32)
     bias = small[:, 2 * d_shard :].reshape(-1).astype(F32)
@@ -282,11 +731,12 @@
             lax.dynamic_slice_in_dim(bias, q_width + kv_width + my_kv * HEAD_DIM, HEAD_DIM),
         ]
     )
+    gate_up_pieces = [
+        w_gate_up[:, e].reshape(d_shard, n_fsdp, ff_shard).transpose(1, 0, 2) for e in range(2)
+    ]
+    x_all, w_qkv_cols, gate_up_pieces = together(x_all, w_qkv_cols, gate_up_pieces)
     w_gate_cols, w_up_cols = (
-        exchange_async(
-            w_gate_up[:, e].reshape(d_shard, n_fsdp, ff_shard).transpose(1, 0, 2), "fsdp"
-        ).reshape(D, ff_shard)
-        for e in range(2)
+        exchange(pieces, "fsdp").reshape(D, ff_shard) for pieces in gate_up_pieces
     )
     cot_all = lax.all_gather(cotangent[0], "fsdp", axis=1, tiled=True).reshape(rows, D)
 
@@ -299,7 +749,8 @@
     ).astype(BF16)
     query = rotated[:, :heads].reshape(2, stretch_len, q_cols)
     own_kv = jnp.concatenate([rotated[:, heads], qkv[:, q_cols + HEAD_DIM :].astype(BF16)], 1)
-    keys_values = lax.all_gather(own_kv, "ctx", axis=0, tiled=True)
+    keys_values = share_keys(own_kv.reshape(2, stretch_len, 2 * HEAD_DIM), n_ctx, 4)
+    keys_values = keys_values.reshape(n_ctx * rows, 2 * HEAD_DIM)
     attended, lse = attend(table, ids, query, keys_values, heads)
     attended16 = attended.reshape(rows, q_cols)
 
@@ -308,62 +759,29 @@
             partial.astype(BF16).reshape(2, stretch_len, D), "fsdp", scatter_dimension=1, tiled=True
         ).astype(F32).reshape(local_count, D)
 
-    def gather(own):
-        return lax.all_gather(
-            own.reshape(2, half_rows, D), "fsdp", axis=1, tiled=True
-        ).reshape(rows, D)
-
-    inputs = tokens.reshape(local_count, D).astype(F32)
-    scale_one = rms_scale(inputs)
-    hidden = inputs + scatter(jnp.dot(attended16, w_out, preferred_element_type=F32))
-    scale_two = rms_scale(hidden)
-    normed2 = gather((hidden * scale_two * gain_two).astype(BF16))
+    def by_member(partial):
+        return partial.astype(BF16).reshape(2, n_fsdp, half_rows, D)
+
+    tokens_own = tokens[0]
+    hidden, normed2 = group_sum(
+        "attention",
+        by_member(jnp.dot(attended16, w_out, preferred_element_type=F32)),
+        tokens_own,
+        gain_two[None],
+        collective=1,
+    )
+    normed2 = normed2.reshape(rows, D)
     gate_val = jnp.dot(normed2, w_gate_cols, preferred_element_type=F32)
     up_val = jnp.dot(normed2, w_up_cols, preferred_element_type=F32)
     sigmoid_gate = jax.nn.sigmoid(gate_val)
     act16 = (jax.nn.silu(gate_val) * up_val).astype(BF16)
-    result = hidden + scatter(jnp.dot(act16, w_down, preferred_element_type=F32))
+    result = hidden.reshape(local_count, D) + scatter(jnp.dot(act16, w_down, preferred_element_type=F32))
     block_output = result.astype(BF16).reshape(tokens.shape)
 
     d_act = contract_cols(cot_all, w_down)
     d_gate16 = (d_act * up_val * sigmoid_gate * (1.0 + gate_val * (1.0 - sigmoid_gate))).astype(BF16)
     d_up16 = (d_act * gate_val * sigmoid_gate).astype(BF16)
-    d_normed2 = scatter(contract_cols(d_gate16, w_gate_cols) + contract_cols(d_up16, w_up_cols))
-    cot = cotangent.reshape(local_count, D).astype(F32)
-    d_hidden_norm, d_gain_two = rms_backward(hidden, scale_two, gain_two, d_normed2)
-    d_hidden = cot + d_hidden_norm
-    dh_all = gather(d_hidden.astype(BF16))
-    d_attended16 = contract_cols(dh_all, w_out).astype(BF16).reshape(2, stretch_len, q_cols)
-    d_query, d_kv = attend_back(
-        table, ids, query, keys_values, attended, d_attended16, lse, heads
-    )
-    d_kv_own = lax.psum_scatter(d_kv, "ctx", scatter_dimension=0, tiled=True).astype(F32)
-
-    d_w_down = contract_rows(act16, cot_all).astype(BF16)
-    d_w_gate, d_w_up = (
-        exchange(contract_rows(normed2, piece).astype(BF16).reshape(n_fsdp, d_shard, ff_shard), "fsdp")
-        for piece in (d_gate16, d_up16)
-    )
-    d_w_gate_up = jnp.stack(
-        [piece.transpose(1, 0, 2).reshape(d_shard, n_fsdp * ff_shard) for piece in (d_w_gate, d_w_up)], 1
-    )
-    d_w_out = contract_rows(attended16, dh_all).astype(BF16)
-
-    d_rotated = jnp.concatenate([d_query.reshape(rows, q_cols), d_kv_own[:, :HEAD_DIM]], 1)
-    d_rotated = unrotate(
-        d_rotated.reshape(rows, heads + 1, HEAD_DIM), cosines, sines
-    ).reshape(rows, q_cols + HEAD_DIM)
-    d_qkv = jnp.concatenate([d_rotated, d_kv_own[:, HEAD_DIM:]], 1)
-    d_bias = jnp.sum(d_qkv, 0)
-    d_qkv16 = d_qkv.astype(BF16)
-    d_normed1 = scatter(contract_cols(d_qkv16, w_qkv_cols))
-    d_input_norm, d_gain_one = rms_backward(inputs, scale_one, gain_one, d_normed1)
-    d_tokens = (d_hidden + d_input_norm).reshape(tokens.shape)
-
-    d_w_pieces = exchange(
-        contract_rows(normed1, d_qkv16).astype(BF16).reshape(n_fsdp, d_shard, -1), "fsdp"
-    )
-
+    d_normed2 = contract_cols(d_gate16, w_gate_cols) + contract_cols(d_up16, w_up_cols)
     def by_columns(pieces):
         queries = [pieces[f][..., :q_cols] for f in range(n_fsdp)]
         rest = []
@@ -379,31 +797,113 @@
                 )
         return jnp.concatenate(queries + rest, -1)
 
-    d_w_qkv = by_columns([d_w_pieces[f] for f in range(n_fsdp)])
+    chunk_rows = d_shard // n_ctx
+    down_rows = -(-ff_shard // (16 * n_ctx)) * 16
+    side = D // 2
+
+    def padded(grad):
+        extra = n_ctx * down_rows - grad.shape[0]
+        return jnp.pad(grad, ((0, extra), (0, 0))).astype(BF16).reshape(n_ctx, down_rows, D)
+
+    d_w_down = padded(contract_rows(act16, cot_all))
+    d_w_gate, d_w_up = (
+        contract_rows(normed2, piece).astype(BF16).reshape(n_fsdp, n_ctx, chunk_rows, ff_shard)
+        for piece in (d_gate16, d_up16)
+    )
+
+    def take(arrays, q):
+        return (
+            lax.dynamic_index_in_dim(arrays[0], q, 1, keepdims=False),
+            lax.dynamic_index_in_dim(arrays[1], q, 0, keepdims=False),
+        )
+
+    mlp_ring = RingSum((d_w_gate, d_w_down[..., :side]), (d_w_up, d_w_down[..., side:]), take)
+    d_hidden, dh_all, d_gain_two = group_sum(
+        "mlp", by_member(d_normed2), hidden, cotangent[0], gain_two[None], collective=2
+    )
+    d_hidden, dh_all, d_gain_two = mlp_ring.beside(d_hidden, dh_all, d_gain_two)
+    dh_all = dh_all.reshape(rows, D)
+    d_attended16 = contract_cols(dh_all, w_out).astype(BF16).reshape(2, stretch_len, q_cols)
+    d_query, d_kv = attend_back(
+        table, ids, query, keys_values, attended, d_attended16, lse, heads
+    )
+    d_query, d_kv = mlp_ring.beside(d_query, d_kv)
+    d_kv_own = return_grads(d_kv.reshape(n_ctx, 2, stretch_len, 2 * HEAD_DIM), 5).reshape(rows, -1)
+    d_kv_own, d_query = mlp_ring.beside(d_kv_own, d_query)
+
+    d_w_out = contract_rows(attended16, dh_all).astype(BF16).reshape(n_ctx, chunk_rows, D)
+    d_rotated = jnp.concatenate([d_query.reshape(rows, q_cols), d_kv_own[:, :HEAD_DIM]], 1)
+    d_rotated = unrotate(
+        d_rotated.reshape(rows, heads + 1, HEAD_DIM), cosines, sines
+    ).reshape(rows, q_cols + HEAD_DIM)
+    d_qkv = jnp.concatenate([d_rotated, d_kv_own[:, HEAD_DIM:]], 1)
+    d_bias = jnp.sum(d_qkv, 0)
+    d_qkv16 = d_qkv.astype(BF16)
+    d_normed1 = by_member(contract_cols(d_qkv16, w_qkv_cols))
+    d_normed1, d_qkv16, d_bias = mlp_ring.beside(d_normed1, d_qkv16, d_bias)
+    d_tokens, d_gain_one = group_sum(
+        "input",
+        d_normed1,
+        tokens_own,
+        d_hidden,
+        gain_one[None],
+        collective=3,
+    )
+    d_tokens, d_gain_one = mlp_ring.beside(d_tokens, d_gain_one)
+    d_tokens = d_tokens.reshape(tokens.shape)
 
     zeros = jnp.zeros_like(d_bias)
     d_bias_full = by_columns([jnp.where(fsdp_index == f, d_bias, zeros) for f in range(n_fsdp)])
-    vector = lax.psum(
-        jnp.concatenate([d_gain_one, d_gain_two, d_bias_full]), ("ctx", "fsdp")
-    )
-    d_gain_attn = lax.dynamic_slice_in_dim(vector[:D], fsdp_index * d_shard, d_shard)
-    d_gain_mlp = lax.dynamic_slice_in_dim(vector[D : 2 * D], fsdp_index * d_shard, d_shard)
-    b_shard = b_qkv.shape[0]
-    d_b_qkv = lax.dynamic_slice_in_dim(vector[2 * D :], fsdp_index * b_shard, b_shard)
-
-    def total(partial):
-        return lax.psum(partial, "ctx").astype(F32)
+    parts = jnp.concatenate(
+        [v.reshape(n_fsdp, -1, HEAD_DIM) for v in (d_gain_one, d_gain_two, d_bias_full)], 1
+    )
+    parts = jnp.pad(parts, ((0, 0), (0, -parts.shape[1] % 8), (0, 0)))
+    vector = vector_sum(parts, n_ctx, 6)
+    d_w_qkv = contract_rows(normed1, d_qkv16).astype(BF16).reshape(n_fsdp, n_ctx, chunk_rows, -1)
+    vector, d_w_qkv, d_w_out = mlp_ring.beside(vector, d_w_qkv, d_w_out)
+    vector = vector.reshape(-1)
+    (gate_sum, down_left), (up_sum, down_right) = mlp_ring.finish()
+    gate_sum, up_sum, d_w_qkv, d_w_out = together(gate_sum, up_sum, d_w_qkv, d_w_out)
+    gate_up_sum = exchange(jnp.stack([gate_sum, up_sum], 1), "fsdp")
+    gate_up_sum = gate_up_sum.transpose(2, 1, 0, 3).reshape(chunk_rows, 2, n_fsdp * ff_shard)
+
+    def halves(block):
+        middle = block.shape[-1] // 2
+        return block[..., :middle], block[..., middle:]
+
+    def joined(first, second):
+        return jnp.concatenate([first, second], -1)
+
+    d_w_gate_up = ring_gather(gate_up_sum, halves, joined).reshape(d_shard, 2, n_fsdp * ff_shard)
+    d_w_down = ring_gather(joined(down_left, down_right), halves, joined)
+    d_w_down = d_w_down.reshape(n_ctx * down_rows, D)[:ff_shard]
+
+    ring = RingSum(
+        (d_w_qkv[..., :q_cols], d_w_out[..., :side]), (d_w_qkv[..., q_cols:], d_w_out[..., side:]), take
+    )
+    (q_sum, out_left), (kv_sum, out_right) = ring.finish()
+    d_w_pieces = exchange(joined(q_sum, kv_sum), "fsdp")
+
+    qkv_sum = by_columns([d_w_pieces[f] for f in range(n_fsdp)])
+    attention_sum = ring_gather(
+        jnp.concatenate([qkv_sum, joined(out_left, out_right)], -1), halves, joined
+    ).reshape(d_shard, -1)
+    d_w_qkv, d_w_out = attention_sum[:, :-D], attention_sum[:, -D:]
+
+    d_gain_attn = vector[:d_shard]
+    d_gain_mlp = vector[d_shard : 2 * d_shard]
+    d_b_qkv = vector[2 * d_shard : 2 * d_shard + b_qkv.shape[0]]
 
     return (
         block_output,
         d_tokens,
         d_gain_attn,
-        total(d_w_qkv),
+        d_w_qkv,
         d_b_qkv,
-        total(d_w_out),
+        d_w_out,
         d_gain_mlp,
-        total(d_w_gate_up),
-        total(d_w_down),
+        d_w_gate_up,
+        d_w_down,
     )
 
 

time: 1010 us -> 748 us (0.74)
  waiting for transfers between devices: 600 us -> 149 us
  Pallas kernels: 29.2 us -> 164 us
  starting transfers between devices: 24.6 us -> 113 us
  blocking collectives: 75.7 us -> 6.27 us
  other arithmetic: 53.9 us -> 91.3 us
  local copies, waits for them, and re-layouts: 141 us -> 130 us
    psum x1 -> x0, waiting for transfers between devices: 355 us -> none  [total(): return lax.psum(partial, 'ctx').astype(F32)]
    pallas_call x0 -> x6, Pallas kernels: none -> 135 us  [the longest x3 67.7 us: group_sum(): pl.pallas_call(functools.partial(sum_kernel, mode, n, cuts), out_shape=ou...]
    ppermute x6 -> x80, starting transfers between devices: 5.33 us -> 92.4 us  [the longest x56 64.6 us: ring_send(): return jax.tree.map(lambda a: lax.ppermute(a, 'ctx', pairs), held)]
    all_gather x3 -> x0, waiting for transfers between devices: 64.5 us -> none  [the longest x1 45 us: body(): keys_values = lax.all_gather(own_kv, 'ctx', axis=0, tiled=True)]
    ppermute x6 -> x80, waiting for transfers between devices: 44.5 us -> 101 us  [the longest x56 41.9 us: ring_send(): return jax.tree.map(lambda a: lax.ppermute(a, 'ctx', pairs), held)]
    reduce_scatter x1 -> x0, waiting for transfers between devices: 55.6 us -> none  [body(): lax.psum_scatter(d_kv, 'ctx', scatter_dimension=0, tiled=True).astype(F32)]
    unnamed x74 -> x93, local copies, waits for them, and re-layouts: 55.7 us -> 9.84 us
    psum x1 -> x0, blocking collectives: 41.4 us -> none  [body(): lax.psum(jnp.concatenate([d_gain_one, d_gain_two, d_bias_full]), ('ctx',...]
  transfers between devices with their start and end apart: 21 -> 88, of which waited for: 10 -> 21; matrix products, arithmetic and copies ran while one was open for 19% -> 34% of each run, Pallas kernels for 0% -> 22%
where the time goes in v2:
time: 748 us; the launch traced here: 736 us
  Pallas kernels  164 us (22%)
  waiting for transfers between devices  149 us (20%)
  local copies, waits for them, and re-layouts  130 us (17%)
  starting transfers between devices  113 us (15%)
  other arithmetic  91.3 us (12%)
  matrix products  65.9 us (9%)
  between operations  16.4 us (2%)
    pallas_call x3, Pallas kernels, group_sum(): pl.pallas_call(functools.partial(sum_kernel, mode, n, cuts), out_shape=ou...  67.7 us
    ppermute x56, starting transfers between devices, ring_send(): return jax.tree.map(lambda a: lax.ppermute(a, 'ctx', pairs), held)  64.6 us
    convert_element_type x54, other arithmetic, ring_add(): (a.astype(F32) + b.astype(F32)).astype(BF16)  51.6 us
    all_to_all x5, waiting for transfers between devices, exchange(): return lax.all_to_all(pieces, axis, split_axis=0, concat_axis=0, tiled=True)  46.5 us
    dot_general x10, matrix products, dot(): lax.dot_general(left, right, (contract, ((), ())), preferred_element_type...  46.2 us
    ppermute x56, waiting for transfers between devices, ring_send(): return jax.tree.map(lambda a: lax.ppermute(a, 'ctx', pairs), held)  41.9 us
    pallas_call x1, Pallas kernels, return_grads(): pl.pallas_call(functools.partial(return_kernel, n), out_shape=jax.ShapeDt...  27.2 us
    ppermute x9, waiting for transfers between devices, ring_gather(): right = lax.ppermute(right, 'ctx', ring_pairs(n, 1))  23.5 us
  transfers between devices with their start and end apart: 88, of which 21 were waited for; matrix products, arithmetic and copies ran while one was open for 34% of the time, Pallas kernels for 22%

profile of v2, /device:TPU:0, one launch (start us, length us, event | category | flops | bytes accessed | tf_op | source)
XLA Modules:
  0.0 736.2 jit_solution(12612047431180557363)
XLA Ops:
  8.9 6.3 all-gather.3
  19.4 4.4 all-to-all-start
  23.9 18.0 %copy.248 = bf16[384,2,4480]{0,2,1:T(8,128)(2,1)} copy(bf16[384,2,4480]{2,1,0:T(2,128)(2,1)} %param.17) | data formatting | bytes 13762560 | tf_op jit(solution)/shard_map/optimization_barrier | solution.py:670
  41.9 6.6 fusion.72
  48.5 3.1 all-to-all-done
  51.6 4.9 all-to-all-start.1
  62.0 43.0 %all-to-all-done.1 = bf16[4,384,1120]{1,2,0:T(8,128)(2,1)} async-done(((bf16[4,384,1120]{1,2,0:T(8,128)(2,1)}), bf16[4,384,1120]{1,2,0:T(8,128)(2,1)}, u32[]{:S(2)}, u32[]{:S(2)}) %all-to-all-start.1) | async-done | bytes 3440672 | tf_op jit(solution)/shard_map/all_to_all | solution.py:666
  105.0 4.7 all-to-all-start.2
  114.0 3.5 convolution_add_fusion.1
  119.6 2.5 reshape.638
  122.2 2.3 fusion.78
  133.3 23.0 %share_keys.1 = bf16[8,2,256,256]{3,2,1,0:T(8,128)(2,1)} custom-call(bf16[2,256,256]{2,1,0:T(8,128)(2,1)} %pad_maximum_fusion.14.own), custom_call_target="tpu_custom_call" | custom-call | bytes 60000000 | tf_op jit(solution)/shard_map/share_keys/pallas_call | solution.py:469
  156.4 13.4 %attend.1 = (bf16[2,256,384]{2,1,0:T(8,128)(2,1)}, f32[2,1,768]{2,1,0:T(1,128)}) custom-call(s32[16]{0:T(128)} %pad_add_fusion.table, s32[2]{0:T(128)} %get-tuple-element.132.ids, bf16[2,256,384]{2,1,0:T(8,128)(2,1)} %reshape.758.q_ref, bf16[4096,256]{1,0:T(8,128)(2,1)} %bitcast.474), custom_call_target="tpu_custom_call" | custom-call | flops 1610612736 | bytes 2097152 | tf_op jit(solution)/shard_map/attend/pallas_call | solution.py:169
  169.8 3.5 convolution_convert_fusion.6
  173.3 25.7 %group_sum_attention.1 = (f32[2,64,1536]{2,1,0:T(8,128)}, bf16[2,4,64,1536]{3,2,1,0:T(8,128)(2,1)}) custom-call(bf16[2,4,64,1536]{3,2,1,0:T(8,128)(2,1)} %bitcast.464, bf16[2,64,1536]{2,1,0:T(8,128)(2,1)} %bitcast.466, f32[1,1536]{1,0:T(1,128)} %bitcast.501), custom_call_target="tpu_custom_call" | custom-call | flops 1966080 | bytes 60000000 | tf_op jit(solution)/shard_map/group_sum_attention/pallas_call | solution.py:371
  199.0 5.6 copy.254
  204.7 5.6 copy.255
  210.3 6.0 fusion.81
  216.3 3.4 fusion.82
  219.7 6.8 multiply_convert_fusion
  226.4 3.4 convolution_convert_fusion.5
  231.8 3.7 convolution_convert_fusion.1
  235.6 12.6 %fusion.83 = f32[512,1536]{1,0:T(8,128)} fusion(bf16[512,1120]{0,1:T(8,128)(2,1)S(1)} %get-tuple-element.136, bf16[1536,1120]{1,0:T(8,128)(2,1)S(1)} %bitcast.471), kind=kOutput, calls=%fused_computation.284 | convolution fusion | flops 1761607680 | bytes 7733248 | tf_op jit(solution)/shard_map/dot_general | solution.py:55
  248.2 5.7 copy.256
  259.9 3.7 convolution_convert_fusion
  263.7 5.6 copy.257
  273.6 6.8 fusion.3
  280.3 25.9 %group_sum_mlp.1 = (f32[2,64,1536]{2,1,0:T(8,128)}, bf16[2,4,64,1536]{3,2,1,0:T(8,128)(2,1)}, f32[1,1536]{1,0:T(1,128)}) custom-call(bf16[2,4,64,1536]{3,2,1,0:T(8,128)(2,1)} %bitcast.487, f32[2,64,1536]{2,1,0:T(8,128)} %get-tuple-element.76.refs_1_, bf16[2,64,1536]{2,1,0:T(8,128)(2,1)} %bitcast.488, f32[1,1536]{1,0:T(1,128)} %bitcast.502), custom_call_target="tpu_custom_call" | custom-call | flops 1966080 | bytes 60000000 | tf_op jit(solution)/shard_map/group_sum_mlp/pallas_call | solution.py:371
  319.5 16.1 %attend_back.1 = (f32[2,256,384]{2,1,0:T(8,128)}, bf16[4096,256]{1,0:T(8,128)(2,1)}) custom-call(s32[16]{0:T(128)} %pad_add_fusion.table, s32[2]{0:T(128)} %get-tuple-element.132.ids, bf16[2,256,384]{2,1,0:T(8,128)(2,1)} %reshape.758.q_ref, bf16[4096,256]{1,0:T(8,128)(2,1)} %bitcast.475, bf16[2,256,384]{2,1,0:T(8,128)(2,1)} %get-tuple-element.75.o_ref, ...), custom_call_target="tpu_custom_call" | custom-call | flops 4026531840 | bytes 4194304 | tf_op jit(solution)/shard_map/attend_back/pallas_call | solution.py:190
  348.3 27.2 %return_grads.1 = f32[2,256,256]{2,1,0:T(8,128)} custom-call(bf16[8,2,256,256]{3,2,1,0:T(8,128)(2,1)} %bitcast.472), custom_call_target="tpu_custom_call" | custom-call | bytes 80000000 | tf_op jit(solution)/shard_map/return_grads/pallas_call | solution.py:521
  377.6 5.6 collective-permute-start.12
  391.4 2.3 copy.266
  396.0 2.4 copy.315
  398.3 2.4 copy.314
  405.6 4.1 convolution_convert_fusion.4
  420.1 2.9 convolution_convert_fusion.3
  423.0 16.1 %group_sum_input.1 = (f32[2,64,1536]{2,1,0:T(8,128)}, f32[1,1536]{1,0:T(1,128)}) custom-call(bf16[2,4,64,1536]{3,2,1,0:T(8,128)(2,1)} %bitcast.486, bf16[2,64,1536]{2,1,0:T(8,128)(2,1)} %bitcast.467, f32[2,64,1536]{2,1,0:T(8,128)} %get-tuple-element.108.refs_2_, f32[1,1536]{1,0:T(1,128)} %bitcast.505), custom_call_target="tpu_custom_call" | custom-call | flops 1966080 | bytes 60000000 | tf_op jit(solution)/shard_map/group_sum_input/pallas_call | solution.py:371
  449.5 16.6 %vector_sum.1 = f32[16,128]{1,0:T(8,128)} custom-call(f32[4,16,128]{2,1,0:T(8,128)} %select_maximum_fusion.parts), custom_call_target="tpu_custom_call" | custom-call | bytes 30000000 | tf_op jit(solution)/shard_map/vector_sum/pallas_call | solution.py:574
  477.4 7.6 %collective-permute-done.71 = bf16[144,768]{1,0:T(8,128)(2,1)S(1)} collective-permute-done((bf16[144,768]{1,0:T(8,128)(2,1)S(1)}, bf16[144,768]{1,0:T(8,128)(2,1)S(1)}, u32[]{:S(2)}, u32[]{:S(2)}) %collective-permute-start.71) | collective-permute-done | bytes 221216 | tf_op jit(solution)/shard_map/ppermute | solution.py:608
  489.2 3.8 broadcast_in_dim.176
  502.5 3.5 all-to-all-start.4
  508.4 2.3 collective-permute-done.47
  514.4 2.1 fusion.41
  529.1 2.1 convert_dynamic-update-slice_fusion.5
  538.5 6.6 collective-permute-done.44
  546.5 3.0 collective-permute-done.51
  560.3 3.6 collective-permute-done.38
  567.8 3.4 reshape.757
  573.2 5.2 broadcast_in_dim.163
  582.9 3.5 collective-permute-done.30
  592.2 6.6 collective-permute-done.31
  602.8 4.9 collective-permute-done.32
  610.2 3.4 all-to-all-start.3
  623.4 2.1 collective-permute-start.54
  628.0 12.2 %collective-permute-done.79 = bf16[144,768]{1,0:T(8,128)(2,1)} collective-permute-done((bf16[144,768]{1,0:T(8,128)(2,1)}, bf16[144,768]{1,0:T(8,128)(2,1)}, u32[]{:S(2)}, u32[]{:S(2)}) %collective-permute-start.79) | collective-permute-done | bytes 221216 | tf_op jit(solution)/shard_map/ppermute | solution.py:661
  643.3 6.4 slice.331
  649.8 2.1 copy_dynamic-update-slice_fusion.6
  652.0 2.1 copy_dynamic-update-slice_fusion.5
  658.3 23.5 %collective-permute-done.56 = bf16[48,3584]{1,0:T(8,128)(2,1)S(1)} collective-permute-done((bf16[48,3584]{1,0:T(8,128)(2,1)S(1)}, bf16[48,3584]{1,0:T(8,128)(2,1)S(1)}, u32[]{:S(2)}, u32[]{:S(2)}) %collective-permute-start.56) | collective-permute-done | bytes 344096 | tf_op jit(solution)/shard_map/ppermute | solution.py:656
  683.9 8.0 %collective-permute-done.59 = bf16[48,3584]{1,0:T(8,128)(2,1)S(1)} collective-permute-done((bf16[48,3584]{1,0:T(8,128)(2,1)S(1)}, bf16[48,3584]{1,0:T(8,128)(2,1)S(1)}, u32[]{:S(2)}, u32[]{:S(2)}) %collective-permute-start.59) | collective-permute-done | bytes 344096 | tf_op jit(solution)/shard_map/ppermute | solution.py:658
  704.3 12.9 %collective-permute-done.67 = bf16[48,2,4480]{2,0,1:T(8,128)(2,1)S(1)} collective-permute-done((bf16[48,2,4480]{2,0,1:T(8,128)(2,1)S(1)}, bf16[48,2,4480]{2,0,1:T(8,128)(2,1)S(1)}, u32[]{:S(2)}, u32[]{:S(2)}) %collective-permute-start.67) | collective-permute-done | bytes 860192 | tf_op jit(solution)/shard_map/ppermute | solution.py:658
  719.7 2.1 copy_dynamic-update-slice_fusion.2
  721.9 2.1 copy_dynamic-update-slice_fusion.1
  726.5 2.1 copy_dynamic-update-slice_fusion
  (426 shorter events, 227.4 us)
Async XLA Ops:
  7.2 44.4 %all-gather.7.cloned.1.call-start = ((), (), s32[]{:S(2)}) async-start(), calls=%async_computation.7 | async-start | bytes 1966080 | tf_op jit(solution)/shard_map/all_gather | solution.py:707
  19.4 32.2 %all-to-all-start = ((bf16[4,384,640]{2,1,0:T(8,128)(2,1)}), bf16[4,384,640]{2,1,0:T(8,128)(2,1)}, u32[]{:S(2)}, u32[]{:S(2)}) async-start(bf16[4,384,640]{2,1,0:T(8,128)(2,1)} %pad_maximum_fusion), calls=%async_computation | async-start | bytes 3932160 | tf_op jit(solution)/shard_map/all_to_all | solution.py:666
  51.6 53.4 %all-to-all-start.1 = ((bf16[4,384,1120]{1,2,0:T(8,128)(2,1)}), bf16[4,384,1120]{1,2,0:T(8,128)(2,1)}, u32[]{:S(2)}, u32[]{:S(2)}) async-start(bf16[4,384,1120]{1,2,0:T(8,128)(2,1)} %bitcast.460), calls=%async_computation.1 | async-start | bytes 6881280 | tf_op jit(solution)/shard_map/all_to_all | solution.py:666
  56.5 163.2 %all-gather.9.cloned.1.call-start = ((), (), s32[]{:S(2)}) async-start(), calls=%async_computation.8 | async-start | bytes 1966080 | tf_op jit(solution)/shard_map/all_gather | solution.py:741
  105.0 99.6 %all-to-all-start.2 = ((bf16[4,384,1120]{1,2,0:T(8,128)(2,1)}), bf16[4,384,1120]{1,2,0:T(8,128)(2,1)}, u32[]{:S(2)}, u32[]{:S(2)}) async-start(bf16[4,384,1120]{1,2,0:T(8,128)(2,1)} %bitcast.459), calls=%async_computation.2 | async-start | bytes 6881280 | tf_op jit(solution)/shard_map/all_to_all | solution.py:666
  109.8 404.6 %reduce-scatter.2.cloned.1.call-start = ((), (), s32[]{:S(2)}) async-start(), calls=%async_computation.6 | async-start | bytes 1966080 | tf_op jit(solution)/shard_map/reduce_scatter | solution.py:758
  255.8 50.5 %collective-permute-start = (bf16[4,48,1120]{2,1,0:T(8,128)(2,1)}, bf16[4,48,1120]{2,1,0:T(8,128)(2,1)}, u32[]{:S(2)}, u32[]{:S(2)}) collective-permute-start(bf16[4,48,1120]{2,1,0:T(8,128)(2,1)} %dynamic-slice_bitcast_fusion.1), channel_id=1, source_target_pairs={{0,8},{8,16},{16,24},{24,28},{28,20},{20,12},{12,4},{4,0},{1,9},{9... | collective-permute-start | bytes 1290248 | tf_op jit(solution)/shard_map/ppermute | solution.py:608
  259.1 47.2 %collective-permute-start.1 = (bf16[144,768]{1,0:T(8,128)(2,1)S(1)}, bf16[144,768]{1,0:T(8,128)(2,1)S(1)}, u32[]{:S(2)}, u32[]{:S(2)}) collective-permute-start(bf16[144,768]{1,0:T(8,128)(2,1)S(1)} %dynamic-slice_bitcast_fusion.3), channel_id=1, source_target_pairs={{0,8},{8,16},{16,24},{24,28},{28,20},{20,12},{12,4},{4,0},{1,9},{9... | collective-permute-start | bytes 663560 | tf_op jit(solution)/shard_map/ppermute | solution.py:608
  270.3 36.0 %collective-permute-start.2 = (bf16[4,48,1120]{2,1,0:T(8,128)(2,1)S(1)}, bf16[4,48,1120]{2,1,0:T(8,128)(2,1)S(1)}, u32[]{:S(2)}, u32[]{:S(2)}) collective-permute-start(bf16[4,48,1120]{2,1,0:T(8,128)(2,1)S(1)} %dynamic-slice_bitcast_fusion), channel_id=1, source_target_pairs={{0,4},{8,0},{16,8},{24,16},{28,24},{20,28},{12,20},{4,12},{1,5},{9... | collective-permute-start | bytes 1290248 | tf_op jit(solution)/shard_map/ppermute | solution.py:608
  272.6 33.7 %collective-permute-start.3 = (bf16[144,768]{1,0:T(8,128)(2,1)S(1)}, bf16[144,768]{1,0:T(8,128)(2,1)S(1)}, u32[]{:S(2)}, u32[]{:S(2)}) collective-permute-start(bf16[144,768]{1,0:T(8,128)(2,1)S(1)} %dynamic-slice_bitcast_fusion.2), channel_id=1, source_target_pairs={{0,4},{8,0},{16,8},{24,16},{28,24},{20,28},{12,20},{4,12},{1,5},{9... | collective-permute-start | bytes 663560 | tf_op jit(solution)/shard_map/ppermute | solution.py:608
  308.4 27.2 %collective-permute-start.4 = (bf16[4,48,1120]{2,1,0:T(8,128)(2,1)S(1)}, bf16[4,48,1120]{2,1,0:T(8,128)(2,1)S(1)}, u32[]{:S(2)}, u32[]{:S(2)}) collective-permute-start(bf16[4,48,1120]{2,1,0:T(8,128)(2,1)S(1)} %fusion.19), channel_id=1, source_target_pairs={{0,8},{8,16},{16,24},{24,28},{28,20},{20,12},{12,4},{4,0},{1,9},{9... | collective-permute-start | bytes 1290248 | tf_op jit(solution)/shard_map/ppermute | solution.py:608
  311.2 24.4 %collective-permute-start.5 = (bf16[144,768]{1,0:T(8,128)(2,1)}, bf16[144,768]{1,0:T(8,128)(2,1)}, u32[]{:S(2)}, u32[]{:S(2)}) collective-permute-start(bf16[144,768]{1,0:T(8,128)(2,1)} %fusion.39), channel_id=1, source_target_pairs={{0,8},{8,16},{16,24},{24,28},{28,20},{20,12},{12,4},{4,0},{1,9},{9... | collective-permute-start | bytes 663560 | tf_op jit(solution)/shard_map/ppermute | solution.py:608
  313.9 21.7 %collective-permute-start.6 = (bf16[4,48,1120]{2,1,0:T(8,128)(2,1)}, bf16[4,48,1120]{2,1,0:T(8,128)(2,1)S(1)}, u32[]{:S(2)}, u32[]{:S(2)}) collective-permute-start(bf16[4,48,1120]{2,1,0:T(8,128)(2,1)} %fusion.18), channel_id=1, source_target_pairs={{0,4},{8,0},{16,8},{24,16},{28,24},{20,28},{12,20},{4,12},{1,5},{9... | collective-permute-start | bytes 1290248 | tf_op jit(solution)/shard_map/ppermute | solution.py:608
  316.7 18.8 %collective-permute-start.7 = (bf16[144,768]{1,0:T(8,128)(2,1)}, bf16[144,768]{1,0:T(8,128)(2,1)}, u32[]{:S(2)}, u32[]{:S(2)}) collective-permute-start(bf16[144,768]{1,0:T(8,128)(2,1)} %fusion.38), channel_id=1, source_target_pairs={{0,4},{8,0},{16,8},{24,16},{28,24},{20,28},{12,20},{4,12},{1,5},{9... | collective-permute-start | bytes 663560 | tf_op jit(solution)/shard_map/ppermute | solution.py:608
  336.9 38.7 %collective-permute-start.8 = (bf16[4,48,1120]{2,1,0:T(8,128)(2,1)S(1)}, bf16[4,48,1120]{2,1,0:T(8,128)(2,1)S(1)}, u32[]{:S(2)}, u32[]{:S(2)}) collective-permute-start(bf16[4,48,1120]{2,1,0:T(8,128)(2,1)S(1)} %fusion.17), channel_id=1, source_target_pairs={{0,8},{8,16},{16,24},{24,28},{28,20},{20,12},{12,4},{4,0},{1,9},{9... | collective-permute-start | bytes 1290248 | tf_op jit(solution)/shard_map/ppermute | solution.py:608
  339.7 35.9 %collective-permute-start.9 = (bf16[144,768]{1,0:T(8,128)(2,1)}, bf16[144,768]{1,0:T(8,128)(2,1)S(1)}, u32[]{:S(2)}, u32[]{:S(2)}) collective-permute-start(bf16[144,768]{1,0:T(8,128)(2,1)} %fusion.37), channel_id=1, source_target_pairs={{0,8},{8,16},{16,24},{24,28},{28,20},{20,12},{12,4},{4,0},{1,9},{9... | collective-permute-start | bytes 663560 | tf_op jit(solution)/shard_map/ppermute | solution.py:608
  342.6 33.0 %collective-permute-start.10 = (bf16[4,48,1120]{2,1,0:T(8,128)(2,1)}, bf16[4,48,1120]{2,1,0:T(8,128)(2,1)S(1)}, u32[]{:S(2)}, u32[]{:S(2)}) collective-permute-start(bf16[4,48,1120]{2,1,0:T(8,128)(2,1)} %fusion.16), channel_id=1, source_target_pairs={{0,4},{8,0},{16,8},{24,16},{28,24},{20,28},{12,20},{4,12},{1,5},{9... | collective-permute-start | bytes 1290248 | tf_op jit(solution)/shard_map/ppermute | solution.py:608
  345.6 30.0 %collective-permute-start.11 = (bf16[144,768]{1,0:T(8,128)(2,1)}, bf16[144,768]{1,0:T(8,128)(2,1)}, u32[]{:S(2)}, u32[]{:S(2)}) collective-permute-start(bf16[144,768]{1,0:T(8,128)(2,1)} %fusion.36), channel_id=1, source_target_pairs={{0,4},{8,0},{16,8},{24,16},{28,24},{20,28},{12,20},{4,12},{1,5},{9... | collective-permute-start | bytes 663560 | tf_op jit(solution)/shard_map/ppermute | solution.py:608
  377.6 32.2 %collective-permute-start.12 = (bf16[4,48,1120]{2,1,0:T(8,128)(2,1)}, bf16[4,48,1120]{2,1,0:T(8,128)(2,1)}, u32[]{:S(2)}, u32[]{:S(2)}) collective-permute-start(bf16[4,48,1120]{2,1,0:T(8,128)(2,1)} %fusion.15), channel_id=1, source_target_pairs={{0,8},{8,16},{16,24},{24,28},{28,20},{20,12},{12,4},{4,0},{1,9},{9... | collective-permute-start | bytes 1290248 | tf_op jit(solution)/shard_map/ppermute | solution.py:608
  383.9 25.9 %collective-permute-start.13 = (bf16[144,768]{1,0:T(8,128)(2,1)}, bf16[144,768]{1,0:T(8,128)(2,1)}, u32[]{:S(2)}, u32[]{:S(2)}) collective-permute-start(bf16[144,768]{1,0:T(8,128)(2,1)} %fusion.35), channel_id=1, source_target_pairs={{0,8},{8,16},{16,24},{24,28},{28,20},{20,12},{12,4},{4,0},{1,9},{9... | collective-permute-start | bytes 663560 | tf_op jit(solution)/shard_map/ppermute | solution.py:608
  386.8 23.0 %collective-permute-start.14 = (bf16[4,48,1120]{2,1,0:T(8,128)(2,1)}, bf16[4,48,1120]{2,1,0:T(8,128)(2,1)}, u32[]{:S(2)}, u32[]{:S(2)}) collective-permute-start(bf16[4,48,1120]{2,1,0:T(8,128)(2,1)} %fusion.14), channel_id=1, source_target_pairs={{0,4},{8,0},{16,8},{24,16},{28,24},{20,28},{12,20},{4,12},{1,5},{9... | collective-permute-start | bytes 1290248 | tf_op jit(solution)/shard_map/ppermute | solution.py:608
  389.7 20.1 %collective-permute-start.15 = (bf16[144,768]{1,0:T(8,128)(2,1)}, bf16[144,768]{1,0:T(8,128)(2,1)}, u32[]{:S(2)}, u32[]{:S(2)}) collective-permute-start(bf16[144,768]{1,0:T(8,128)(2,1)} %fusion.34), channel_id=1, source_target_pairs={{0,4},{8,0},{16,8},{24,16},{28,24},{20,28},{12,20},{4,12},{1,5},{9... | collective-permute-start | bytes 663560 | tf_op jit(solution)/shard_map/ppermute | solution.py:608
  411.2 28.0 %collective-permute-start.16 = (bf16[4,48,1120]{2,1,0:T(8,128)(2,1)S(1)}, bf16[4,48,1120]{2,1,0:T(8,128)(2,1)S(1)}, u32[]{:S(2)}, u32[]{:S(2)}) collective-permute-start(bf16[4,48,1120]{2,1,0:T(8,128)(2,1)S(1)} %fusion.13), channel_id=1, source_target_pairs={{0,8},{8,16},{16,24},{24,28},{28,20},{20,12},{12,4},{4,0},{1,9},{9... | collective-permute-start | bytes 1290248 | tf_op jit(solution)/shard_map/ppermute | solution.py:608
  414.1 25.1 %collective-permute-start.17 = (bf16[144,768]{1,0:T(8,128)(2,1)}, bf16[144,768]{1,0:T(8,128)(2,1)S(1)}, u32[]{:S(2)}, u32[]{:S(2)}) collective-permute-start(bf16[144,768]{1,0:T(8,128)(2,1)} %fusion.33), channel_id=1, source_target_pairs={{0,8},{8,16},{16,24},{24,28},{28,20},{20,12},{12,4},{4,0},{1,9},{9... | collective-permute-start | bytes 663560 | tf_op jit(solution)/shard_map/ppermute | solution.py:608
  417.0 22.2 %collective-permute-start.18 = (bf16[4,48,1120]{2,1,0:T(8,128)(2,1)S(1)}, bf16[4,48,1120]{2,1,0:T(8,128)(2,1)S(1)}, u32[]{:S(2)}, u32[]{:S(2)}) collective-permute-start(bf16[4,48,1120]{2,1,0:T(8,128)(2,1)S(1)} %fusion.12), channel_id=1, source_target_pairs={{0,4},{8,0},{16,8},{24,16},{28,24},{20,28},{12,20},{4,12},{1,5},{9... | collective-permute-start | bytes 1290248 | tf_op jit(solution)/shard_map/ppermute | solution.py:608
  419.2 20.0 %collective-permute-start.19 = (bf16[144,768]{1,0:T(8,128)(2,1)}, bf16[144,768]{1,0:T(8,128)(2,1)}, u32[]{:S(2)}, u32[]{:S(2)}) collective-permute-start(bf16[144,768]{1,0:T(8,128)(2,1)} %fusion.32), channel_id=1, source_target_pairs={{0,4},{8,0},{16,8},{24,16},{28,24},{20,28},{12,20},{4,12},{1,5},{9... | collective-permute-start | bytes 663560 | tf_op jit(solution)/shard_map/ppermute | solution.py:608
  441.1 25.0 %collective-permute-start.20 = (bf16[4,48,1120]{2,1,0:T(8,128)(2,1)}, bf16[4,48,1120]{2,1,0:T(8,128)(2,1)S(1)}, u32[]{:S(2)}, u32[]{:S(2)}) collective-permute-start(bf16[4,48,1120]{2,1,0:T(8,128)(2,1)} %fusion.11), channel_id=1, source_target_pairs={{0,8},{8,16},{16,24},{24,28},{28,20},{20,12},{12,4},{4,0},{1,9},{9... | collective-permute-start | bytes 1290248 | tf_op jit(solution)/shard_map/ppermute | solution.py:608
  443.0 23.1 %collective-permute-start.21 = (bf16[144,768]{1,0:T(8,128)(2,1)}, bf16[144,768]{1,0:T(8,128)(2,1)}, u32[]{:S(2)}, u32[]{:S(2)}) collective-permute-start(bf16[144,768]{1,0:T(8,128)(2,1)} %fusion.31), channel_id=1, source_target_pairs={{0,8},{8,16},{16,24},{24,28},{28,20},{20,12},{12,4},{4,0},{1,9},{9... | collective-permute-start | bytes 663560 | tf_op jit(solution)/shard_map/ppermute | solution.py:608
  445.8 20.4 %collective-permute-start.22 = (bf16[4,48,1120]{2,1,0:T(8,128)(2,1)S(1)}, bf16[4,48,1120]{2,1,0:T(8,128)(2,1)S(1)}, u32[]{:S(2)}, u32[]{:S(2)}) collective-permute-start(bf16[4,48,1120]{2,1,0:T(8,128)(2,1)S(1)} %fusion.10), channel_id=1, source_target_pairs={{0,4},{8,0},{16,8},{24,16},{28,24},{20,28},{12,20},{4,12},{1,5},{9... | collective-permute-start | bytes 1290248 | tf_op jit(solution)/shard_map/ppermute | solution.py:608
  448.0 18.1 %collective-permute-start.23 = (bf16[144,768]{1,0:T(8,128)(2,1)}, bf16[144,768]{1,0:T(8,128)(2,1)}, u32[]{:S(2)}, u32[]{:S(2)}) collective-permute-start(bf16[144,768]{1,0:T(8,128)(2,1)} %fusion.30), channel_id=1, source_target_pairs={{0,4},{8,0},{16,8},{24,16},{28,24},{20,28},{12,20},{4,12},{1,5},{9... | collective-permute-start | bytes 663560 | tf_op jit(solution)/shard_map/ppermute | solution.py:608
  468.6 25.5 %collective-permute-start.24 = (bf16[4,48,1120]{2,1,0:T(8,128)(2,1)S(1)}, bf16[4,48,1120]{2,1,0:T(8,128)(2,1)S(1)}, u32[]{:S(2)}, u32[]{:S(2)}) collective-permute-start(bf16[4,48,1120]{2,1,0:T(8,128)(2,1)S(1)} %fusion.9), channel_id=1, source_target_pairs={{0,8},{8,16},{16,24},{24,28},{28,20},{20,12},{12,4},{4,0},{1,9},{9... | collective-permute-start | bytes 1290248 | tf_op jit(solution)/shard_map/ppermute | solution.py:608
  470.5 24.7 %collective-permute-start.25 = (bf16[4,48,1120]{2,1,0:T(8,128)(2,1)S(1)}, bf16[4,48,1120]{2,1,0:T(8,128)(2,1)S(1)}, u32[]{:S(2)}, u32[]{:S(2)}) collective-permute-start(bf16[4,48,1120]{2,1,0:T(8,128)(2,1)S(1)} %fusion.7), channel_id=1, source_target_pairs={{0,4},{8,0},{16,8},{24,16},{28,24},{20,28},{12,20},{4,12},{1,5},{9... | collective-permute-start | bytes 1290248 | tf_op jit(solution)/shard_map/ppermute | solution.py:608
  473.0 12.0 %collective-permute-start.71 = (bf16[144,768]{1,0:T(8,128)(2,1)S(1)}, bf16[144,768]{1,0:T(8,128)(2,1)S(1)}, u32[]{:S(2)}, u32[]{:S(2)}) collective-permute-start(bf16[144,768]{1,0:T(8,128)(2,1)S(1)} %fusion.27), channel_id=1, source_target_pairs={{0,4},{8,0},{16,8},{24,16},{28,24},{20,28},{12,20},{4,12},{1,5},{9... | collective-permute-start | bytes 663560 | tf_op jit(solution)/shard_map/ppermute | solution.py:608
  475.6 10.4 %collective-permute-start.70 = (bf16[144,768]{1,0:T(8,128)(2,1)S(1)}, bf16[144,768]{1,0:T(8,128)(2,1)S(1)}, u32[]{:S(2)}, u32[]{:S(2)}) collective-permute-start(bf16[144,768]{1,0:T(8,128)(2,1)S(1)} %fusion.29), channel_id=1, source_target_pairs={{0,8},{8,16},{16,24},{24,28},{28,20},{20,12},{12,4},{4,0},{1,9},{9... | collective-permute-start | bytes 663560 | tf_op jit(solution)/shard_map/ppermute | solution.py:608
  486.8 41.1 %collective-permute-start.72 = (bf16[144,1536]{1,0:T(8,128)(2,1)}, bf16[144,1536]{1,0:T(8,128)(2,1)}, u32[]{:S(2)}, u32[]{:S(2)}) collective-permute-start(bf16[144,1536]{1,0:T(8,128)(2,1)} %pad_maximum_fusion.13), channel_id=1, source_target_pairs={{0,8},{8,16},{16,24},{24,28},{28,20},{20,12},{12,4},{4,0},{1,9},{9... | collective-permute-start | bytes 1327112 | tf_op jit(solution)/shard_map/ppermute | solution.py:656
  488.1 43.1 %collective-permute-start.73 = (bf16[144,1536]{1,0:T(8,128)(2,1)}, bf16[144,1536]{1,0:T(8,128)(2,1)}, u32[]{:S(2)}, u32[]{:S(2)}) collective-permute-start(bf16[144,1536]{1,0:T(8,128)(2,1)} %pad_maximum_fusion.13), channel_id=1, source_target_pairs={{0,4},{8,0},{16,8},{24,16},{28,24},{20,28},{12,20},{4,12},{1,5},{9... | collective-permute-start | bytes 1327112 | tf_op jit(solution)/shard_map/ppermute | solution.py:658
  496.6 15.3 %collective-permute-start.33 = (bf16[4,48,256]{2,1,0:T(8,128)(2,1)S(1)}, bf16[4,48,256]{2,1,0:T(8,128)(2,1)}, u32[]{:S(2)}, u32[]{:S(2)}) collective-permute-start(bf16[4,48,256]{2,1,0:T(8,128)(2,1)S(1)} %dynamic-slice_bitcast_fusion.5), channel_id=1, source_target_pairs={{0,4},{8,0},{16,8},{24,16},{28,24},{20,28},{12,20},{4,12},{1,5},{9... | collective-permute-start | bytes 294920 | tf_op jit(solution)/shard_map/ppermute | solution.py:608
  498.5 18.0 %collective-permute-start.26 = (bf16[4,48,384]{2,1,0:T(8,128)(2,1)}, bf16[4,48,384]{2,1,0:T(8,128)(2,1)}, u32[]{:S(2)}, u32[]{:S(2)}) collective-permute-start(bf16[4,48,384]{2,1,0:T(8,128)(2,1)} %dynamic-slice_bitcast_fusion.4), channel_id=1, source_target_pairs={{0,8},{8,16},{16,24},{24,28},{28,20},{20,12},{12,4},{4,0},{1,9},{9... | collective-permute-start | bytes 442376 | tf_op jit(solution)/shard_map/ppermute | solution.py:608
  502.5 64.0 %all-to-all-start.4 = ((bf16[4,2,48,1120]{3,2,1,0:T(8,128)(2,1)}), bf16[4,2,48,1120]{3,2,1,0:T(8,128)(2,1)S(1)}, u32[]{:S(2)}, u32[]{:S(2)}) async-start(bf16[4,2,48,1120]{3,2,1,0:T(8,128)(2,1)} %copy.290), calls=%async_computation.5 | async-start | bytes 1769472 | tf_op jit(solution)/shard_map/all_to_all | solution.py:666
  518.2 17.1 %collective-permute-start.27 = (bf16[4,48,384]{2,1,0:T(8,128)(2,1)S(1)}, bf16[4,48,384]{2,1,0:T(8,128)(2,1)S(1)}, u32[]{:S(2)}, u32[]{:S(2)}) collective-permute-start(bf16[4,48,384]{2,1,0:T(8,128)(2,1)S(1)} %fusion.48), channel_id=1, source_target_pairs={{0,8},{8,16},{16,24},{24,28},{28,20},{20,12},{12,4},{4,0},{1,9},{9... | collective-permute-start | bytes 442376 | tf_op jit(solution)/shard_map/ppermute | solution.py:608
  531.2 48.5 %collective-permute-start.74 = (bf16[144,1536]{1,0:T(8,128)(2,1)}, bf16[144,1536]{1,0:T(8,128)(2,1)}, u32[]{:S(2)}, u32[]{:S(2)}) collective-permute-start(bf16[144,1536]{1,0:T(8,128)(2,1)} %collective-permute-done.72), channel_id=1, source_target_pairs={{0,8},{8,16},{16,24},{24,28},{28,20},{20,12},{12,4},{4,0},{1,9},{9... | collective-permute-start | bytes 1327112 | tf_op jit(solution)/shard_map/ppermute | solution.py:656
  534.1 54.4 %collective-permute-start.75 = (bf16[144,1536]{1,0:T(8,128)(2,1)}, bf16[144,1536]{1,0:T(8,128)(2,1)}, u32[]{:S(2)}, u32[]{:S(2)}) collective-permute-start(bf16[144,1536]{1,0:T(8,128)(2,1)} %collective-permute-done.73), channel_id=1, source_target_pairs={{0,4},{8,0},{16,8},{24,16},{28,24},{20,28},{12,20},{4,12},{1,5},{9... | collective-permute-start | bytes 1327112 | tf_op jit(solution)/shard_map/ppermute | solution.py:658
  535.3 15.7 %collective-permute-start.36 = (bf16[4,48,256]{2,1,0:T(8,128)(2,1)S(1)}, bf16[4,48,256]{2,1,0:T(8,128)(2,1)S(1)}, u32[]{:S(2)}, u32[]{:S(2)}) collective-permute-start(bf16[4,48,256]{2,1,0:T(8,128)(2,1)S(1)} %fusion.53), channel_id=1, source_target_pairs={{0,4},{8,0},{16,8},{24,16},{28,24},{20,28},{12,20},{4,12},{1,5},{9... | collective-permute-start | bytes 294920 | tf_op jit(solution)/shard_map/ppermute | solution.py:608
  536.3 15.4 %collective-permute-start.28 = (bf16[4,48,384]{2,1,0:T(8,128)(2,1)S(1)}, bf16[4,48,384]{2,1,0:T(8,128)(2,1)S(1)}, u32[]{:S(2)}, u32[]{:S(2)}) collective-permute-start(bf16[4,48,384]{2,1,0:T(8,128)(2,1)S(1)} %fusion.47), channel_id=1, source_target_pairs={{0,8},{8,16},{16,24},{24,28},{28,20},{20,12},{12,4},{4,0},{1,9},{9... | collective-permute-start | bytes 442376 | tf_op jit(solution)/shard_map/ppermute | solution.py:608
  554.0 10.9 %collective-permute-start.29 = (bf16[4,48,384]{2,1,0:T(8,128)(2,1)S(1)}, bf16[4,48,384]{2,1,0:T(8,128)(2,1)S(1)}, u32[]{:S(2)}, u32[]{:S(2)}) collective-permute-start(bf16[4,48,384]{2,1,0:T(8,128)(2,1)S(1)} %fusion.46), channel_id=1, source_target_pairs={{0,8},{8,16},{16,24},{24,28},{28,20},{20,12},{12,4},{4,0},{1,9},{9... | collective-permute-start | bytes 442376 | tf_op jit(solution)/shard_map/ppermute | solution.py:608
  557.5 62.2 %collective-permute-start.46 = (bf16[48,768]{1,0:T(8,128)(2,1)}, bf16[48,768]{1,0:T(8,128)(2,1)S(1)}, u32[]{:S(2)}, u32[]{:S(2)}) collective-permute-start(bf16[48,768]{1,0:T(8,128)(2,1)} %fusion.64), channel_id=1, source_target_pairs={{0,8},{8,16},{16,24},{24,28},{28,20},{20,12},{12,4},{4,0},{1,9},{9... | collective-permute-start | bytes 221192 | tf_op jit(solution)/shard_map/ppermute | solution.py:608
  563.9 58.5 %collective-permute-start.53 = (bf16[48,768]{1,0:T(8,128)(2,1)}, bf16[48,768]{1,0:T(8,128)(2,1)}, u32[]{:S(2)}, u32[]{:S(2)}) collective-permute-start(bf16[48,768]{1,0:T(8,128)(2,1)} %fusion.57), channel_id=1, source_target_pairs={{0,4},{8,0},{16,8},{24,16},{28,24},{20,28},{12,20},{4,12},{1,5},{9... | collective-permute-start | bytes 221192 | tf_op jit(solution)/shard_map/ppermute | solution.py:608
  564.9 36.0 %collective-permute-start.39 = (bf16[4,48,256]{2,1,0:T(8,128)(2,1)}, bf16[4,48,256]{2,1,0:T(8,128)(2,1)}, u32[]{:S(2)}, u32[]{:S(2)}) collective-permute-start(bf16[4,48,256]{2,1,0:T(8,128)(2,1)} %fusion.50), channel_id=1, source_target_pairs={{0,4},{8,0},{16,8},{24,16},{28,24},{20,28},{12,20},{4,12},{1,5},{9... | collective-permute-start | bytes 294920 | tf_op jit(solution)/shard_map/ppermute | solution.py:608
  586.4 29.1 %collective-permute-start.76 = (bf16[144,1536]{1,0:T(8,128)(2,1)}, bf16[144,1536]{1,0:T(8,128)(2,1)S(1)}, u32[]{:S(2)}, u32[]{:S(2)}) collective-permute-start(bf16[144,1536]{1,0:T(8,128)(2,1)} %collective-permute-done.74), channel_id=1, source_target_pairs={{0,8},{8,16},{16,24},{24,28},{28,20},{20,12},{12,4},{4,0},{1,9},{9... | collective-permute-start | bytes 1327112 | tf_op jit(solution)/shard_map/ppermute | solution.py:656
  588.5 10.3 %collective-permute-start.31 = (bf16[4,48,384]{2,1,0:T(8,128)(2,1)S(1)}, bf16[4,48,384]{2,1,0:T(8,128)(2,1)S(1)}, u32[]{:S(2)}, u32[]{:S(2)}) collective-permute-start(bf16[4,48,384]{2,1,0:T(8,128)(2,1)S(1)} %fusion.44), channel_id=1, source_target_pairs={{0,8},{8,16},{16,24},{24,28},{28,20},{20,12},{12,4},{4,0},{1,9},{9... | collective-permute-start | bytes 442376 | tf_op jit(solution)/shard_map/ppermute | solution.py:608
  598.8 14.8 %collective-permute-start.77 = (bf16[144,1536]{1,0:T(8,128)(2,1)}, bf16[144,1536]{1,0:T(8,128)(2,1)S(1)}, u32[]{:S(2)}, u32[]{:S(2)}) collective-permute-start(bf16[144,1536]{1,0:T(8,128)(2,1)} %collective-permute-done.75), channel_id=1, source_target_pairs={{0,4},{8,0},{16,8},{24,16},{28,24},{20,28},{12,20},{4,12},{1,5},{9... | collective-permute-start | bytes 1327112 | tf_op jit(solution)/shard_map/ppermute | solution.py:658
  607.7 42.0 %collective-permute-start.62 = (bf16[48,2,4480]{2,0,1:T(8,128)(2,1)}, bf16[48,2,4480]{2,0,1:T(8,128)(2,1)S(1)}, u32[]{:S(2)}, u32[]{:S(2)}) collective-permute-start(bf16[48,2,4480]{2,0,1:T(8,128)(2,1)} %reshape.667), channel_id=1, source_target_pairs={{0,8},{8,16},{16,24},{24,28},{28,20},{20,12},{12,4},{4,0},{1,9},{9... | collective-permute-start | bytes 2580488 | tf_op jit(solution)/shard_map/ppermute | solution.py:656
  613.7 38.2 %collective-permute-start.63 = (bf16[48,2,4480]{2,0,1:T(8,128)(2,1)}, bf16[48,2,4480]{2,0,1:T(8,128)(2,1)S(1)}, u32[]{:S(2)}, u32[]{:S(2)}) collective-permute-start(bf16[48,2,4480]{2,0,1:T(8,128)(2,1)} %reshape.667), channel_id=1, source_target_pairs={{0,4},{8,0},{16,8},{24,16},{28,24},{20,28},{12,20},{4,12},{1,5},{9... | collective-permute-start | bytes 2580488 | tf_op jit(solution)/shard_map/ppermute | solution.py:658
  615.5 24.7 %collective-permute-start.79 = (bf16[144,768]{1,0:T(8,128)(2,1)}, bf16[144,768]{1,0:T(8,128)(2,1)}, u32[]{:S(2)}, u32[]{:S(2)}) collective-permute-start(bf16[144,768]{1,0:T(8,128)(2,1)} %slice.330), channel_id=1, source_target_pairs={{0,4},{8,0},{16,8},{24,16},{28,24},{20,28},{12,20},{4,12},{1,5},{9... | collective-permute-start | bytes 663560 | tf_op jit(solution)/shard_map/ppermute | solution.py:661
  619.7 21.6 %collective-permute-start.78 = (bf16[144,768]{1,0:T(8,128)(2,1)S(1)}, bf16[144,768]{1,0:T(8,128)(2,1)S(1)}, u32[]{:S(2)}, u32[]{:S(2)}) collective-permute-start(bf16[144,768]{1,0:T(8,128)(2,1)S(1)} %slice.329), channel_id=1, source_target_pairs={{0,8},{8,16},{16,24},{24,28},{28,20},{20,12},{12,4},{4,0},{1,9},{9... | collective-permute-start | bytes 663560 | tf_op jit(solution)/shard_map/ppermute | solution.py:660
  623.4 32.7 %collective-permute-start.54 = (bf16[48,3584]{1,0:T(8,128)(2,1)S(1)}, bf16[48,3584]{1,0:T(8,128)(2,1)S(1)}, u32[]{:S(2)}, u32[]{:S(2)}) collective-permute-start(bf16[48,3584]{1,0:T(8,128)(2,1)S(1)} %constant_dynamic-update-slice_fusion.9), channel_id=1, source_target_pairs={{0,8},{8,16},{16,24},{24,28},{28,20},{20,12},{12,4},{4,0},{1,9},{9... | collective-permute-start | bytes 1032200 | tf_op jit(solution)/shard_map/ppermute | solution.py:656
  640.2 16.8 %collective-permute-start.55 = (bf16[48,3584]{1,0:T(8,128)(2,1)S(1)}, bf16[48,3584]{1,0:T(8,128)(2,1)S(1)}, u32[]{:S(2)}, u32[]{:S(2)}) collective-permute-start(bf16[48,3584]{1,0:T(8,128)(2,1)S(1)} %constant_dynamic-update-slice_fusion.9), channel_id=1, source_target_pairs={{0,4},{8,0},{16,8},{24,16},{28,24},{20,28},{12,20},{4,12},{1,5},{9... | collective-permute-start | bytes 1032200 | tf_op jit(solution)/shard_map/ppermute | solution.py:658
  654.1 40.1 %collective-permute-start.64 = (bf16[48,2,4480]{2,0,1:T(8,128)(2,1)S(1)}, bf16[48,2,4480]{2,0,1:T(8,128)(2,1)S(1)}, u32[]{:S(2)}, u32[]{:S(2)}) collective-permute-start(bf16[48,2,4480]{2,0,1:T(8,128)(2,1)S(1)} %collective-permute-done.62), channel_id=1, source_target_pairs={{0,8},{8,16},{16,24},{24,28},{28,20},{20,12},{12,4},{4,0},{1,9},{9... | collective-permute-start | bytes 2580488 | tf_op jit(solution)/shard_map/ppermute | solution.py:656
  655.0 43.0 %collective-permute-start.65 = (bf16[48,2,4480]{2,0,1:T(8,128)(2,1)S(1)}, bf16[48,2,4480]{2,0,1:T(8,128)(2,1)S(1)}, u32[]{:S(2)}, u32[]{:S(2)}) collective-permute-start(bf16[48,2,4480]{2,0,1:T(8,128)(2,1)S(1)} %collective-permute-done.63), channel_id=1, source_target_pairs={{0,4},{8,0},{16,8},{24,16},{28,24},{20,28},{12,20},{4,12},{1,5},{9... | collective-permute-start | bytes 2580488 | tf_op jit(solution)/shard_map/ppermute | solution.py:658
  656.1 25.6 %collective-permute-start.56 = (bf16[48,3584]{1,0:T(8,128)(2,1)S(1)}, bf16[48,3584]{1,0:T(8,128)(2,1)S(1)}, u32[]{:S(2)}, u32[]{:S(2)}) collective-permute-start(bf16[48,3584]{1,0:T(8,128)(2,1)S(1)} %collective-permute-done.54), channel_id=1, source_target_pairs={{0,8},{8,16},{16,24},{24,28},{28,20},{20,12},{12,4},{4,0},{1,9},{9... | collective-permute-start | bytes 1032200 | tf_op jit(solution)/shard_map/ppermute | solution.py:656
  657.1 26.2 %collective-permute-start.57 = (bf16[48,3584]{1,0:T(8,128)(2,1)S(1)}, bf16[48,3584]{1,0:T(8,128)(2,1)S(1)}, u32[]{:S(2)}, u32[]{:S(2)}) collective-permute-start(bf16[48,3584]{1,0:T(8,128)(2,1)S(1)} %collective-permute-done.55), channel_id=1, source_target_pairs={{0,4},{8,0},{16,8},{24,16},{28,24},{20,28},{12,20},{4,12},{1,5},{9... | collective-permute-start | bytes 1032200 | tf_op jit(solution)/shard_map/ppermute | solution.py:658
  681.7 10.5 %collective-permute-start.58 = (bf16[48,3584]{1,0:T(8,128)(2,1)S(1)}, bf16[48,3584]{1,0:T(8,128)(2,1)S(1)}, u32[]{:S(2)}, u32[]{:S(2)}) collective-permute-start(bf16[48,3584]{1,0:T(8,128)(2,1)S(1)} %collective-permute-done.56), channel_id=1, source_target_pairs={{0,8},{8,16},{16,24},{24,28},{28,20},{20,12},{12,4},{4,0},{1,9},{9... | collective-permute-start | bytes 1032200 | tf_op jit(solution)/shard_map/ppermute | solution.py:656
  694.3 23.6 %collective-permute-start.66 = (bf16[48,2,4480]{2,0,1:T(8,128)(2,1)S(1)}, bf16[48,2,4480]{2,0,1:T(8,128)(2,1)S(1)}, u32[]{:S(2)}, u32[]{:S(2)}) collective-permute-start(bf16[48,2,4480]{2,0,1:T(8,128)(2,1)S(1)} %collective-permute-done.64), channel_id=1, source_target_pairs={{0,8},{8,16},{16,24},{24,28},{28,20},{20,12},{12,4},{4,0},{1,9},{9... | collective-permute-start | bytes 2580488 | tf_op jit(solution)/shard_map/ppermute | solution.py:656
  698.1 19.1 %collective-permute-start.67 = (bf16[48,2,4480]{2,0,1:T(8,128)(2,1)S(1)}, bf16[48,2,4480]{2,0,1:T(8,128)(2,1)S(1)}, u32[]{:S(2)}, u32[]{:S(2)}) collective-permute-start(bf16[48,2,4480]{2,0,1:T(8,128)(2,1)S(1)} %collective-permute-done.65), channel_id=1, source_target_pairs={{0,4},{8,0},{16,8},{24,16},{28,24},{20,28},{12,20},{4,12},{1,5},{9... | collective-permute-start | bytes 2580488 | tf_op jit(solution)/shard_map/ppermute | solution.py:658
  (60 other events, 686.5 us)
Sparse Core Ops, SparseCore 0:
  9.6 25.7 all-gather.6
  58.9 29.5 all-gather.8
  248.4 26.2 reduce-scatter.1

commit v3 on v2

--- a/solution.py
+++ b/solution.py
@@ -593,73 +593,141 @@
     )(parts)
 
 
-def ring_pairs(n, step):
-    return [(ring_index(p, n), ring_index((p + step) % n, n)) for p in range(n)]
-
-
-def ring_begin(chunks, take, step):
-    n = lax.axis_size("ctx")
-    place = ring_place(lax.axis_index("ctx"), n)
-    return take(chunks, (place + n - step) % n)
-
-
-def ring_send(held, step):
-    pairs = ring_pairs(lax.axis_size("ctx"), step)
-    return jax.tree.map(lambda a: lax.ppermute(a, "ctx", pairs), held)
-
-
-def ring_add(arrived, chunks, take, step, hop):
-    n = lax.axis_size("ctx")
-    place = ring_place(lax.axis_index("ctx"), n)
-    mine = take(chunks, (place + n * n - step * (hop + 1)) % n)
-    return jax.tree.map(lambda a, b: (a.astype(F32) + b.astype(F32)).astype(BF16), arrived, mine)
-
-
-class RingSum:
-    def __init__(self, right, left, take):
-        self.sides = [(right, 1), (left, -1)]
-        self.take = take
-        self.held = [ring_begin(chunks, take, step) for chunks, step in self.sides]
-        self.hop = 0
-        self.hops = lax.axis_size("ctx") - 1
-
-    def beside(self, *values):
-        if self.hop == self.hops:
-            return values
-        self.hop += 1
-        arrived = [ring_send(h, step) for h, (_, step) in zip(self.held, self.sides)]
-        if values:
-            arrived, *values = together(arrived, *values)
-        self.held = [
-            ring_add(a, chunks, self.take, step, self.hop)
-            for a, (chunks, step) in zip(arrived, self.sides)
-        ]
-        return values
-
-    def finish(self):
-        while self.hop < self.hops:
-            self.beside()
-        return self.held
-
-
-def ring_gather(own, halves, joined):
-    n = lax.axis_size("ctx")
-    place = ring_place(lax.axis_index("ctx"), n)
-    out = jnp.zeros((n,) + own.shape, F32)
-
-    def put(out, block, q):
-        return lax.dynamic_update_index_in_dim(out, block.astype(F32), q % n, 0)
-
-    out = put(out, own, place)
-    right = left = own
-    for hop in range(1, n // 2):
-        right = lax.ppermute(right, "ctx", ring_pairs(n, 1))
-        out = put(out, right, place + n - hop)
-        left = lax.ppermute(left, "ctx", ring_pairs(n, -1))
-        out = put(out, left, place + hop)
-    right = lax.ppermute(halves(right)[0], "ctx", ring_pairs(n, 1))
-    left = lax.ppermute(halves(left)[1], "ctx", ring_pairs(n, -1))
-    return put(out, joined(right, left), place + n // 2)
+def ring_sum_kernel(n, plan, arrays, *refs):
+    ins, outs = refs[:arrays], refs[arrays : 2 * arrays]
+    refs = refs[2 * arrays :]
+    count = len(plan)
+    arrived, stages, sends, recvs = (refs[i * count : (i + 1) * count] for i in range(4))
+    ctx = lax.axis_index("ctx")
+    me = lax.axis_index("fsdp")
+    place = ring_place(ctx, n)
+    around = {step: (ring_index((place + n + step) % n, n), me) for step in (1, -1)}
+    greet([around[1], around[-1]])
+
+    def copy(i, hop, src):
+        step = plan[i][3]
+        return remote(src, arrived[i].at[hop], sends[i].at[hop], recvs[i].at[hop], around[step])
+
+    def chunk(i, hop):
+        step = plan[i][3]
+        return ring_index((place + n * n - step * (hop + 1)) % n, n)
+
+    def window(i, group, hop):
+        which, low, high, _ = plan[i]
+        return ins[which][group, chunk(i, hop), :, low:high].astype(F32)
+
+    for i, (which, low, high, _) in enumerate(plan):
+        copy(i, 0, ins[which].at[:, chunk(i, 0), :, pl.ds(low, high - low)]).start()
+
+    def add(i, hop, store):
+        copy(i, hop - 1, stages[i].at[0]).wait_recv()
+
+        def group_add(group, carry):
+            store(group, (arrived[i][hop - 1, group].astype(F32) + window(i, group, hop)).astype(BF16))
+            return carry
+
+        lax.fori_loop(0, ins[plan[i][0]].shape[0], group_add, 0)
+
+    def one_hop(hop, carry):
+        slot = hop % 2
+        for i in range(count):
+            @pl.when(hop > 2)
+            def _():
+                copy(i, hop - 2, stages[i].at[slot]).wait_send()
+
+            def store(group, value):
+                stages[i][slot, group] = value
+
+            add(i, hop, store)
+            if i:
+                copy(i - 1, hop, stages[i - 1].at[slot]).start()
+        copy(count - 1, hop, stages[count - 1].at[slot]).start()
+        return carry
+
+    lax.fori_loop(1, n - 1, one_hop, 0)
+    for i, (which, low, high, _) in enumerate(plan):
+        def store(group, value):
+            outs[which][group, :, low:high] = value
+
+        add(i, n - 1, store)
+    for i, (which, low, high, _) in enumerate(plan):
+        copy(i, 0, ins[which].at[:, chunk(i, 0), :, pl.ds(low, high - low)]).wait_send()
+        for hop in (n - 3, n - 2):
+            copy(i, hop, stages[i].at[hop % 2]).wait_send()
+
+
+def ring_sum(arrays, plan, collective):
+    n = arrays[0].shape[1]
+    dma = pltpu.SemaphoreType.DMA
+    blocks = [
+        (arrays[which].shape[0], arrays[which].shape[2], high - low) for which, low, high, _ in plan
+    ]
+    return pl.pallas_call(
+        functools.partial(ring_sum_kernel, n, plan, len(arrays)),
+        out_shape=tuple(
+            jax.ShapeDtypeStruct((a.shape[0],) + a.shape[2:], BF16) for a in arrays
+        ),
+        in_specs=in_vmem(len(arrays)),
+        out_specs=tuple(in_vmem(len(arrays))),
+        scratch_shapes=[pltpu.VMEM((n - 1,) + b, BF16) for b in blocks]
+        + [pltpu.VMEM((2,) + b, BF16) for b in blocks]
+        + [dma((n - 1,)) for _ in blocks] * 2,
+        compiler_params=pltpu.CompilerParams(
+            vmem_limit_bytes=VMEM_LIMIT, collective_id=collective, has_side_effects=True
+        ),
+        cost_estimate=pl.CostEstimate(flops=0, bytes_accessed=200_000_000, transcendentals=0),
+        name="ring_sum",
+    )(*arrays)
+
+
+def ring_gather_kernel(n, own, out, sends, recvs):
+    ctx = lax.axis_index("ctx")
+    me = lax.axis_index("fsdp")
+    place = ring_place(ctx, n)
+    around = {step: (ring_index((place + n + step) % n, n), me) for step in (1, -1)}
+    greet([around[1], around[-1]])
+    middle = own.shape[-1] // 2
+    far = n // 2
+
+    def copy(step, half, hop):
+        lanes = pl.ds(half * middle, middle)
+        block = out.at[ring_index((place + n - step * hop) % n, n), :, lanes]
+        src = block if hop else own.at[:, lanes]
+        row = half if step == 1 else 2 + half
+        return remote(src, block, sends.at[row, hop], recvs.at[row, hop], around[step])
+
+    def hops(step, half):
+        return far if (step == 1) == (half == 0) else far - 1
+
+    lines = [(1, 0), (-1, 1), (1, 1), (-1, 0)]
+    for step, half in lines:
+        copy(step, half, 0).start()
+    out[ctx] = own[...]
+    for hop in range(1, far + 1):
+        for step, half in lines:
+            if hop <= hops(step, half):
+                copy(step, half, hop - 1).wait_recv()
+                if hop < hops(step, half):
+                    copy(step, half, hop).start()
+    for step, half in lines:
+        for hop in range(hops(step, half)):
+            copy(step, half, hop).wait_send()
+
+
+def ring_gather(own, n, collective):
+    dma = pltpu.SemaphoreType.DMA
+    return pl.pallas_call(
+        functools.partial(ring_gather_kernel, n),
+        out_shape=jax.ShapeDtypeStruct((n,) + own.shape, BF16),
+        in_specs=in_vmem(1),
+        out_specs=in_vmem(1)[0],
+        scratch_shapes=[dma((4, n // 2))] * 2,
+        compiler_params=pltpu.CompilerParams(
+            vmem_limit_bytes=VMEM_LIMIT, collective_id=collective, has_side_effects=True
+        ),
+        cost_estimate=pl.CostEstimate(flops=0, bytes_accessed=80_000_000, transcendentals=0),
+        name="ring_gather",
+    )(own)
 
 
 def exchange(pieces, axis):
@@ -731,13 +799,9 @@
             lax.dynamic_slice_in_dim(bias, q_width + kv_width + my_kv * HEAD_DIM, HEAD_DIM),
         ]
     )
-    gate_up_pieces = [
-        w_gate_up[:, e].reshape(d_shard, n_fsdp, ff_shard).transpose(1, 0, 2) for e in range(2)
-    ]
+    gate_up_pieces = w_gate_up.reshape(d_shard, 2, n_fsdp, ff_shard).transpose(2, 1, 0, 3)
     x_all, w_qkv_cols, gate_up_pieces = together(x_all, w_qkv_cols, gate_up_pieces)
-    w_gate_cols, w_up_cols = (
-        exchange(pieces, "fsdp").reshape(D, ff_shard) for pieces in gate_up_pieces
-    )
+    gate_up_cols = exchange(gate_up_pieces, "fsdp")
     cot_all = lax.all_gather(cotangent[0], "fsdp", axis=1, tiled=True).reshape(rows, D)
 
     x32 = x_all.astype(F32)
@@ -771,6 +835,7 @@
         collective=1,
     )
     normed2 = normed2.reshape(rows, D)
+    w_gate_cols, w_up_cols = (gate_up_cols[:, e].reshape(D, ff_shard) for e in range(2))
     gate_val = jnp.dot(normed2, w_gate_cols, preferred_element_type=F32)
     up_val = jnp.dot(normed2, w_up_cols, preferred_element_type=F32)
     sigmoid_gate = jax.nn.sigmoid(gate_val)
@@ -811,25 +876,25 @@
         for piece in (d_gate16, d_up16)
     )
 
-    def take(arrays, q):
-        return (
-            lax.dynamic_index_in_dim(arrays[0], q, 1, keepdims=False),
-            lax.dynamic_index_in_dim(arrays[1], q, 0, keepdims=False),
-        )
-
-    mlp_ring = RingSum((d_w_gate, d_w_down[..., :side]), (d_w_up, d_w_down[..., side:]), take)
+    gate_sum, up_sum, down_sum = ring_sum(
+        (d_w_gate, d_w_up, d_w_down[None]),
+        ((0, 0, ff_shard, 1), (1, 0, ff_shard, -1), (2, 0, side, 1), (2, side, D, -1)),
+        7,
+    )
+    d_normed2, gate_sum, up_sum, down_sum = together(by_member(d_normed2), gate_sum, up_sum, down_sum)
+    gate_up_sum = exchange(jnp.stack([gate_sum, up_sum], 1), "fsdp")
+    gate_up_sum = gate_up_sum.transpose(2, 1, 0, 3).reshape(chunk_rows, 2, n_fsdp * ff_shard)
+    d_w_gate_up = lax.all_gather(gate_up_sum, "ctx", axis=0, tiled=True).astype(F32)
+    d_w_down = lax.all_gather(down_sum[0], "ctx", axis=0, tiled=True)[:ff_shard].astype(F32)
     d_hidden, dh_all, d_gain_two = group_sum(
-        "mlp", by_member(d_normed2), hidden, cotangent[0], gain_two[None], collective=2
-    )
-    d_hidden, dh_all, d_gain_two = mlp_ring.beside(d_hidden, dh_all, d_gain_two)
+        "mlp", d_normed2, hidden, cotangent[0], gain_two[None], collective=2
+    )
     dh_all = dh_all.reshape(rows, D)
     d_attended16 = contract_cols(dh_all, w_out).astype(BF16).reshape(2, stretch_len, q_cols)
     d_query, d_kv = attend_back(
         table, ids, query, keys_values, attended, d_attended16, lse, heads
     )
-    d_query, d_kv = mlp_ring.beside(d_query, d_kv)
     d_kv_own = return_grads(d_kv.reshape(n_ctx, 2, stretch_len, 2 * HEAD_DIM), 5).reshape(rows, -1)
-    d_kv_own, d_query = mlp_ring.beside(d_kv_own, d_query)
 
     d_w_out = contract_rows(attended16, dh_all).astype(BF16).reshape(n_ctx, chunk_rows, D)
     d_rotated = jnp.concatenate([d_query.reshape(rows, q_cols), d_kv_own[:, :HEAD_DIM]], 1)
@@ -840,7 +905,6 @@
     d_bias = jnp.sum(d_qkv, 0)
     d_qkv16 = d_qkv.astype(BF16)
     d_normed1 = by_member(contract_cols(d_qkv16, w_qkv_cols))
-    d_normed1, d_qkv16, d_bias = mlp_ring.beside(d_normed1, d_qkv16, d_bias)
     d_tokens, d_gain_one = group_sum(
         "input",
         d_normed1,
@@ -849,7 +913,6 @@
         gain_one[None],
         collective=3,
     )
-    d_tokens, d_gain_one = mlp_ring.beside(d_tokens, d_gain_one)
     d_tokens = d_tokens.reshape(tokens.shape)
 
     zeros = jnp.zeros_like(d_bias)
@@ -860,34 +923,16 @@
     parts = jnp.pad(parts, ((0, 0), (0, -parts.shape[1] % 8), (0, 0)))
     vector = vector_sum(parts, n_ctx, 6)
     d_w_qkv = contract_rows(normed1, d_qkv16).astype(BF16).reshape(n_fsdp, n_ctx, chunk_rows, -1)
-    vector, d_w_qkv, d_w_out = mlp_ring.beside(vector, d_w_qkv, d_w_out)
     vector = vector.reshape(-1)
-    (gate_sum, down_left), (up_sum, down_right) = mlp_ring.finish()
-    gate_sum, up_sum, d_w_qkv, d_w_out = together(gate_sum, up_sum, d_w_qkv, d_w_out)
-    gate_up_sum = exchange(jnp.stack([gate_sum, up_sum], 1), "fsdp")
-    gate_up_sum = gate_up_sum.transpose(2, 1, 0, 3).reshape(chunk_rows, 2, n_fsdp * ff_shard)
-
-    def halves(block):
-        middle = block.shape[-1] // 2
-        return block[..., :middle], block[..., middle:]
-
-    def joined(first, second):
-        return jnp.concatenate([first, second], -1)
-
-    d_w_gate_up = ring_gather(gate_up_sum, halves, joined).reshape(d_shard, 2, n_fsdp * ff_shard)
-    d_w_down = ring_gather(joined(down_left, down_right), halves, joined)
-    d_w_down = d_w_down.reshape(n_ctx * down_rows, D)[:ff_shard]
-
-    ring = RingSum(
-        (d_w_qkv[..., :q_cols], d_w_out[..., :side]), (d_w_qkv[..., q_cols:], d_w_out[..., side:]), take
-    )
-    (q_sum, out_left), (kv_sum, out_right) = ring.finish()
-    d_w_pieces = exchange(joined(q_sum, kv_sum), "fsdp")
-
+    pieces, out_sum = ring_sum(
+        (d_w_qkv, d_w_out[None]),
+        ((0, 0, q_cols, 1), (0, q_cols, d_w_qkv.shape[-1], -1), (1, 0, side, 1), (1, side, D, -1)),
+        8,
+    )
+    d_w_pieces = exchange(pieces, "fsdp")
     qkv_sum = by_columns([d_w_pieces[f] for f in range(n_fsdp)])
-    attention_sum = ring_gather(
-        jnp.concatenate([qkv_sum, joined(out_left, out_right)], -1), halves, joined
-    ).reshape(d_shard, -1)
+    attention_sum = ring_gather(jnp.concatenate([qkv_sum, out_sum[0]], -1), n_ctx, 9)
+    attention_sum = attention_sum.reshape(d_shard, -1).astype(F32)
     d_w_qkv, d_w_out = attention_sum[:, :-D], attention_sum[:, -D:]
 
     d_gain_attn = vector[:d_shard]

time: 748 us -> 679 us (0.908)
  Pallas kernels: 164 us -> 400 us
  waiting for transfers between devices: 149 us -> 15.8 us
  starting transfers between devices: 113 us -> 14.3 us
  other arithmetic: 91.3 us -> 26 us
  blocking collectives: 6.27 us -> 21.5 us
  local copies, waits for them, and re-layouts: 130 us -> 118 us
    pallas_call x0 -> x3, Pallas kernels: none -> 201 us  [the longest x2 169 us: ring_sum(): pl.pallas_call(functools.partial(ring_sum_kernel, n, plan, len(arrays)),...]
    ppermute x80 -> x0, waiting for transfers between devices: 101 us -> none  [the longest x56 41.9 us: ring_send(): return jax.tree.map(lambda a: lax.ppermute(a, 'ctx', pairs), held)]
    ppermute x80 -> x0, starting transfers between devices: 92.4 us -> none  [the longest x56 64.6 us: ring_send(): return jax.tree.map(lambda a: lax.ppermute(a, 'ctx', pairs), held)]
    convert_element_type x57 -> x2, other arithmetic: 52 us -> 8.27 us  [the longest x1 5.83 us: body(): lax.all_gather(down_sum[0], 'ctx', axis=0, tiled=True)[:ff_shard]]
    unnamed x93 -> x74, local copies, waits for them, and re-layouts: 9.84 us -> 43.7 us
    all_to_all x5 -> x3, waiting for transfers between devices: 46.5 us -> 14.4 us  [exchange(): return lax.all_to_all(pieces, axis, split_axis=0, concat_axis=0, tiled=True)]
    dynamic_update_slice x8 -> x0, local copies, waits for them, and re-layouts: 15.9 us -> none  [put(): return lax.dynamic_update_index_in_dim(out, block.astype(F32), q % n, 0)]
    all_to_all x0 -> x1, blocking collectives: none -> 15.2 us  [exchange(): return lax.all_to_all(pieces, axis, split_axis=0, concat_axis=0, tiled=True)]
  transfers between devices with their start and end apart: 88 -> 8, of which waited for: 21 -> 2; matrix products, arithmetic and copies ran while one was open for 34% -> 22% of each run, Pallas kernels for 22% -> 60%
where the time goes in v3:
time: 679 us; the launch traced here: 671 us
  Pallas kernels  400 us (59%)
  local copies, waits for them, and re-layouts  118 us (17%)
  matrix products  59.4 us (9%)
  other arithmetic  26 us (4%)
  blocking collectives  21.5 us (3%)
  waiting for transfers between devices  15.8 us (2%)
  between operations  15.4 us (2%)
  starting transfers between devices  14.3 us (2%)
    pallas_call x2, Pallas kernels, ring_sum(): pl.pallas_call(functools.partial(ring_sum_kernel, n, plan, len(arrays)),...  169 us
    pallas_call x3, Pallas kernels, group_sum(): pl.pallas_call(functools.partial(sum_kernel, mode, n, cuts), out_shape=ou...  81.2 us
    unnamed x74, local copies, waits for them, and re-layouts  43.7 us
    dot_general x10, matrix products, dot(): lax.dot_general(left, right, (contract, ((), ())), preferred_element_type...  40 us
    pallas_call x1, Pallas kernels, return_grads(): pl.pallas_call(functools.partial(return_kernel, n), out_shape=jax.ShapeDt...  38.2 us
    pallas_call x1, Pallas kernels, ring_gather(): pl.pallas_call(functools.partial(ring_gather_kernel, n), out_shape=jax.Sh...  31.5 us
    pallas_call x1, Pallas kernels, vector_sum(): pl.pallas_call(functools.partial(vector_kernel, n_ctx, n), out_shape=jax....  27.4 us
    optimization_barrier x2, local copies, waits for them, and re-layouts, together(): return lax.optimization_barrier(values)  24.5 us
  transfers between devices with their start and end apart: 8, of which 2 were waited for; matrix products, arithmetic and copies ran while one was open for 22% of the time, Pallas kernels for 60%

profile of v3, /device:TPU:0, one launch (start us, length us, event | category | flops | bytes accessed | tf_op | source)
XLA Modules:
  0.0 670.6 jit_solution(4678179129085573929)
XLA Ops:
  8.9 6.3 all-gather.4
  15.2 1.1 fusion.23
  16.3 1.4 fusion.22
  17.8 1.6 pad_maximum_fusion
  19.4 4.4 all-to-all-start
  23.8 18.0 %copy.91 = bf16[384,2,4480]{0,2,1:T(8,128)(2,1)} copy(bf16[384,2,4480]{2,1,0:T(2,128)(2,1)} %param.17) | data formatting | bytes 13762560 | tf_op jit(solution)/shard_map/optimization_barrier | solution.py:738
  41.8 9.8 %all-to-all-done = bf16[4,384,640]{2,1,0:T(8,128)(2,1)} async-done(((bf16[4,384,640]{2,1,0:T(8,128)(2,1)}), bf16[4,384,640]{2,1,0:T(8,128)(2,1)}, u32[]{:S(2)}, u32[]{:S(2)}) %all-to-all-start) | async-done | bytes 1966112 | tf_op jit(solution)/shard_map/all_to_all | solution.py:734
  51.6 6.5 copy.96
  58.2 5.5 all-to-all-start.1
  66.0 1.2 broadcast_multiply_fusion
  68.7 1.8 multiply_cosine_fusion
  70.5 1.8 fusion.1
  72.3 3.1 convolution_add_fusion.1
  75.4 1.1 slice.246
  77.2 2.5 reshape.251
  79.7 2.3 fusion.25
  83.4 1.1 copy.111
  84.5 2.0 reshape.292.q_ref
  86.5 1.1 pad_maximum_fusion.14
  87.6 1.6 pad_maximum_fusion.13.own
  89.3 23.2 %share_keys.1 = bf16[8,2,256,256]{3,2,1,0:T(8,128)(2,1)} custom-call(bf16[2,256,256]{2,1,0:T(8,128)(2,1)} %pad_maximum_fusion.13.own), custom_call_target="tpu_custom_call" | custom-call | bytes 60000000 | tf_op jit(solution)/shard_map/share_keys/pallas_call | solution.py:469
  112.5 13.5 %attend.1 = (bf16[2,256,384]{2,1,0:T(8,128)(2,1)}, f32[2,1,768]{2,1,0:T(1,128)}) custom-call(s32[16]{0:T(128)} %pad_add_fusion.table, s32[2]{0:T(128)} %get-tuple-element.107.ids, bf16[2,256,384]{2,1,0:T(8,128)(2,1)} %reshape.292.q_ref, bf16[4096,256]{1,0:T(8,128)(2,1)} %bitcast.135), custom_call_target="tpu_custom_call" | custom-call | flops 1610612736 | bytes 2097152 | tf_op jit(solution)/shard_map/attend/pallas_call | solution.py:169
  126.0 3.5 convolution_convert_fusion.6
  129.5 39.1 %group_sum_attention.1 = (f32[2,64,1536]{2,1,0:T(8,128)}, bf16[2,4,64,1536]{3,2,1,0:T(8,128)(2,1)}) custom-call(bf16[2,4,64,1536]{3,2,1,0:T(8,128)(2,1)} %bitcast.121, bf16[2,64,1536]{2,1,0:T(8,128)(2,1)} %bitcast.127, f32[1,1536]{1,0:T(1,128)} %bitcast.154), custom_call_target="tpu_custom_call" | custom-call | flops 1966080 | bytes 60000000 | tf_op jit(solution)/shard_map/group_sum_attention/pallas_call | solution.py:371
  168.7 6.7 fusion.21
  175.4 5.6 copy.97
  181.0 5.6 copy.98
  186.6 6.0 fusion.28
  192.6 3.4 fusion.29
  196.0 7.1 %multiply_convert_fusion = (bf16[512,1120]{0,1:T(8,128)(2,1)}, bf16[512,1120]{0,1:T(8,128)(2,1)}, bf16[512,1120]{0,1:T(8,128)(2,1)S(1)}) fusion(f32[512,1120]{0,1:T(8,128)} %fusion.28, f32[512,1120]{0,1:T(8,128)} %fusion.29, bf16[512,1536]{1,0:T(8,128)(2,1)} %bitcast.163, bf16[1120,1536]{1,0:T(8,128)(2,1)S(1)} %copy-done), kind=kOutput, calls=%fused_computation.18 | convolution fusion | flops 1770782720 | bytes 13041664 | tf_op jit(solution)/shard_map/dot_general | solution.py:55
  203.1 3.4 convolution_convert_fusion.5
  207.1 3.7 convolution_convert_fusion.1
  210.8 3.8 copy.99
  214.6 3.8 convolution_convert_fusion
  218.4 3.9 copy.100
  222.3 3.9 convolution_convert_fusion.2
  226.3 2.1 pad.9
  228.4 110.3 %ring_sum.2 = (bf16[4,48,1120]{2,1,0:T(8,128)(2,1)}, bf16[4,48,1120]{2,1,0:T(8,128)(2,1)}, bf16[1,144,1536]{2,1,0:T(8,128)(2,1)}) custom-call(bf16[4,8,48,1120]{3,2,1,0:T(8,128)(2,1)} %bitcast.118, bf16[4,8,48,1120]{3,2,1,0:T(8,128)(2,1)} %bitcast.119, bf16[1,8,144,1536]{3,2,1,0:T(8,128)(2,1)} %bitcast.120), custom_call_target="tpu_custom_call" | custom-call | bytes 200000000 | tf_op jit(solution)/shard_map/ring_sum/pallas_call | solution.py:665
  338.7 4.4 fusion.30
  343.2 3.5 fusion.4
  347.0 15.2 %all_to_all.20 = bf16[4,2,48,1120]{3,2,1,0:T(8,128)(2,1)S(1)} all-to-all(bf16[4,2,48,1120]{3,2,1,0:T(8,128)(2,1)S(1)} %copy.108), channel_id=1, replica_groups=mesh['ctx'=8,'fsdp'=4] {'fsdp'}, dimensions={0} | all-to-all | bytes 1720320 | tf_op jit(solution)/shard_map/all_to_all | solution.py:734
  362.7 1.6 reshape.275
  364.9 25.8 %group_sum_mlp.1 = (f32[2,64,1536]{2,1,0:T(8,128)}, bf16[2,4,64,1536]{3,2,1,0:T(8,128)(2,1)}, f32[1,1536]{1,0:T(1,128)}) custom-call(bf16[2,4,64,1536]{3,2,1,0:T(8,128)(2,1)} %bitcast.142, f32[2,64,1536]{2,1,0:T(8,128)} %get-tuple-element.41.refs_1_, bf16[2,64,1536]{2,1,0:T(8,128)(2,1)} %bitcast.144, f32[1,1536]{1,0:T(1,128)} %bitcast.155), custom_call_target="tpu_custom_call" | custom-call | flops 1966080 | bytes 60000000 | tf_op jit(solution)/shard_map/group_sum_mlp/pallas_call | solution.py:371
  390.7 3.2 convolution_convert_fusion.8
  393.9 16.1 %attend_back.1 = (f32[2,256,384]{2,1,0:T(8,128)}, bf16[4096,256]{1,0:T(8,128)(2,1)}) custom-call(s32[16]{0:T(128)} %pad_add_fusion.table, s32[2]{0:T(128)} %get-tuple-element.107.ids, bf16[2,256,384]{2,1,0:T(8,128)(2,1)} %reshape.292.q_ref, bf16[4096,256]{1,0:T(8,128)(2,1)} %bitcast.136, bf16[2,256,384]{2,1,0:T(8,128)(2,1)} %get-tuple-element.40.o_ref, ...), custom_call_target="tpu_custom_call" | custom-call | flops 4026531840 | bytes 4194304 | tf_op jit(solution)/shard_map/attend_back/pallas_call | solution.py:190
  410.0 38.2 %return_grads.1 = f32[2,256,256]{2,1,0:T(8,128)} custom-call(bf16[8,2,256,256]{3,2,1,0:T(8,128)(2,1)} %bitcast.133), custom_call_target="tpu_custom_call" | custom-call | bytes 80000000 | tf_op jit(solution)/shard_map/return_grads/pallas_call | solution.py:521
  448.1 1.1 fusion.26
  451.0 1.3 copy.117
  452.3 1.5 multiply_add_fusion
  454.7 4.1 convolution_convert_fusion.4
  458.9 16.2 %group_sum_input.1 = (f32[2,64,1536]{2,1,0:T(8,128)}, f32[1,1536]{1,0:T(1,128)}) custom-call(bf16[2,4,64,1536]{3,2,1,0:T(8,128)(2,1)} %bitcast.143, bf16[2,64,1536]{2,1,0:T(8,128)(2,1)} %bitcast.128, f32[2,64,1536]{2,1,0:T(8,128)} %get-tuple-element.52.refs_2_, f32[1,1536]{1,0:T(1,128)} %bitcast.158), custom_call_target="tpu_custom_call" | custom-call | flops 1966080 | bytes 60000000 | tf_op jit(solution)/shard_map/group_sum_input/pallas_call | solution.py:371
  476.8 27.4 %vector_sum.1 = f32[16,128]{1,0:T(8,128)} custom-call(f32[4,16,128]{2,1,0:T(8,128)} %select_maximum_fusion.parts), custom_call_target="tpu_custom_call" | custom-call | bytes 30000000 | tf_op jit(solution)/shard_map/vector_sum/pallas_call | solution.py:574
  504.2 3.4 convolution_convert_fusion.7
  507.6 2.9 convolution_convert_fusion.3
  510.5 59.1 %ring_sum.3 = (bf16[4,48,640]{2,1,0:T(8,128)(2,1)}, bf16[1,48,1536]{2,1,0:T(8,128)(2,1)}) custom-call(bf16[4,8,48,640]{3,2,1,0:T(8,128)(2,1)} %bitcast.137, bf16[1,8,48,1536]{3,2,1,0:T(8,128)(2,1)} %bitcast.145), custom_call_target="tpu_custom_call" | custom-call | bytes 200000000 | tf_op jit(solution)/shard_map/ring_sum/pallas_call | solution.py:665
  569.6 3.6 all-to-all-start.2
  574.4 4.6 all-to-all-done.2
  580.8 31.5 %ring_gather.1 = bf16[8,48,3584]{2,1,0:T(8,128)(2,1)} custom-call(bf16[48,3584]{1,0:T(8,128)(2,1)} %copy-done.18), custom_call_target="tpu_custom_call" | custom-call | bytes 80000000 | tf_op jit(solution)/shard_map/ring_gather/pallas_call | solution.py:719
  612.4 2.4 bitcast_convert_fusion
  614.8 1.9 slice.274
  616.7 1.6 slice.275
  618.3 1.8 fusion.14
  620.1 5.8 fusion
  626.0 37.0 %copy.110 = f32[384,2,4480]{2,1,0:T(2,128)} copy(bf16[384,2,4480]{2,0,1:T(8,128)(2,1)} %all-gather.10.cloned.1.call-done) | data formatting | bytes 20643840
  (135 shorter events, 17.0 us)
Async XLA Ops:
  7.2 188.8 %copy-start = (bf16[1120,1536]{1,0:T(8,128)(2,1)S(1)}, bf16[1120,1536]{1,0:T(8,128)(2,1)}, u32[]{:S(2)}) copy-start(bf16[1120,1536]{1,0:T(8,128)(2,1)} %param.18) | copy-start | bytes 10321924
  7.2 44.4 %all-gather.12.cloned.1.call-start = ((), (), s32[]{:S(2)}) async-start(), calls=%async_computation.7 | async-start | bytes 1966080 | tf_op jit(solution)/shard_map/all_gather | solution.py:775
  19.4 32.2 %all-to-all-start = ((bf16[4,384,640]{2,1,0:T(8,128)(2,1)}), bf16[4,384,640]{2,1,0:T(8,128)(2,1)}, u32[]{:S(2)}, u32[]{:S(2)}) async-start(bf16[4,384,640]{2,1,0:T(8,128)(2,1)} %pad_maximum_fusion), calls=%async_computation | async-start | bytes 3932160 | tf_op jit(solution)/shard_map/all_to_all | solution.py:734
  58.2 6.3 copy-start.23
  58.2 110.5 %all-to-all-start.1 = ((bf16[4,2,384,1120]{2,3,1,0:T(8,128)(2,1)}), bf16[4,2,384,1120]{2,3,1,0:T(8,128)(2,1)}, u32[]{:S(2)}, u32[]{:S(2)}) async-start(bf16[4,2,384,1120]{2,3,1,0:T(8,128)(2,1)} %copy.96), calls=%async_computation.1 | async-start | bytes 13762560 | tf_op jit(solution)/shard_map/all_to_all | solution.py:734
  63.7 132.3 %all-gather.14.cloned.1.call-start = ((), (), s32[]{:S(2)}) async-start(), calls=%async_computation.8 | async-start | bytes 1966080 | tf_op jit(solution)/shard_map/all_gather | solution.py:805
  64.4 553.9 %reduce-scatter.2.cloned.1.call-start = ((), (), s32[]{:S(2)}) async-start(), calls=%async_computation.5 | async-start | bytes 1966080 | tf_op jit(solution)/shard_map/reduce_scatter | solution.py:822
  67.9 4.4 copy-start.10
  79.7 2.3 copy-start.7
  79.7 2.3 copy-start.9
  82.3 0.8 copy-start.2
  82.3 1.0 copy-start.3
  186.6 6.0 copy-start.4
  186.6 6.0 copy-start.22
  203.1 3.4 copy-start.26
  206.6 413.6 %all-gather.16.cloned.1.call-start = ((), (), s32[]{:S(2)}) async-start(), calls=%async_computation.9 | async-start | bytes 3981312 | tf_op jit(solution)/shard_map/all_gather | solution.py:888
  228.4 110.3 %copy-start.25 = (bf16[512,1120]{0,1:T(8,128)(2,1)S(1)}, bf16[512,1120]{0,1:T(8,128)(2,1)}, u32[]{:S(2)}) copy-start(bf16[512,1120]{0,1:T(8,128)(2,1)} %get-tuple-element.111) | copy-start | bytes 3440644
  338.7 4.4 copy-start.5
  338.7 4.4 copy-start.24
  343.2 3.6 copy-start.16
  343.2 3.6 copy-start.17
  346.7 279.3 %all-gather.10.cloned.1.call-start = ((), (), s32[]{:S(2)}) async-start(), calls=%async_computation.6 | async-start | bytes 7741440 | tf_op jit(solution)/shard_map/all_gather | solution.py:887
  364.2 26.5 %copy-start.12 = (bf16[384,1536]{1,0:T(8,128)(2,1)S(1)}, bf16[384,1536]{1,0:T(8,128)(2,1)}, u32[]{:S(2)}) copy-start(bf16[384,1536]{1,0:T(8,128)(2,1)} %param.15) | copy-start | bytes 3538948
  410.0 40.2 %copy-start.15 = (f32[2,256,384]{2,1,0:T(8,128)S(1)}, f32[2,256,384]{2,1,0:T(8,128)}, u32[]{:S(2)}) copy-start(f32[2,256,384]{2,1,0:T(8,128)} %get-tuple-element.50) | copy-start | bytes 2359300
  450.6 1.7 copy-start.8
  453.8 1.0 copy-start.13
  458.9 16.2 %copy-start.21 = (f32[1,1536]{1,0:T(1,128)S(1)}, f32[1,1536]{1,0:T(1,128)}, u32[]{:S(2)}) copy-start(f32[1,1536]{1,0:T(1,128)} %get-tuple-element.55) | copy-start | bytes 18436
  458.9 45.3 %copy-start.19 = (bf16[2,256,384]{2,1,0:T(8,128)(2,1)S(1)}, bf16[2,256,384]{2,1,0:T(8,128)(2,1)}, u32[]{:S(2)}) copy-start(bf16[2,256,384]{2,1,0:T(8,128)(2,1)} %get-tuple-element.40.o_ref) | copy-start | bytes 1179652
  504.2 3.4 copy-start.11
  510.5 62.7 %copy-start.20 = (f32[16,128]{1,0:T(8,128)S(1)}, f32[16,128]{1,0:T(8,128)}, u32[]{:S(2)}) copy-start(f32[16,128]{1,0:T(8,128)} %vector_sum.1) | copy-start | bytes 24580
  569.6 9.4 %all-to-all-start.2 = ((bf16[4,48,640]{2,1,0:T(8,128)(2,1)}), bf16[4,48,640]{2,1,0:T(8,128)(2,1)S(1)}, u32[]{:S(2)}, u32[]{:S(2)}) async-start(bf16[4,48,640]{2,1,0:T(8,128)(2,1)} %get-tuple-element.56), calls=%async_computation.3 | async-start | bytes 491520 | tf_op jit(solution)/shard_map/all_to_all | solution.py:734
  580.1 0.7 copy-start.18
  616.7 1.6 copy-start.6
  626.0 37.0 %copy-start.14 = (f32[2,64,1536]{2,1,0:T(8,128)S(1)}, f32[2,64,1536]{2,1,0:T(8,128)}, u32[]{:S(2)}) copy-start(f32[2,64,1536]{2,1,0:T(8,128)} %get-tuple-element.53) | copy-start | bytes 2359300
  626.0 37.9 %copy-start.1 = (bf16[1120,1536]{1,0:T(8,128)(2,1)S(1)}, bf16[1120,1536]{1,0:T(8,128)(2,1)}, u32[]{:S(2)}) copy-start(bf16[1120,1536]{1,0:T(8,128)(2,1)} %param.18) | copy-start | bytes 10321924
Sparse Core Ops, SparseCore 0:
  9.6 25.7 all-gather.11
  66.1 29.5 all-gather.13
  206.7 28.0 reduce-scatter.1
  346.8 63.6 all-gather.15
  413.2 132.8 all-gather.9

commit v4 on v3

--- a/solution.py
+++ b/solution.py
@@ -231,7 +231,7 @@
     return ctx, me, partner, others, senders
 
 
-def sum_kernel(mode, n, cuts, *refs):
+def sum_phases(mode, n, cuts, *refs):
     gathers = mode != "input"
     if mode == "attention":
         partial, tokens, gain, hidden_out, all_out = refs[:5]
@@ -245,7 +245,6 @@
     rows = partial.shape[2]
     piece = rows // cuts
     chunks = [(w, i * piece) for w in range(2) for i in range(cuts)]
-    greet([(ctx, partner)] + [(ctx, o) for o in others])
 
     def part(ref, w, lead, start):
         return ref.at[w, lead, pl.ds(start, piece)]
@@ -263,6 +262,7 @@
             )
             copy.start()
             first.append(copy)
+    yield
 
     second = []
 
@@ -290,6 +290,7 @@
         if c:
             post(c - 1)
     post(len(chunks) - 1)
+    yield
 
     if mode != "attention":
         d_gain[...] = jnp.zeros_like(d_gain)
@@ -338,6 +339,7 @@
     if not gathers:
         return
     near_copies.append(spread(len(chunks) - 1))
+    yield
 
     forwards = []
     for c, (w, start) in enumerate(chunks):
@@ -347,16 +349,22 @@
             copy = remote(block, block, fwd_s.at[c, k], fwd_r.at[c, k], (ctx, partner))
             copy.start()
             forwards.append(copy)
+    yield
     for copy in third:
         copy.wait_send()
     for copy in near_copies + forwards:
         copy.wait()
 
 
-def group_sum(mode, partial, *operands, collective):
+def sum_kernel(mode, n, cuts, *refs):
+    ctx, _, partner, others, _ = group_places(n)
+    greet([(ctx, partner)] + [(ctx, o) for o in others])
+    for _ in sum_phases(mode, n, cuts, *refs):
+        pass
+
+
+def sum_shapes(mode, partial):
     _, n, rows, width = partial.shape
-    cuts = 2
-    chunks = 2 * cuts
     chips = n // 2
     row_shape = (2, rows, width)
     full = jax.ShapeDtypeStruct(row_shape, F32)
@@ -368,27 +376,38 @@
         "input": (full, gain_sum),
     }[mode]
     dma = pltpu.SemaphoreType.DMA
+    chunks = 2 * SUM_CUTS
+    scratch = [
+        pltpu.VMEM((2, chips, rows, width), BF16),
+        pltpu.VMEM((2, chips - 1, rows, width), BF16),
+        pltpu.VMEM((2, chips - 1, rows, width), BF16),
+        pltpu.VMEM(row_shape, BF16),
+        dma((chunks, chips)),
+        dma((chunks, chips)),
+        dma((chunks, chips - 1)),
+        dma((chunks, chips - 1)),
+        dma((chunks,)),
+        dma((chunks,)),
+        dma((chunks, chips - 1)),
+        dma((chunks, chips - 1)),
+        dma((chunks, chips - 1)),
+        dma((chunks, chips - 1)),
+    ]
+    return out_shape, scratch
+
+
+SUM_CUTS = 2
+
+
+def group_sum(mode, partial, *operands, collective):
+    _, n, rows, width = partial.shape
+    out_shape, scratch = sum_shapes(mode, partial)
     return pl.pallas_call(
-        functools.partial(sum_kernel, mode, n, cuts),
+        functools.partial(sum_kernel, mode, n, SUM_CUTS),
         out_shape=out_shape,
         in_specs=in_vmem(1 + len(operands)),
         out_specs=tuple(in_vmem(len(out_shape))),
-        scratch_shapes=[
-            pltpu.VMEM((2, chips, rows, width), BF16),
-            pltpu.VMEM((2, chips - 1, rows, width), BF16),
-            pltpu.VMEM((2, chips - 1, rows, width), BF16),
-            pltpu.VMEM(row_shape, BF16),
-            dma((chunks, chips)),
-            dma((chunks, chips)),
-            dma((chunks, chips - 1)),
-            dma((chunks, chips - 1)),
-            dma((chunks,)),
-            dma((chunks,)),
-            dma((chunks, chips - 1)),
-            dma((chunks, chips - 1)),
-            dma((chunks, chips - 1)),
-            dma((chunks, chips - 1)),
-        ],
+        scratch_shapes=scratch,
         compiler_params=pltpu.CompilerParams(
             vmem_limit_bytes=VMEM_LIMIT, collective_id=collective, has_side_effects=True
         ),
@@ -540,69 +559,24 @@
     )(partial)
 
 
-def vector_kernel(n_ctx, n, parts, out, near, summed, far, near_s, near_r, far_s, far_r):
-    ctx = lax.axis_index("ctx")
-    me = lax.axis_index("fsdp")
-    members = [(me + k) % n for k in range(1, n)]
-    others = [(ctx + k) % n_ctx for k in range(1, n_ctx)]
-    greet([(ctx, m) for m in members] + [(o, me) for o in others])
-    first = []
-    for k in range(n - 1):
-        copy = remote(parts.at[members[k]], near.at[k], near_s.at[k], near_r.at[k], (ctx, members[k]))
-        copy.start()
-        first.append(copy)
-    total = parts[me]
-    for k in range(n - 1):
-        first[k].wait()
-        total += near[k]
-    summed[...] = total
-    second = []
-    for k in range(n_ctx - 1):
-        copy = remote(summed, far.at[k], far_s.at[k], far_r.at[k], (others[k], me))
-        copy.start()
-        second.append(copy)
-    for k in range(n_ctx - 1):
-        second[k].wait()
-        total += far[k]
-    out[...] = total
-
-
-def vector_sum(parts, n_ctx, collective):
-    n = parts.shape[0]
-    block = parts.shape[1:]
-    dma = pltpu.SemaphoreType.DMA
-    return pl.pallas_call(
-        functools.partial(vector_kernel, n_ctx, n),
-        out_shape=jax.ShapeDtypeStruct(block, F32),
-        in_specs=in_vmem(1),
-        out_specs=in_vmem(1)[0],
-        scratch_shapes=[
-            pltpu.VMEM((n - 1,) + block, F32),
-            pltpu.VMEM(block, F32),
-            pltpu.VMEM((n_ctx - 1,) + block, F32),
-            dma((n - 1,)),
-            dma((n - 1,)),
-            dma((n_ctx - 1,)),
-            dma((n_ctx - 1,)),
-        ],
-        compiler_params=pltpu.CompilerParams(
-            vmem_limit_bytes=VMEM_LIMIT, collective_id=collective, has_side_effects=True
-        ),
-        cost_estimate=pl.CostEstimate(flops=0, bytes_accessed=30_000_000, transcendentals=0),
-        name="vector_sum",
-    )(parts)
-
-
-def ring_sum_kernel(n, plan, arrays, *refs):
-    ins, outs = refs[:arrays], refs[arrays : 2 * arrays]
-    refs = refs[2 * arrays :]
+def ring_sum_kernel(n, members, plan, swaps, arrays, mode, extra_ins, extra_outs, *refs):
+    ins, refs = refs[:arrays], refs[arrays:]
+    side_ins, refs = refs[:extra_ins], refs[extra_ins:]
+    outs, refs = refs[:arrays], refs[arrays:]
+    side_outs, refs = refs[:extra_outs], refs[extra_outs:]
     count = len(plan)
     arrived, stages, sends, recvs = (refs[i * count : (i + 1) * count] for i in range(4))
+    refs = refs[4 * count :]
+    done, swap_s, swap_r = (refs[i * len(swaps) : (i + 1) * len(swaps)] for i in range(3))
+    refs = refs[3 * len(swaps) :]
     ctx = lax.axis_index("ctx")
     me = lax.axis_index("fsdp")
     place = ring_place(ctx, n)
     around = {step: (ring_index((place + n + step) % n, n), me) for step in (1, -1)}
-    greet([around[1], around[-1]])
+    greet([around[1], around[-1]] + [(ctx, (me + k) % members) for k in range(1, members)])
+    beside = iter(())
+    if mode:
+        beside = sum_phases(mode, members, SUM_CUTS, *side_ins, *side_outs, *refs)
 
     def copy(i, hop, src):
         step = plan[i][3]
@@ -616,8 +590,13 @@
         which, low, high, _ = plan[i]
         return ins[which][group, chunk(i, hop), :, low:high].astype(F32)
 
-    for i, (which, low, high, _) in enumerate(plan):
-        copy(i, 0, ins[which].at[:, chunk(i, 0), :, pl.ds(low, high - low)]).start()
+    def first(i):
+        which, low, high, _ = plan[i]
+        return copy(i, 0, ins[which].at[:, chunk(i, 0), :, pl.ds(low, high - low)])
+
+    for i in range(count):
+        first(i).start()
+    next(beside, None)
 
     def add(i, hop, store):
         copy(i, hop - 1, stages[i].at[0]).wait_recv()
@@ -644,90 +623,146 @@
         copy(count - 1, hop, stages[count - 1].at[slot]).start()
         return carry
 
-    lax.fori_loop(1, n - 1, one_hop, 0)
+    hop = 1
+    if mode:
+        for _ in range(min(4, n - 3)):
+            one_hop(jnp.int32(hop), 0)
+            hop += 1
+            next(beside, None)
+    lax.fori_loop(hop, n - 1, one_hop, 0)
     for i, (which, low, high, _) in enumerate(plan):
+        target = done[swaps.index(which)] if which in swaps else outs[which]
+
         def store(group, value):
-            outs[which][group, :, low:high] = value
+            target[group, :, low:high] = value
 
         add(i, n - 1, store)
-    for i, (which, low, high, _) in enumerate(plan):
-        copy(i, 0, ins[which].at[:, chunk(i, 0), :, pl.ds(low, high - low)]).wait_send()
+    swapped = []
+    for j, which in enumerate(swaps):
+        for k in range(1, members):
+            other = (me + k) % members
+            swapped.append(
+                remote(
+                    done[j].at[other],
+                    outs[which].at[me],
+                    swap_s[j].at[k - 1],
+                    swap_r[j].at[k - 1],
+                    (ctx, other),
+                )
+            )
+            swapped[-1].start()
+        outs[which][me] = done[j][me]
+    for _ in beside:
+        pass
+    for i in range(count):
+        first(i).wait_send()
         for hop in (n - 3, n - 2):
             copy(i, hop, stages[i].at[hop % 2]).wait_send()
-
-
-def ring_sum(arrays, plan, collective):
+    for move in swapped:
+        move.wait()
+
+
+def ring_sum(arrays, plan, swaps, members, collective, mode=None, operands=()):
     n = arrays[0].shape[1]
     dma = pltpu.SemaphoreType.DMA
     blocks = [
         (arrays[which].shape[0], arrays[which].shape[2], high - low) for which, low, high, _ in plan
     ]
+    sums = [(a.shape[0],) + a.shape[2:] for a in arrays]
+    extra_shape, extra_scratch = sum_shapes(mode, operands[0]) if mode else ((), [])
+    out_shape = tuple(jax.ShapeDtypeStruct(shape, BF16) for shape in sums) + tuple(extra_shape)
     return pl.pallas_call(
-        functools.partial(ring_sum_kernel, n, plan, len(arrays)),
-        out_shape=tuple(
-            jax.ShapeDtypeStruct((a.shape[0],) + a.shape[2:], BF16) for a in arrays
-        ),
-        in_specs=in_vmem(len(arrays)),
-        out_specs=tuple(in_vmem(len(arrays))),
+        functools.partial(
+            ring_sum_kernel, n, members, plan, swaps, len(arrays), mode, len(operands), len(extra_shape)
+        ),
+        out_shape=out_shape,
+        in_specs=in_vmem(len(arrays) + len(operands)),
+        out_specs=tuple(in_vmem(len(out_shape))),
         scratch_shapes=[pltpu.VMEM((n - 1,) + b, BF16) for b in blocks]
         + [pltpu.VMEM((2,) + b, BF16) for b in blocks]
-        + [dma((n - 1,)) for _ in blocks] * 2,
+        + [dma((n - 1,)) for _ in blocks] * 2
+        + [pltpu.VMEM(sums[which], BF16) for which in swaps]
+        + [dma((members - 1,)) for _ in swaps] * 2
+        + extra_scratch,
         compiler_params=pltpu.CompilerParams(
             vmem_limit_bytes=VMEM_LIMIT, collective_id=collective, has_side_effects=True
         ),
         cost_estimate=pl.CostEstimate(flops=0, bytes_accessed=200_000_000, transcendentals=0),
         name="ring_sum",
-    )(*arrays)
-
-
-def ring_gather_kernel(n, own, out, sends, recvs):
+    )(*arrays, *operands)
+
+
+def ring_gather_kernel(n, count, *refs):
+    owns, outs, sends, recvs = (refs[i * count : (i + 1) * count] for i in range(4))
     ctx = lax.axis_index("ctx")
     me = lax.axis_index("fsdp")
     place = ring_place(ctx, n)
     around = {step: (ring_index((place + n + step) % n, n), me) for step in (1, -1)}
     greet([around[1], around[-1]])
-    middle = own.shape[-1] // 2
     far = n // 2
 
-    def copy(step, half, hop):
+    def copy(i, step, half, hop):
+        middle = owns[i].shape[-1] // 2
         lanes = pl.ds(half * middle, middle)
-        block = out.at[ring_index((place + n - step * hop) % n, n), :, lanes]
-        src = block if hop else own.at[:, lanes]
+        block = outs[i].at[ring_index((place + n - step * hop) % n, n), :, lanes]
+        src = block if hop else owns[i].at[:, lanes]
         row = half if step == 1 else 2 + half
-        return remote(src, block, sends.at[row, hop], recvs.at[row, hop], around[step])
+        return remote(src, block, sends[i].at[row, hop], recvs[i].at[row, hop], around[step])
 
     def hops(step, half):
         return far if (step == 1) == (half == 0) else far - 1
 
-    lines = [(1, 0), (-1, 1), (1, 1), (-1, 0)]
-    for step, half in lines:
-        copy(step, half, 0).start()
-    out[ctx] = own[...]
+    lines = [(i, step, half) for step, half in ((1, 0), (-1, 1), (1, 1), (-1, 0)) for i in range(count)]
+    for i, step, half in lines:
+        copy(i, step, half, 0).start()
+    for own, out in zip(owns, outs):
+        out[ctx] = own[...]
     for hop in range(1, far + 1):
-        for step, half in lines:
+        for i, step, half in lines:
             if hop <= hops(step, half):
-                copy(step, half, hop - 1).wait_recv()
+                copy(i, step, half, hop - 1).wait_recv()
                 if hop < hops(step, half):
-                    copy(step, half, hop).start()
-    for step, half in lines:
+                    copy(i, step, half, hop).start()
+    for i, step, half in lines:
         for hop in range(hops(step, half)):
-            copy(step, half, hop).wait_send()
-
-
-def ring_gather(own, n, collective):
-    dma = pltpu.SemaphoreType.DMA
+            copy(i, step, half, hop).wait_send()
+
+
+def ring_gather(owns, n, collective):
+    count = len(owns)
     return pl.pallas_call(
-        functools.partial(ring_gather_kernel, n),
-        out_shape=jax.ShapeDtypeStruct((n,) + own.shape, BF16),
-        in_specs=in_vmem(1),
-        out_specs=in_vmem(1)[0],
-        scratch_shapes=[dma((4, n // 2))] * 2,
+        functools.partial(ring_gather_kernel, n, count),
+        out_shape=tuple(jax.ShapeDtypeStruct((n,) + own.shape, BF16) for own in owns),
+        in_specs=in_vmem(count),
+        out_specs=tuple(in_vmem(count)),
+        scratch_shapes=[pltpu.SemaphoreType.DMA((4, n // 2))] * (2 * count),
         compiler_params=pltpu.CompilerParams(
             vmem_limit_bytes=VMEM_LIMIT, collective_id=collective, has_side_effects=True
         ),
-        cost_estimate=pl.CostEstimate(flops=0, bytes_accessed=80_000_000, transcendentals=0),
+        cost_estimate=pl.CostEstimate(flops=0, bytes_accessed=120_000_000, transcendentals=0),
         name="ring_gather",
-    )(own)
+    )(*owns)
+
+
+def weave_kernel(planes, out):
+    for e in range(2):
+        out[:, e, :] = planes[e].astype(F32)
+
+
+def weave(planes):
+    _, rows, lanes = planes.shape
+    block = 32 if rows % 32 == 0 else rows
+    return pl.pallas_call(
+        weave_kernel,
+        grid=(rows // block,),
+        out_shape=jax.ShapeDtypeStruct((rows, 2, lanes), F32),
+        in_specs=[pl.BlockSpec((2, block, lanes), lambda i: (0, i, 0))],
+        out_specs=pl.BlockSpec((block, 2, lanes), lambda i: (i, 0, 0)),
+        cost_estimate=pl.CostEstimate(
+            flops=0, bytes_accessed=12 * rows * lanes, transcendentals=0
+        ),
+        name="weave",
+    )(planes)
 
 
 def exchange(pieces, axis):
@@ -835,9 +870,12 @@
         collective=1,
     )
     normed2 = normed2.reshape(rows, D)
-    w_gate_cols, w_up_cols = (gate_up_cols[:, e].reshape(D, ff_shard) for e in range(2))
-    gate_val = jnp.dot(normed2, w_gate_cols, preferred_element_type=F32)
-    up_val = jnp.dot(normed2, w_up_cols, preferred_element_type=F32)
+    w_gate_cols, w_up_cols = (gate_up_cols[:, e] for e in range(2))
+    normed2_parts = normed2.reshape(rows, n_fsdp, d_shard)
+    gate_val, up_val = (
+        jnp.einsum("tsk,skf->tf", normed2_parts, w, preferred_element_type=F32)
+        for w in (w_gate_cols, w_up_cols)
+    )
     sigmoid_gate = jax.nn.sigmoid(gate_val)
     act16 = (jax.nn.silu(gate_val) * up_val).astype(BF16)
     result = hidden.reshape(local_count, D) + scatter(jnp.dot(act16, w_down, preferred_element_type=F32))
@@ -846,7 +884,10 @@
     d_act = contract_cols(cot_all, w_down)
     d_gate16 = (d_act * up_val * sigmoid_gate * (1.0 + gate_val * (1.0 - sigmoid_gate))).astype(BF16)
     d_up16 = (d_act * gate_val * sigmoid_gate).astype(BF16)
-    d_normed2 = contract_cols(d_gate16, w_gate_cols) + contract_cols(d_up16, w_up_cols)
+    d_normed2 = sum(
+        jnp.einsum("tf,skf->tsk", d, w, preferred_element_type=F32)
+        for d, w in ((d_gate16, w_gate_cols), (d_up16, w_up_cols))
+    )
     def by_columns(pieces):
         queries = [pieces[f][..., :q_cols] for f in range(n_fsdp)]
         rest = []
@@ -876,19 +917,22 @@
         for piece in (d_gate16, d_up16)
     )
 
-    gate_sum, up_sum, down_sum = ring_sum(
+    gate_sum, up_sum, down_sum, d_hidden, dh_all, d_gain_two = ring_sum(
         (d_w_gate, d_w_up, d_w_down[None]),
         ((0, 0, ff_shard, 1), (1, 0, ff_shard, -1), (2, 0, side, 1), (2, side, D, -1)),
+        (0, 1),
+        n_fsdp,
         7,
-    )
-    d_normed2, gate_sum, up_sum, down_sum = together(by_member(d_normed2), gate_sum, up_sum, down_sum)
-    gate_up_sum = exchange(jnp.stack([gate_sum, up_sum], 1), "fsdp")
-    gate_up_sum = gate_up_sum.transpose(2, 1, 0, 3).reshape(chunk_rows, 2, n_fsdp * ff_shard)
-    d_w_gate_up = lax.all_gather(gate_up_sum, "ctx", axis=0, tiled=True).astype(F32)
-    d_w_down = lax.all_gather(down_sum[0], "ctx", axis=0, tiled=True)[:ff_shard].astype(F32)
-    d_hidden, dh_all, d_gain_two = group_sum(
-        "mlp", d_normed2, hidden, cotangent[0], gain_two[None], collective=2
-    )
+        "mlp",
+        (by_member(d_normed2), hidden, cotangent[0], gain_two[None]),
+    )
+    planes = jnp.stack(
+        [
+            total.transpose(1, 0, 2).reshape(chunk_rows, n_fsdp * ff_shard)
+            for total in (gate_sum, up_sum)
+        ]
+    )
+    d_w_gate_up = weave(lax.all_gather(planes, "ctx", axis=1, tiled=True))
     dh_all = dh_all.reshape(rows, D)
     d_attended16 = contract_cols(dh_all, w_out).astype(BF16).reshape(2, stretch_len, q_cols)
     d_query, d_kv = attend_back(
@@ -918,23 +962,40 @@
     zeros = jnp.zeros_like(d_bias)
     d_bias_full = by_columns([jnp.where(fsdp_index == f, d_bias, zeros) for f in range(n_fsdp)])
     parts = jnp.concatenate(
-        [v.reshape(n_fsdp, -1, HEAD_DIM) for v in (d_gain_one, d_gain_two, d_bias_full)], 1
-    )
-    parts = jnp.pad(parts, ((0, 0), (0, -parts.shape[1] % 8), (0, 0)))
-    vector = vector_sum(parts, n_ctx, 6)
+        [v.reshape(n_fsdp, -1) for v in (d_gain_one, d_gain_two, d_bias_full)], 1
+    ).astype(BF16)
+    length = parts.shape[1]
+    few = 2 * HEAD_DIM
+    vector_rows = -(-length // (n_ctx * few))
+    parts = jnp.pad(parts, ((0, 0), (0, n_ctx * vector_rows * few - length)))
+    parts = parts.reshape(n_fsdp, n_ctx, vector_rows, few)
+    parts = jnp.pad(parts, ((0, 0), (0, 0), (0, -vector_rows % 16), (0, 0)))
     d_w_qkv = contract_rows(normed1, d_qkv16).astype(BF16).reshape(n_fsdp, n_ctx, chunk_rows, -1)
-    vector = vector.reshape(-1)
-    pieces, out_sum = ring_sum(
-        (d_w_qkv, d_w_out[None]),
-        ((0, 0, q_cols, 1), (0, q_cols, d_w_qkv.shape[-1], -1), (1, 0, side, 1), (1, side, D, -1)),
+    pieces, out_sum, vector = ring_sum(
+        (d_w_qkv, d_w_out[None], parts),
+        (
+            (0, 0, q_cols, 1),
+            (0, q_cols, d_w_qkv.shape[-1], -1),
+            (1, 0, side, 1),
+            (1, side, D, -1),
+            (2, 0, few, 1),
+        ),
+        (0, 2),
+        n_fsdp,
         8,
     )
-    d_w_pieces = exchange(pieces, "fsdp")
-    qkv_sum = by_columns([d_w_pieces[f] for f in range(n_fsdp)])
-    attention_sum = ring_gather(jnp.concatenate([qkv_sum, out_sum[0]], -1), n_ctx, 9)
-    attention_sum = attention_sum.reshape(d_shard, -1).astype(F32)
-    d_w_qkv, d_w_out = attention_sum[:, :-D], attention_sum[:, -D:]
-
+    qkv_sum = by_columns([pieces[f] for f in range(n_fsdp)])
+    vector = jnp.sum(vector.astype(F32), 0)[:vector_rows].astype(BF16)
+    vector = jnp.pad(vector, ((0, chunk_rows - vector_rows), (0, 0)))
+    attention_sum, d_w_down = ring_gather(
+        (jnp.concatenate([qkv_sum, out_sum[0], vector], -1), down_sum[0]), n_ctx, 9
+    )
+    d_w_down = d_w_down.reshape(n_ctx * down_rows, D)[:ff_shard].astype(F32)
+    vector = attention_sum[:, :vector_rows, -few:].astype(F32).reshape(-1)
+    attention_sum = attention_sum.reshape(d_shard, -1)
+    qkv_width = qkv_sum.shape[-1]
+    d_w_qkv = attention_sum[:, :qkv_width].astype(F32)
+    d_w_out = attention_sum[:, qkv_width : qkv_width + D].astype(F32)
     d_gain_attn = vector[:d_shard]
     d_gain_mlp = vector[d_shard : 2 * d_shard]
     d_b_qkv = vector[2 * d_shard : 2 * d_shard + b_qkv.shape[0]]

time: 679 us -> 632 us (0.931)
  local copies, waits for them, and re-layouts: 118 us -> 72.5 us
  blocking collectives: 21.5 us -> 6.27 us
  Pallas kernels: 400 us -> 415 us
    unnamed x74 -> x69, local copies, waits for them, and re-layouts: 43.7 us -> 11.5 us
    slice x5, local copies, waits for them, and re-layouts: 21.4 us -> 0.02 us  [the longest x4 0.01 us: by_columns(): queries = [pieces[f][..., :q_cols] for f in range(n_fsdp)]]
    pallas_call x7 -> x6, Pallas kernels: 310 us -> 326 us  [the longest x2 192 us: ring_sum(): pl.pallas_call(functools.partial(ring_sum_kernel, n, members, plan, swaps...]
    all_to_all x1 -> x0, blocking collectives: 15.2 us -> none  [exchange(): return lax.all_to_all(pieces, axis, split_axis=0, concat_axis=0, tiled=True)]
    dot_general x2 -> x4, matrix products: 9.37 us -> 20.4 us  [the longest x2 11.3 us: body(): jnp.einsum('tsk,skf->tf', normed2_parts, w, preferred_element_type=F32)]
    dot_general x10 -> x8, matrix products: 40 us -> 32.3 us  [dot(): lax.dot_general(left, right, (contract, ((), ())), preferred_element_type...]
    all_to_all x3 -> x2, waiting for transfers between devices: 14.4 us -> 9.76 us  [exchange(): return lax.all_to_all(pieces, axis, split_axis=0, concat_axis=0, tiled=True)]
  transfers between devices with their start and end apart: 8 -> 6, of which waited for: 2 -> 1; matrix products, arithmetic and copies ran while one was open for 22% -> 23% of each run, Pallas kernels for 60% -> 65%
where the time goes in v4:
time: 632 us; the launch traced here: 623 us
  Pallas kernels  415 us (66%)
  local copies, waits for them, and re-layouts  72.5 us (11%)
  matrix products  62.7 us (10%)
  other arithmetic  29.9 us (5%)
  between operations  15.4 us (2%)
  waiting for transfers between devices  11.2 us (2%)
  starting transfers between devices  10.3 us (2%)
    pallas_call x2, Pallas kernels, ring_sum(): pl.pallas_call(functools.partial(ring_sum_kernel, n, members, plan, swaps...  192 us
    pallas_call x1, Pallas kernels, ring_gather(): pl.pallas_call(functools.partial(ring_gather_kernel, n, count), out_shape...  68.8 us
    pallas_call x2, Pallas kernels, group_sum(): pl.pallas_call(functools.partial(sum_kernel, mode, n, SUM_CUTS), out_shap...  53.3 us
    pallas_call x1, Pallas kernels, return_grads(): pl.pallas_call(functools.partial(return_kernel, n), out_shape=jax.ShapeDt...  35.6 us
    dot_general x8, matrix products, dot(): lax.dot_general(left, right, (contract, ((), ())), preferred_element_type...  32.3 us
    optimization_barrier x2, local copies, waits for them, and re-layouts, together(): return lax.optimization_barrier(values)  24.6 us
    pallas_call x1, Pallas kernels, share_keys(): pl.pallas_call(functools.partial(share_kernel, n), out_shape=jax.ShapeDty...  23.1 us
    pallas_call x1, Pallas kernels, attend_back(): pl.pallas_call(functools.partial(attend_back_kernel, heads), out_shape=(j...  16.1 us
  transfers between devices with their start and end apart: 6, of which 1 were waited for; matrix products, arithmetic and copies ran while one was open for 23% of the time, Pallas kernels for 65%

profile of v4, /device:TPU:0, one launch (start us, length us, event | category | flops | bytes accessed | tf_op | source)
XLA Modules:
  0.0 622.9 jit_solution(13519072241195882362)
XLA Ops:
  7.9 1.0 pad_maximum_fusion.15
  8.9 6.3 %all-gather.3 = bf16[4,1,1280]{2,1,0:T(2,128)(2,1)S(1)} all-gather(bf16[1,1,1280]{2,1,0:T(2,128)(2,1)S(1)} %reshape.294), channel_id=3, replica_groups=mesh['ctx'=8,'fsdp'=4] {'fsdp'}, dimensions={0}, use_global_device_ids=true | all-gather | bytes 12800 | tf_op jit(solution)/shard_map/all_gather | solution.py:805
  15.2 1.1 fusion.35
  16.3 1.4 fusion.34
  17.8 1.6 pad_maximum_fusion
  19.4 4.4 all-to-all-start
  23.9 18.0 %copy.105 = bf16[384,2,4480]{0,2,1:T(8,128)(2,1)} copy(bf16[384,2,4480]{2,1,0:T(2,128)(2,1)} %param.17) | data formatting | bytes 13762560 | tf_op jit(solution)/shard_map/optimization_barrier | solution.py:773
  41.9 9.8 %all-to-all-done = bf16[4,384,640]{2,1,0:T(8,128)(2,1)} async-done(((bf16[4,384,640]{2,1,0:T(8,128)(2,1)}), bf16[4,384,640]{2,1,0:T(8,128)(2,1)}, u32[]{:S(2)}, u32[]{:S(2)}) %all-to-all-start) | async-done | bytes 1966112 | tf_op jit(solution)/shard_map/all_to_all | solution.py:769
  51.6 6.5 %copy.110 = bf16[4,2,384,1120]{2,3,1,0:T(8,128)(2,1)} copy(bf16[4,2,384,1120]{2,3,0,1:T(8,128)(2,1)} %bitcast.119) | data formatting | bytes 13762560 | tf_op jit(solution)/shard_map/optimization_barrier | solution.py:773
  58.2 5.6 all-to-all-start.1
  66.1 1.2 broadcast_multiply_fusion
  68.8 1.8 multiply_cosine_fusion
  70.6 1.8 fusion
  72.4 3.1 convolution_add_fusion
  75.5 1.0 copy-done.13
  76.5 1.1 slice.250
  77.6 2.5 reshape.257
  80.2 2.3 fusion.37
  82.5 1.6 slice.329
  85.4 1.1 copy.128
  86.5 2.0 reshape.302.q_ref
  88.6 1.1 pad_maximum_fusion.14
  89.7 1.6 pad_maximum_fusion.13.own
  91.3 23.1 %share_keys.1 = bf16[8,2,256,256]{3,2,1,0:T(8,128)(2,1)} custom-call(bf16[2,256,256]{2,1,0:T(8,128)(2,1)} %pad_maximum_fusion.13.own), custom_call_target="tpu_custom_call" | custom-call | bytes 60000000 | tf_op jit(solution)/shard_map/share_keys/pallas_call | solution.py:488
  114.4 13.6 %attend.1 = (bf16[2,256,384]{2,1,0:T(8,128)(2,1)}, f32[2,1,768]{2,1,0:T(1,128)}) custom-call(s32[16]{0:T(128)} %pad_add_fusion.table, s32[2]{0:T(128)} %get-tuple-element.68.ids, bf16[2,256,384]{2,1,0:T(8,128)(2,1)} %reshape.302.q_ref, bf16[4096,256]{1,0:T(8,128)(2,1)} %bitcast.135), custom_call_target="tpu_custom_call" | custom-call | flops 1610612736 | bytes 2097152 | tf_op jit(solution)/shard_map/attend/pallas_call | solution.py:169
  128.0 3.5 convolution_convert_fusion.6
  131.5 37.2 %group_sum_attention.1 = (f32[2,64,1536]{2,1,0:T(8,128)}, bf16[2,4,64,1536]{3,2,1,0:T(8,128)(2,1)}) custom-call(bf16[2,4,64,1536]{3,2,1,0:T(8,128)(2,1)} %bitcast.123, bf16[2,64,1536]{2,1,0:T(8,128)(2,1)} %bitcast.128, f32[1,1536]{1,0:T(1,128)} %bitcast.156), custom_call_target="tpu_custom_call" | custom-call | flops 1966080 | bytes 60000000 | tf_op jit(solution)/shard_map/group_sum_attention/pallas_call | solution.py:405
  168.7 3.9 reshape_reshape.3
  172.6 5.9 convolution_bitcast_fusion.1
  178.6 5.4 convolution_bitcast_fusion
  183.9 7.1 %multiply_convert_fusion = (bf16[512,1120]{0,1:T(8,128)(2,1)}, bf16[512,1120]{0,1:T(8,128)(2,1)}, bf16[512,1120]{0,1:T(8,128)(2,1)S(1)}) fusion(f32[512,1120]{0,1:T(8,128)} %convolution_bitcast_fusion.1, f32[512,1120]{0,1:T(8,128)} %convolution_bitcast_fusion, bf16[512,1536]{1,0:T(8,128)(2,1)} %bitcast.166, bf16[1120,1536]{1,0:T(8,128)(2,1)S(1)} %copy-done), kind=kOutput, calls=%fused_computation.21 | convolution fusion | flops 1770782720 | bytes 13041664 | tf_op jit(solution)/shard_map/dot_general | solution.py:55
  191.1 3.4 convolution_convert_fusion.5
  194.7 3.7 convolution_convert_fusion.1
  198.4 3.7 copy.115
  202.1 3.8 convolution_convert_fusion
  205.9 3.7 copy.116
  209.5 4.9 fusion.3
  214.5 4.2 add_convert_fusion
  218.7 1.2 copy.117
  219.9 1.5 reshape.267.refs_3_
  221.4 3.7 convolution_convert_fusion.2
  225.1 2.1 pad.17
  227.3 119.5 %ring_sum.2 = (bf16[4,48,1120]{2,1,0:T(8,128)(2,1)}, bf16[4,48,1120]{2,1,0:T(8,128)(2,1)}, bf16[1,144,1536]{2,1,0:T(8,128)(2,1)}, f32[2,64,1536]{2,1,0:T(8,128)}...) custom-call(bf16[4,8,48,1120]{3,2,1,0:T(8,128)(2,1)} %bitcast.120, bf16[4,8,48,1120]{3,2,1,0:T(8,128)(2,1)} %bitcast.121, ...), custom_call_target="tpu_custom_call" | custom-call | bytes 200000000 | tf_op jit(solution)/shard_map/ring_sum/pallas_call | solution.py:674
  346.8 1.2 copy.127
  348.9 1.0 pad_maximum_fusion.4
  350.6 3.1 convolution_convert_fusion.8
  353.7 16.1 %attend_back.1 = (f32[2,256,384]{2,1,0:T(8,128)}, bf16[4096,256]{1,0:T(8,128)(2,1)}) custom-call(s32[16]{0:T(128)} %pad_add_fusion.table, s32[2]{0:T(128)} %get-tuple-element.68.ids, bf16[2,256,384]{2,1,0:T(8,128)(2,1)} %reshape.302.q_ref, bf16[4096,256]{1,0:T(8,128)(2,1)} %bitcast.136, bf16[2,256,384]{2,1,0:T(8,128)(2,1)} %get-tuple-element.39.o_ref, ...), custom_call_target="tpu_custom_call" | custom-call | flops 4026531840 | bytes 4194304 | tf_op jit(solution)/shard_map/attend_back/pallas_call | solution.py:190
  369.8 35.6 %return_grads.1 = f32[2,256,256]{2,1,0:T(8,128)} custom-call(bf16[8,2,256,256]{3,2,1,0:T(8,128)(2,1)} %bitcast.133), custom_call_target="tpu_custom_call" | custom-call | bytes 80000000 | tf_op jit(solution)/shard_map/return_grads/pallas_call | solution.py:540
  405.4 1.1 fusion.38
  408.3 1.3 copy.136
  409.6 1.5 multiply_add_fusion
  412.0 4.5 convolution_convert_fusion.4
  416.6 16.2 %group_sum_input.1 = (f32[2,64,1536]{2,1,0:T(8,128)}, f32[1,1536]{1,0:T(1,128)}) custom-call(bf16[2,4,64,1536]{3,2,1,0:T(8,128)(2,1)} %bitcast.144, bf16[2,64,1536]{2,1,0:T(8,128)(2,1)} %bitcast.129, f32[2,64,1536]{2,1,0:T(8,128)} %get-tuple-element.47.refs_2_, f32[1,1536]{1,0:T(1,128)} %bitcast.161), custom_call_target="tpu_custom_call" | custom-call | flops 1966080 | bytes 60000000 | tf_op jit(solution)/shard_map/group_sum_input/pallas_call | solution.py:405
  436.6 3.3 convolution_convert_fusion.7
  439.9 2.9 convolution_convert_fusion.3
  442.8 72.6 %ring_sum.3 = (bf16[4,48,640]{2,1,0:T(8,128)(2,1)}, bf16[1,48,1536]{2,1,0:T(8,128)(2,1)}, bf16[4,16,256]{2,1,0:T(8,128)(2,1)}) custom-call(bf16[4,8,48,640]{3,2,1,0:T(8,128)(2,1)} %bitcast.137, bf16[1,8,48,1536]{3,2,1,0:T(8,128)(2,1)} %bitcast.146, bf16[4,8,16,256]{3,2,1,0:T(8,128)(2,1)} %pad.19.refs_2_), custom_call_target="tpu_custom_call" | custom-call | bytes 200000000 | tf_op jit(solution)/shard_map/ring_sum/pallas_call | solution.py:674
  516.2 0.9 slice_bitcast_fusion.8
  518.9 68.8 %ring_gather.1 = (bf16[8,48,3840]{2,1,0:T(8,128)(2,1)}, bf16[8,144,1536]{2,1,0:T(8,128)(2,1)}) custom-call(bf16[48,3840]{1,0:T(8,128)(2,1)} %copy-done.16, bf16[144,1536]{1,0:T(8,128)(2,1)} %bitcast.151), custom_call_target="tpu_custom_call" | custom-call | bytes 120000000 | tf_op jit(solution)/shard_map/ring_gather/pallas_call | solution.py:733
  589.7 3.4 slice_convert_fusion.1
  593.1 3.1 slice_convert_fusion.2
  596.2 3.8 slice_convert_fusion
  600.1 1.8 fusion.18
  601.9 12.0 %weave.1 = f32[384,2,4480]{2,1,0:T(2,128)} custom-call(bf16[2,384,4480]{2,1,0:T(8,128)(2,1)} %all-gather.8.cloned.1.call-done.planes), custom_call_target="tpu_custom_call" | custom-call | bytes 20643840 | tf_op jit(solution)/shard_map/weave/pallas_call | solution.py:755
  613.9 2.1 copy.171
  (132 shorter events, 17.8 us)
Async XLA Ops:
  7.2 176.8 %copy-start = (bf16[1120,1536]{1,0:T(8,128)(2,1)S(1)}, bf16[1120,1536]{1,0:T(8,128)(2,1)}, u32[]{:S(2)}) copy-start(bf16[1120,1536]{1,0:T(8,128)(2,1)} %param.18) | copy-start | bytes 10321924
  7.2 44.4 %all-gather.10.cloned.1.call-start = ((), (), s32[]{:S(2)}) async-start(), calls=%async_computation.5 | async-start | bytes 1966080 | tf_op jit(solution)/shard_map/all_gather | solution.py:810
  19.4 32.2 %all-to-all-start = ((bf16[4,384,640]{2,1,0:T(8,128)(2,1)}), bf16[4,384,640]{2,1,0:T(8,128)(2,1)}, u32[]{:S(2)}, u32[]{:S(2)}) async-start(bf16[4,384,640]{2,1,0:T(8,128)(2,1)} %pad_maximum_fusion), calls=%async_computation | async-start | bytes 3932160 | tf_op jit(solution)/shard_map/all_to_all | solution.py:769
  58.2 6.4 %copy-start.20 = (s32[8]{0:T(128)S(1)}, s32[8]{0:T(128)}, u32[]{:S(2)}) copy-start(s32[8]{0:T(128)} %param.11) | copy-start | bytes 100
  58.2 114.5 %all-to-all-start.1 = ((bf16[4,2,384,1120]{2,3,1,0:T(8,128)(2,1)}), bf16[4,2,384,1120]{2,3,1,0:T(8,128)(2,1)}, u32[]{:S(2)}, u32[]{:S(2)}) async-start(bf16[4,2,384,1120]{2,3,1,0:T(8,128)(2,1)} %copy.110), calls=%async_computation.1 | async-start | bytes 13762560 | tf_op jit(solution)/shard_map/all_to_all | solution.py:769
  63.7 120.2 %all-gather.12.cloned.1.call-start = ((), (), s32[]{:S(2)}) async-start(), calls=%async_computation.6 | async-start | bytes 1966080 | tf_op jit(solution)/shard_map/all_gather | solution.py:840
  64.5 535.6 %reduce-scatter.2.cloned.1.call-start = ((), (), s32[]{:S(2)}) async-start(), calls=%async_computation.3 | async-start | bytes 1966080 | tf_op jit(solution)/shard_map/reduce_scatter | solution.py:857
  68.0 4.4 copy-start.9
  75.4 1.1 copy-start.13
  80.2 3.9 copy-start.6
  80.2 3.9 copy-start.8
  84.4 0.8 copy-start.2
  84.4 1.0 copy-start.3
  172.6 5.9 copy-start.11
  191.0 3.4 copy-start.21
  194.5 407.4 %all-gather.8.cloned.1.call-start = ((), (), s32[]{:S(2)}) async-start(), calls=%async_computation.4 | async-start | bytes 7741440 | tf_op jit(solution)/shard_map/all_gather | solution.py:935
  209.5 4.9 copy-start.22
  346.8 1.6 copy-start.17
  348.4 2.2 copy-start.12
  369.8 37.7 %copy-start.15 = (f32[2,256,384]{2,1,0:T(8,128)S(1)}, f32[2,256,384]{2,1,0:T(8,128)}, u32[]{:S(2)}) copy-start(f32[2,256,384]{2,1,0:T(8,128)} %get-tuple-element.45) | copy-start | bytes 2359300
  407.9 1.7 copy-start.7
  411.1 1.0 copy-start.14
  416.6 18.4 %copy-start.19 = (f32[1,1536]{1,0:T(1,128)S(1)}, f32[1,1536]{1,0:T(1,128)}, u32[]{:S(2)}) copy-start(f32[1,1536]{1,0:T(1,128)} %get-tuple-element.50) | copy-start | bytes 18436
  416.6 20.0 %copy-start.18 = (bf16[2,256,384]{2,1,0:T(8,128)(2,1)S(1)}, bf16[2,256,384]{2,1,0:T(8,128)(2,1)}, u32[]{:S(2)}) copy-start(bf16[2,256,384]{2,1,0:T(8,128)(2,1)} %get-tuple-element.39.o_ref) | copy-start | bytes 1179652
  436.6 3.3 copy-start.10
  518.2 0.7 copy-start.16
  593.1 3.1 copy-start.4
  596.2 3.9 copy-start.5
  601.9 14.1 %copy-start.1 = (bf16[1120,1536]{1,0:T(8,128)(2,1)S(1)}, bf16[1120,1536]{1,0:T(8,128)(2,1)}, u32[]{:S(2)}) copy-start(bf16[1120,1536]{1,0:T(8,128)(2,1)} %param.18) | copy-start | bytes 10321924
Sparse Core Ops, SparseCore 0:
  9.6 25.7 all-gather.9
  66.1 29.5 all-gather.11
  194.6 28.0 reduce-scatter.1
  350.1 137.2 all-gather.7

commit v5 on v4

--- a/solution.py
+++ b/solution.py
@@ -4,6 +4,7 @@
 import jax.numpy as jnp
 from jax import lax
 from jax.experimental import pallas as pl
+from jax.experimental.layout import Layout, with_layout_constraint
 from jax.experimental.pallas import tpu as pltpu
 from jax.sharding import PartitionSpec as P
 
@@ -765,6 +766,55 @@
     )(planes)
 
 
+def project_kernel(heads, x_ref, gain, w_ref, bias, cos_ref, sin_ref, normed_ref, q_ref, kv_ref):
+    values = x_ref[...].astype(F32)
+    normed = (values * rms_scale(values) * gain[...]).astype(BF16)
+    normed_ref[...] = normed
+    qkv = jnp.dot(normed, w_ref[...], preferred_element_type=F32) + bias[...]
+    cosines, sines = cos_ref[...], sin_ref[...]
+    for h in range(heads + 1):
+        vector = qkv[:, h * HEAD_DIM : (h + 1) * HEAD_DIM]
+        turned = vector * cosines + pltpu.roll(vector, HEAD_DIM // 2, 1) * sines
+        if h < heads:
+            q_ref[:, h * HEAD_DIM : (h + 1) * HEAD_DIM] = turned.astype(BF16)
+        else:
+            kv_ref[:, :HEAD_DIM] = turned.astype(BF16)
+    kv_ref[:, HEAD_DIM:] = qkv[:, (heads + 1) * HEAD_DIM :].astype(BF16)
+
+
+def project(x_all, gain, weights, bias, cosines, sines, heads):
+    rows = x_all.shape[0]
+    block = 128
+    width = weights.shape[1]
+
+    def tall(lanes):
+        return pl.BlockSpec((block, lanes), lambda i: (i, 0))
+
+    def fixed(shape):
+        return pl.BlockSpec(shape, lambda i: (0, 0))
+
+    lanes = (D, heads * HEAD_DIM, 2 * HEAD_DIM)
+    return pl.pallas_call(
+        functools.partial(project_kernel, heads),
+        grid=(rows // block,),
+        out_shape=tuple(jax.ShapeDtypeStruct((rows, n), BF16) for n in lanes),
+        in_specs=[
+            tall(D),
+            fixed((1, D)),
+            fixed((D, width)),
+            fixed((1, width)),
+            tall(HEAD_DIM),
+            tall(HEAD_DIM),
+        ],
+        out_specs=tuple(tall(n) for n in lanes),
+        compiler_params=pltpu.CompilerParams(vmem_limit_bytes=VMEM_LIMIT),
+        cost_estimate=pl.CostEstimate(
+            flops=2 * rows * D * width, bytes_accessed=4 * rows * D + 2 * D * width, transcendentals=0
+        ),
+        name="project",
+    )(x_all, gain, weights, bias, cosines, sines)
+
+
 def exchange(pieces, axis):
     return lax.all_to_all(pieces, axis, split_axis=0, concat_axis=0, tiled=True)
 
@@ -834,20 +884,22 @@
             lax.dynamic_slice_in_dim(bias, q_width + kv_width + my_kv * HEAD_DIM, HEAD_DIM),
         ]
     )
-    gate_up_pieces = w_gate_up.reshape(d_shard, 2, n_fsdp, ff_shard).transpose(2, 1, 0, 3)
+    gate_up_pieces = w_gate_up.reshape(d_shard, 2, n_fsdp, ff_shard).transpose(2, 1, 3, 0)
+    gate_up_pieces = with_layout_constraint(gate_up_pieces, Layout((0, 1, 2, 3)))
     x_all, w_qkv_cols, gate_up_pieces = together(x_all, w_qkv_cols, gate_up_pieces)
     gate_up_cols = exchange(gate_up_pieces, "fsdp")
-    cot_all = lax.all_gather(cotangent[0], "fsdp", axis=1, tiled=True).reshape(rows, D)
-
-    x32 = x_all.astype(F32)
-    normed1 = (x32 * rms_scale(x32) * gain_one).astype(BF16)
-    qkv = jnp.dot(normed1, w_qkv_cols, preferred_element_type=F32) + bias_cols
+
     cosines, sines = rope_tables(position)
-    rotated = rotate(
-        qkv[:, : q_cols + HEAD_DIM].reshape(rows, heads + 1, HEAD_DIM), cosines, sines
-    ).astype(BF16)
-    query = rotated[:, :heads].reshape(2, stretch_len, q_cols)
-    own_kv = jnp.concatenate([rotated[:, heads], qkv[:, q_cols + HEAD_DIM :].astype(BF16)], 1)
+    normed1, query, own_kv = project(
+        x_all,
+        gain_one[None],
+        w_qkv_cols,
+        bias_cols[None],
+        jnp.concatenate([cosines[:, 0], cosines[:, 0]], 1),
+        jnp.concatenate([-sines[:, 0], sines[:, 0]], 1),
+        heads,
+    )
+    query = query.reshape(2, stretch_len, q_cols)
     keys_values = share_keys(own_kv.reshape(2, stretch_len, 2 * HEAD_DIM), n_ctx, 4)
     keys_values = keys_values.reshape(n_ctx * rows, 2 * HEAD_DIM)
     attended, lse = attend(table, ids, query, keys_values, heads)
@@ -869,11 +921,13 @@
         gain_two[None],
         collective=1,
     )
+    normed2, cot_own = together(normed2, cotangent[0])
     normed2 = normed2.reshape(rows, D)
+    cot_all = lax.all_gather(cot_own, "fsdp", axis=1, tiled=True).reshape(rows, D)
     w_gate_cols, w_up_cols = (gate_up_cols[:, e] for e in range(2))
     normed2_parts = normed2.reshape(rows, n_fsdp, d_shard)
     gate_val, up_val = (
-        jnp.einsum("tsk,skf->tf", normed2_parts, w, preferred_element_type=F32)
+        jnp.einsum("tsk,sfk->tf", normed2_parts, w, preferred_element_type=F32)
         for w in (w_gate_cols, w_up_cols)
     )
     sigmoid_gate = jax.nn.sigmoid(gate_val)
@@ -885,7 +939,7 @@
     d_gate16 = (d_act * up_val * sigmoid_gate * (1.0 + gate_val * (1.0 - sigmoid_gate))).astype(BF16)
     d_up16 = (d_act * gate_val * sigmoid_gate).astype(BF16)
     d_normed2 = sum(
-        jnp.einsum("tf,skf->tsk", d, w, preferred_element_type=F32)
+        jnp.einsum("tf,sfk->tsk", d, w, preferred_element_type=F32)
         for d, w in ((d_gate16, w_gate_cols), (d_up16, w_up_cols))
     )
     def by_columns(pieces):
@@ -948,17 +1002,9 @@
     d_qkv = jnp.concatenate([d_rotated, d_kv_own[:, HEAD_DIM:]], 1)
     d_bias = jnp.sum(d_qkv, 0)
     d_qkv16 = d_qkv.astype(BF16)
-    d_normed1 = by_member(contract_cols(d_qkv16, w_qkv_cols))
-    d_tokens, d_gain_one = group_sum(
-        "input",
-        d_normed1,
-        tokens_own,
-        d_hidden,
-        gain_one[None],
-        collective=3,
-    )
-    d_tokens = d_tokens.reshape(tokens.shape)
-
+    d_normed1 = contract_cols(d_qkv16, w_qkv_cols)
+    x32 = x_all.astype(F32)
+    d_gain_one = jnp.sum(d_normed1 * x32 * rms_scale(x32), 0)
     zeros = jnp.zeros_like(d_bias)
     d_bias_full = by_columns([jnp.where(fsdp_index == f, d_bias, zeros) for f in range(n_fsdp)])
     parts = jnp.concatenate(
@@ -971,7 +1017,7 @@
     parts = parts.reshape(n_fsdp, n_ctx, vector_rows, few)
     parts = jnp.pad(parts, ((0, 0), (0, 0), (0, -vector_rows % 16), (0, 0)))
     d_w_qkv = contract_rows(normed1, d_qkv16).astype(BF16).reshape(n_fsdp, n_ctx, chunk_rows, -1)
-    pieces, out_sum, vector = ring_sum(
+    pieces, out_sum, vector, d_tokens, _ = ring_sum(
         (d_w_qkv, d_w_out[None], parts),
         (
             (0, 0, q_cols, 1),
@@ -983,7 +1029,10 @@
         (0, 2),
         n_fsdp,
         8,
-    )
+        "input",
+        (by_member(d_normed1), tokens_own, d_hidden, gain_one[None]),
+    )
+    d_tokens = d_tokens.reshape(tokens.shape)
     qkv_sum = by_columns([pieces[f] for f in range(n_fsdp)])
     vector = jnp.sum(vector.astype(F32), 0)[:vector_rows].astype(BF16)
     vector = jnp.pad(vector, ((0, chunk_rows - vector_rows), (0, 0)))

time: 632 us -> 621 us (0.983)
  local copies, waits for them, and re-layouts: 72.5 us -> 61.2 us
  Pallas kernels: 415 us -> 426 us
    pallas_call x2, Pallas kernels: 192 us -> 209 us  [ring_sum(): pl.pallas_call(functools.partial(ring_sum_kernel, n, members, plan, swaps...]
    pallas_call x2 -> x1, Pallas kernels: 53.3 us -> 43.3 us  [group_sum(): pl.pallas_call(functools.partial(sum_kernel, mode, n, SUM_CUTS), out_shap...]
    all_to_all x2, waiting for transfers between devices: 9.76 us -> 3.21 us  [exchange(): return lax.all_to_all(pieces, axis, split_axis=0, concat_axis=0, tiled=True)]
    optimization_barrier x2 -> x1, local copies, waits for them, and re-layouts: 24.6 us -> 18 us  [together(): return lax.optimization_barrier(values)]
    dot_general x5 -> x4, matrix products: 23.5 us -> 20.5 us  [the longest x2 11.4 us: body(): jnp.einsum('tsk,sfk->tf', normed2_parts, w, preferred_element_type=F32)]
  transfers between devices with their start and end apart: 6 -> 6, of which waited for: 1 -> 2; matrix products, arithmetic and copies ran while one was open for 23% -> 21% of each run, Pallas kernels for 65% -> 68%
where the time goes in v5:
time: 621 us; the launch traced here: 613 us
  Pallas kernels  426 us (69%)
  local copies, waits for them, and re-layouts  61.2 us (10%)
  matrix products  59.9 us (10%)
  other arithmetic  25.5 us (4%)
  between operations  15.1 us (2%)
  starting transfers between devices  10.7 us (2%)
  waiting for transfers between devices  8.11 us (1%)
  blocking collectives  6.27 us (1%)
    pallas_call x2, Pallas kernels, ring_sum(): pl.pallas_call(functools.partial(ring_sum_kernel, n, members, plan, swaps...  209 us
    pallas_call x1, Pallas kernels, ring_gather(): pl.pallas_call(functools.partial(ring_gather_kernel, n, count), out_shape...  68.8 us
    pallas_call x1, Pallas kernels, group_sum(): pl.pallas_call(functools.partial(sum_kernel, mode, n, SUM_CUTS), out_shap...  43.3 us
    pallas_call x1, Pallas kernels, return_grads(): pl.pallas_call(functools.partial(return_kernel, n), out_shape=jax.ShapeDt...  35.5 us
    dot_general x8, matrix products, dot(): lax.dot_general(left, right, (contract, ((), ())), preferred_element_type...  32.5 us
    pallas_call x1, Pallas kernels, share_keys(): pl.pallas_call(functools.partial(share_kernel, n), out_shape=jax.ShapeDty...  23 us
    optimization_barrier x1, local copies, waits for them, and re-layouts, together(): return lax.optimization_barrier(values)  18 us
    pallas_call x1, Pallas kernels, attend_back(): pl.pallas_call(functools.partial(attend_back_kernel, heads), out_shape=(j...  16.1 us
  transfers between devices with their start and end apart: 6, of which 2 were waited for; matrix products, arithmetic and copies ran while one was open for 21% of the time, Pallas kernels for 68%

profile of v5, /device:TPU:0, one launch (start us, length us, event | category | flops | bytes accessed | tf_op | source)
XLA Modules:
  0.0 612.9 jit_solution(4397506209786834685)
XLA Ops:
  7.9 1.0 pad_maximum_fusion.15
  8.9 6.3 %all-gather.2 = bf16[4,1,1280]{2,1,0:T(2,128)(2,1)S(1)} all-gather(bf16[1,1,1280]{2,1,0:T(2,128)(2,1)S(1)} %reshape.283), channel_id=3, replica_groups=mesh['ctx'=8,'fsdp'=4] {'fsdp'}, dimensions={0}, use_global_device_ids=true | all-gather | bytes 12800 | tf_op jit(solution)/shard_map/all_gather | solution.py:855
  15.2 1.1 fusion.34
  16.3 1.4 fusion.33
  17.8 1.6 pad_maximum_fusion
  19.4 4.4 all-to-all-start
  23.9 18.0 %copy.56 = bf16[384,2,4480]{0,2,1:T(8,128)(2,1)} copy(bf16[384,2,4480]{2,1,0:T(2,128)(2,1)} %param.17) | data formatting | bytes 13762560 | tf_op jit(solution)/shard_map/optimization_barrier | solution.py:823
  41.9 6.5 %copy.79 = bf16[384,2,4,1120]{0,3,1,2:T(8,128)(2,1)} copy(bf16[384,2,4,1120]{0,3,2,1:T(8,128)(2,1)} %bitcast.119) | data formatting | bytes 13762560 | tf_op jit(solution)/shard_map/reshape | solution.py:887
  48.4 3.2 all-to-all-done
  51.6 5.5 all-to-all-start.1
  60.0 1.2 broadcast_multiply_fusion
  62.5 1.0 fusion.19
  63.5 0.7 copy-done.7
  64.3 1.0 pad_maximum_fusion.13
  65.3 5.4 project.1
  70.7 23.0 %share_keys.1 = bf16[8,2,256,256]{3,2,1,0:T(8,128)(2,1)} custom-call(bf16[2,256,256]{2,1,0:T(8,128)(2,1)} %bitcast.155), custom_call_target="tpu_custom_call" | custom-call | bytes 60000000 | tf_op jit(solution)/shard_map/share_keys/pallas_call | solution.py:489
  93.6 13.2 %attend.1 = (bf16[2,256,384]{2,1,0:T(8,128)(2,1)}, f32[2,1,768]{2,1,0:T(1,128)}) custom-call(s32[16]{0:T(128)} %pad_add_fusion.table, s32[2]{0:T(128)} %get-tuple-element.76.ids, bf16[2,256,384]{2,1,0:T(8,128)(2,1)} %bitcast.171, bf16[4096,256]{1,0:T(8,128)(2,1)} %bitcast.138), custom_call_target="tpu_custom_call" | custom-call | flops 1610612736 | bytes 2097152 | tf_op jit(solution)/shard_map/attend/pallas_call | solution.py:170
  106.8 3.5 convolution_convert_fusion.5
  110.4 43.3 %group_sum_attention.1 = (f32[2,64,1536]{2,1,0:T(8,128)}, bf16[2,4,64,1536]{3,2,1,0:T(8,128)(2,1)}) custom-call(bf16[2,4,64,1536]{3,2,1,0:T(8,128)(2,1)} %bitcast.126, bf16[2,64,1536]{2,1,0:T(8,128)(2,1)} %bitcast.131, f32[1,1536]{1,0:T(1,128)} %bitcast.158), custom_call_target="tpu_custom_call" | custom-call | flops 1966080 | bytes 60000000 | tf_op jit(solution)/shard_map/group_sum_attention/pallas_call | solution.py:406
  153.9 3.9 reshape_reshape.3
  157.9 6.1 convolution_bitcast_fusion.1
  164.0 5.4 convolution_bitcast_fusion
  169.3 4.2 all-gather.7.cloned.1.call-done
  173.5 7.1 %multiply_convert_fusion = (bf16[512,1120]{0,1:T(8,128)(2,1)}, bf16[512,1120]{0,1:T(8,128)(2,1)}, bf16[512,1120]{0,1:T(8,128)(2,1)S(1)}) fusion(f32[512,1120]{0,1:T(8,128)} %convolution_bitcast_fusion.1, f32[512,1120]{0,1:T(8,128)} %convolution_bitcast_fusion, bf16[512,1536]{1,0:T(8,128)(2,1)} %bitcast.169, bf16[1120,1536]{1,0:T(8,128)(2,1)S(1)} %copy-done), kind=kOutput, calls=%fused_computation.21 | convolution fusion | flops 1770782720 | bytes 13041664 | tf_op jit(solution)/shard_map/dot_general | solution.py:56
  180.6 3.4 convolution_convert_fusion.4
  184.4 3.7 convolution_convert_fusion.1
  188.2 3.7 copy.60
  191.8 3.8 convolution_convert_fusion
  195.6 3.7 copy.61
  199.3 4.9 fusion.3
  204.2 4.2 add_convert_fusion
  208.4 1.2 copy.62
  209.6 1.5 reshape.259.refs_3_
  211.1 3.7 convolution_convert_fusion.2
  214.9 2.0 pad.17
  216.9 119.6 %ring_sum.2 = (bf16[4,48,1120]{2,1,0:T(8,128)(2,1)}, bf16[4,48,1120]{2,1,0:T(8,128)(2,1)}, bf16[1,144,1536]{2,1,0:T(8,128)(2,1)}, f32[2,64,1536]{2,1,0:T(8,128)}...) custom-call(bf16[4,8,48,1120]{3,2,1,0:T(8,128)(2,1)} %bitcast.120, bf16[4,8,48,1120]{3,2,1,0:T(8,128)(2,1)} %bitcast.121, ...), custom_call_target="tpu_custom_call" | custom-call | bytes 200000000 | tf_op jit(solution)/shard_map/ring_sum/pallas_call | solution.py:675
  336.5 1.2 copy.65
  338.0 1.3 copy.64
  339.7 1.0 pad_maximum_fusion.4
  341.1 3.5 convolution_convert_fusion.7
  344.6 16.1 %attend_back.1 = (f32[2,256,384]{2,1,0:T(8,128)}, bf16[4096,256]{1,0:T(8,128)(2,1)}) custom-call(s32[16]{0:T(128)} %pad_add_fusion.table, s32[2]{0:T(128)} %get-tuple-element.76.ids, bf16[2,256,384]{2,1,0:T(8,128)(2,1)} %bitcast.172, bf16[4096,256]{1,0:T(8,128)(2,1)} %bitcast.139, bf16[2,256,384]{2,1,0:T(8,128)(2,1)} %get-tuple-element.45.o_ref, ...), custom_call_target="tpu_custom_call" | custom-call | flops 4026531840 | bytes 4194304 | tf_op jit(solution)/shard_map/attend_back/pallas_call | solution.py:191
  360.7 35.5 %return_grads.1 = f32[2,256,256]{2,1,0:T(8,128)} custom-call(bf16[8,2,256,256]{3,2,1,0:T(8,128)(2,1)} %bitcast.136), custom_call_target="tpu_custom_call" | custom-call | bytes 80000000 | tf_op jit(solution)/shard_map/return_grads/pallas_call | solution.py:541
  396.1 1.1 fusion.35
  397.2 1.1 pad_maximum_fusion.2
  398.3 1.6 reshape.265
  399.9 1.1 multiply_add_fusion
  401.7 1.0 copy-done.3
  404.8 4.5 fusion.32
  409.4 0.7 pad.19.refs_2_
  410.1 3.4 convolution_convert_fusion.6
  413.5 2.7 convolution_convert_fusion.3
  416.2 89.4 %ring_sum.3 = (bf16[4,48,640]{2,1,0:T(8,128)(2,1)}, bf16[1,48,1536]{2,1,0:T(8,128)(2,1)}, bf16[4,16,256]{2,1,0:T(8,128)(2,1)}, f32[2,64,1536]{2,1,0:T(8,128)}, f32[1,1536]{1,0:T(1,128)}) custom-call(bf16[4,8,48,640]{3,2,1,0:T(8,128)(2,1)} %bitcast.140, bf16[1,8,48,1536]{3,2,1,0:T(8,128)(2,1)} %bitcast.147, bf16[4,8,16,256]{3,2,1,0:T(8,128)(2,1)} %pad.19.refs_2_, ...), custom_call_target="tpu_custom_call" | custom-call | bytes 200000000 | tf_op jit(solution)/shard_map/ring_sum/pallas_call | solution.py:675
  505.6 0.8 reduce
  506.4 0.9 slice_bitcast_fusion.8
  507.4 0.9 bitcast_dynamic-update-slice_fusion
  508.4 0.7 copy-done.13
  509.1 68.8 %ring_gather.1 = (bf16[8,48,3840]{2,1,0:T(8,128)(2,1)}, bf16[8,144,1536]{2,1,0:T(8,128)(2,1)}) custom-call(bf16[48,3840]{1,0:T(8,128)(2,1)} %copy-done.13, bf16[144,1536]{1,0:T(8,128)(2,1)} %bitcast.150), custom_call_target="tpu_custom_call" | custom-call | bytes 120000000 | tf_op jit(solution)/shard_map/ring_gather/pallas_call | solution.py:734
  578.0 0.8 slice_convert_fusion.3
  579.9 3.4 slice_convert_fusion.1
  583.3 3.1 slice_convert_fusion.2
  586.5 3.8 slice_convert_fusion
  590.3 1.8 fusion.15
  592.1 12.0 %weave.1 = f32[384,2,4480]{2,1,0:T(2,128)} custom-call(bf16[2,384,4480]{2,1,0:T(8,128)(2,1)} %all-gather.9.cloned.1.call-done.planes), custom_call_target="tpu_custom_call" | custom-call | bytes 20643840 | tf_op jit(solution)/shard_map/weave/pallas_call | solution.py:756
  604.1 2.1 copy.100
  (110 shorter events, 10.4 us)
Async XLA Ops:
  7.2 166.3 %copy-start = (bf16[1120,1536]{1,0:T(8,128)(2,1)S(1)}, bf16[1120,1536]{1,0:T(8,128)(2,1)}, u32[]{:S(2)}) copy-start(bf16[1120,1536]{1,0:T(8,128)(2,1)} %param.18) | copy-start | bytes 10321924
  7.2 44.4 %all-gather.11.cloned.1.call-start = ((), (), s32[]{:S(2)}) async-start(), calls=%async_computation.6 | async-start | bytes 1966080 | tf_op jit(solution)/shard_map/all_gather | solution.py:860
  19.4 32.2 %all-to-all-start = ((bf16[4,384,640]{2,1,0:T(8,128)(2,1)}), bf16[4,384,640]{2,1,0:T(8,128)(2,1)}, u32[]{:S(2)}, u32[]{:S(2)}) async-start(bf16[4,384,640]{2,1,0:T(8,128)(2,1)} %pad_maximum_fusion), calls=%async_computation | async-start | bytes 3932160 | tf_op jit(solution)/shard_map/all_to_all | solution.py:819
  51.6 5.6 copy-start.17
  51.6 106.3 %all-to-all-start.1 = ((bf16[4,2,1120,384]{3,2,1,0:T(8,128)(2,1)}), bf16[4,2,1120,384]{3,2,1,0:T(8,128)(2,1)}, u32[]{:S(2)}, u32[]{:S(2)}) async-start(bf16[4,2,1120,384]{3,2,1,0:T(8,128)(2,1)} %bitcast.118), calls=%async_computation.1 | async-start | bytes 13762560 | tf_op jit(solution)/shard_map/all_to_all | solution.py:819
  57.1 116.4 %all-gather.7.cloned.1.call-start = ((), (), s32[]{:S(2)}) async-start(), calls=%async_computation.4 | async-start | bytes 1966080 | tf_op jit(solution)/shard_map/all_gather | solution.py:926
  63.5 0.7 copy-start.7
  63.5 1.7 copy-start.9
  153.7 436.6 %reduce-scatter.2.cloned.1.call-start = ((), (), s32[]{:S(2)}) async-start(), calls=%async_computation.3 | async-start | bytes 1966080 | tf_op jit(solution)/shard_map/reduce_scatter | solution.py:909
  157.9 6.1 copy-start.11
  180.6 3.4 copy-start.18
  184.0 408.1 %all-gather.9.cloned.1.call-start = ((), (), s32[]{:S(2)}) async-start(), calls=%async_computation.5 | async-start | bytes 7741440 | tf_op jit(solution)/shard_map/all_gather | solution.py:989
  199.3 4.9 copy-start.19
  338.0 2.7 copy-start.2
  360.6 36.5 %copy-start.12 = (f32[2,256,384]{2,1,0:T(8,128)S(1)}, f32[2,256,384]{2,1,0:T(8,128)}, u32[]{:S(2)}) copy-start(f32[2,256,384]{2,1,0:T(8,128)} %get-tuple-element.54) | copy-start | bytes 2359300
  397.2 2.7 copy-start.8
  397.2 2.7 copy-start.10
  401.6 3.2 copy-start.15
  401.7 1.0 copy-start.3
  404.8 5.3 copy-start.14
  410.1 3.4 copy-start.4
  410.1 3.4 copy-start.16
  508.4 0.7 copy-start.13
  583.3 3.1 copy-start.5
  586.5 3.9 copy-start.6
  592.1 14.1 %copy-start.1 = (bf16[1120,1536]{1,0:T(8,128)(2,1)S(1)}, bf16[1120,1536]{1,0:T(8,128)(2,1)}, u32[]{:S(2)}) copy-start(bf16[1120,1536]{1,0:T(8,128)(2,1)} %param.18) | copy-start | bytes 10321924
Sparse Core Ops, SparseCore 0:
  9.6 25.7 all-gather.10
  153.8 19.6 all-gather.6
  184.1 27.9 reduce-scatter.1
  340.8 140.3 all-gather.8

commit v6 on v5

--- a/solution.py
+++ b/solution.py
@@ -560,8 +560,12 @@
     )(partial)
 
 
-def ring_sum_kernel(n, members, plan, swaps, arrays, mode, extra_ins, extra_outs, *refs):
-    ins, refs = refs[:arrays], refs[arrays:]
+def ring_sum_kernel(n, members, plan, swaps, sizes, mode, extra_ins, extra_outs, *refs):
+    arrays = len(sizes)
+    ins = []
+    for size in sizes:
+        ins.append(refs[:size])
+        refs = refs[size:]
     side_ins, refs = refs[:extra_ins], refs[extra_ins:]
     outs, refs = refs[:arrays], refs[arrays:]
     side_outs, refs = refs[:extra_outs], refs[extra_outs:]
@@ -587,38 +591,33 @@
         step = plan[i][3]
         return ring_index((place + n * n - step * (hop + 1)) % n, n)
 
-    def window(i, group, hop):
+    def term(i, hop):
         which, low, high, _ = plan[i]
-        return ins[which][group, chunk(i, hop), :, low:high].astype(F32)
-
-    def first(i):
-        which, low, high, _ = plan[i]
-        return copy(i, 0, ins[which].at[:, chunk(i, 0), :, pl.ds(low, high - low)])
+        if len(ins[which]) == 1:
+            return ins[which][0][chunk(i, hop), :, low:high].astype(F32)
+        left, right = ins[which]
+        return jnp.dot(left[chunk(i, hop)], right[:, low:high], preferred_element_type=F32)
 
     for i in range(count):
-        first(i).start()
+        stages[i][0] = term(i, 0).astype(BF16)
+        if i:
+            copy(i - 1, 0, stages[i - 1].at[0]).start()
+    copy(count - 1, 0, stages[count - 1].at[0]).start()
     next(beside, None)
 
-    def add(i, hop, store):
+    def add(i, hop):
+        mine = term(i, hop)
         copy(i, hop - 1, stages[i].at[0]).wait_recv()
-
-        def group_add(group, carry):
-            store(group, (arrived[i][hop - 1, group].astype(F32) + window(i, group, hop)).astype(BF16))
-            return carry
-
-        lax.fori_loop(0, ins[plan[i][0]].shape[0], group_add, 0)
+        return (arrived[i][hop - 1].astype(F32) + mine).astype(BF16)
 
     def one_hop(hop, carry):
         slot = hop % 2
         for i in range(count):
-            @pl.when(hop > 2)
+            @pl.when(hop > 1)
             def _():
                 copy(i, hop - 2, stages[i].at[slot]).wait_send()
 
-            def store(group, value):
-                stages[i][slot, group] = value
-
-            add(i, hop, store)
+            stages[i][slot] = add(i, hop)
             if i:
                 copy(i - 1, hop, stages[i - 1].at[slot]).start()
         copy(count - 1, hop, stages[count - 1].at[slot]).start()
@@ -633,11 +632,10 @@
     lax.fori_loop(hop, n - 1, one_hop, 0)
     for i, (which, low, high, _) in enumerate(plan):
         target = done[swaps.index(which)] if which in swaps else outs[which]
-
-        def store(group, value):
-            target[group, :, low:high] = value
-
-        add(i, n - 1, store)
+        value = add(i, n - 1)
+        rows = target.shape[1]
+        for group in range(target.shape[0]):
+            target[group, :, low:high] = value[group * rows : (group + 1) * rows]
     swapped = []
     for j, which in enumerate(swaps):
         for k in range(1, members):
@@ -656,28 +654,37 @@
     for _ in beside:
         pass
     for i in range(count):
-        first(i).wait_send()
         for hop in (n - 3, n - 2):
             copy(i, hop, stages[i].at[hop % 2]).wait_send()
     for move in swapped:
         move.wait()
 
 
-def ring_sum(arrays, plan, swaps, members, collective, mode=None, operands=()):
-    n = arrays[0].shape[1]
+def ring_sum(arrays, groups, plan, swaps, members, collective, mode=None, operands=()):
+    n = arrays[0][0].shape[0]
     dma = pltpu.SemaphoreType.DMA
-    blocks = [
-        (arrays[which].shape[0], arrays[which].shape[2], high - low) for which, low, high, _ in plan
+    talls = [array[0].shape[1] for array in arrays]
+    blocks = [(talls[which], high - low) for which, low, high, _ in plan]
+    sums = [
+        (g, tall // g, array[-1].shape[-1]) for array, g, tall in zip(arrays, groups, talls)
     ]
-    sums = [(a.shape[0],) + a.shape[2:] for a in arrays]
+    flat = [operand for array in arrays for operand in array]
     extra_shape, extra_scratch = sum_shapes(mode, operands[0]) if mode else ((), [])
     out_shape = tuple(jax.ShapeDtypeStruct(shape, BF16) for shape in sums) + tuple(extra_shape)
     return pl.pallas_call(
         functools.partial(
-            ring_sum_kernel, n, members, plan, swaps, len(arrays), mode, len(operands), len(extra_shape)
+            ring_sum_kernel,
+            n,
+            members,
+            plan,
+            swaps,
+            tuple(len(array) for array in arrays),
+            mode,
+            len(operands),
+            len(extra_shape),
         ),
         out_shape=out_shape,
-        in_specs=in_vmem(len(arrays) + len(operands)),
+        in_specs=in_vmem(len(flat) + len(operands)),
         out_specs=tuple(in_vmem(len(out_shape))),
         scratch_shapes=[pltpu.VMEM((n - 1,) + b, BF16) for b in blocks]
         + [pltpu.VMEM((2,) + b, BF16) for b in blocks]
@@ -690,7 +697,7 @@
         ),
         cost_estimate=pl.CostEstimate(flops=0, bytes_accessed=200_000_000, transcendentals=0),
         name="ring_sum",
-    )(*arrays, *operands)
+    )(*flat, *operands)
 
 
 def ring_gather_kernel(n, count, *refs):
@@ -961,18 +968,16 @@
     down_rows = -(-ff_shard // (16 * n_ctx)) * 16
     side = D // 2
 
-    def padded(grad):
-        extra = n_ctx * down_rows - grad.shape[0]
-        return jnp.pad(grad, ((0, extra), (0, 0))).astype(BF16).reshape(n_ctx, down_rows, D)
-
-    d_w_down = padded(contract_rows(act16, cot_all))
-    d_w_gate, d_w_up = (
-        contract_rows(normed2, piece).astype(BF16).reshape(n_fsdp, n_ctx, chunk_rows, ff_shard)
-        for piece in (d_gate16, d_up16)
-    )
-
+    def by_chunk(values):
+        split = values.T.reshape(n_fsdp, n_ctx, chunk_rows, rows)
+        return split.transpose(1, 0, 2, 3).reshape(n_ctx, n_fsdp * chunk_rows, rows)
+
+    act_chunks = jnp.pad(act16.T, ((0, n_ctx * down_rows - ff_shard), (0, 0)))
+    act_chunks = act_chunks.reshape(n_ctx, down_rows, rows)
+    normed2_chunks = by_chunk(normed2)
     gate_sum, up_sum, down_sum, d_hidden, dh_all, d_gain_two = ring_sum(
-        (d_w_gate, d_w_up, d_w_down[None]),
+        ((normed2_chunks, d_gate16), (normed2_chunks, d_up16), (act_chunks, cot_all)),
+        (n_fsdp, n_fsdp, 1),
         ((0, 0, ff_shard, 1), (1, 0, ff_shard, -1), (2, 0, side, 1), (2, side, D, -1)),
         (0, 1),
         n_fsdp,
@@ -994,7 +999,6 @@
     )
     d_kv_own = return_grads(d_kv.reshape(n_ctx, 2, stretch_len, 2 * HEAD_DIM), 5).reshape(rows, -1)
 
-    d_w_out = contract_rows(attended16, dh_all).astype(BF16).reshape(n_ctx, chunk_rows, D)
     d_rotated = jnp.concatenate([d_query.reshape(rows, q_cols), d_kv_own[:, :HEAD_DIM]], 1)
     d_rotated = unrotate(
         d_rotated.reshape(rows, heads + 1, HEAD_DIM), cosines, sines
@@ -1016,12 +1020,14 @@
     parts = jnp.pad(parts, ((0, 0), (0, n_ctx * vector_rows * few - length)))
     parts = parts.reshape(n_fsdp, n_ctx, vector_rows, few)
     parts = jnp.pad(parts, ((0, 0), (0, 0), (0, -vector_rows % 16), (0, 0)))
-    d_w_qkv = contract_rows(normed1, d_qkv16).astype(BF16).reshape(n_fsdp, n_ctx, chunk_rows, -1)
+    parts = parts.transpose(1, 0, 2, 3).reshape(n_ctx, -1, few)
+    attended_chunks = attended16.T.reshape(n_ctx, chunk_rows, rows)
     pieces, out_sum, vector, d_tokens, _ = ring_sum(
-        (d_w_qkv, d_w_out[None], parts),
+        ((by_chunk(normed1), d_qkv16), (attended_chunks, dh_all), (parts,)),
+        (n_fsdp, 1, n_fsdp),
         (
             (0, 0, q_cols, 1),
-            (0, q_cols, d_w_qkv.shape[-1], -1),
+            (0, q_cols, d_qkv16.shape[-1], -1),
             (1, 0, side, 1),
             (1, side, D, -1),
             (2, 0, few, 1),

time: 621 us -> 609 us (0.981)
  matrix products: 59.9 us -> 42.1 us
  local copies, waits for them, and re-layouts: 61.2 us -> 69.3 us
    dot_general x8 -> x3, matrix products: 32.5 us -> 12 us  [dot(): lax.dot_general(left, right, (contract, ((), ())), preferred_element_type...]
    transpose x0 -> x5, local copies, waits for them, and re-layouts: none -> 8.21 us  [the longest x2 5.58 us: by_chunk(): return split.transpose(1, 0, 2, 3).reshape(n_ctx, n_fsdp * chunk_rows, rows)]
    convert_element_type x2 -> x0, local copies, waits for them, and re-layouts: 7.31 us -> none  [body(): contract_rows(normed2, piece).astype(BF16)]
  transfers between devices with their start and end apart: 6 -> 6, of which waited for: 2 -> 1; matrix products, arithmetic and copies ran while one was open for 21% -> 22% of each run, Pallas kernels for 68% -> 69%
where the time goes in v6:
time: 609 us; the launch traced here: 601 us
  Pallas kernels  427 us (70%)
  local copies, waits for them, and re-layouts  69.3 us (11%)
  matrix products  42.1 us (7%)
  other arithmetic  26.5 us (4%)
  between operations  15.5 us (3%)
  starting transfers between devices  10.6 us (2%)
  blocking collectives  6.27 us (1%)
    pallas_call x2, Pallas kernels, ring_sum(): pl.pallas_call(functools.partial(ring_sum_kernel, n, members, plan, swaps...  213 us
    pallas_call x1, Pallas kernels, ring_gather(): pl.pallas_call(functools.partial(ring_gather_kernel, n, count), out_shape...  68.9 us
    pallas_call x1, Pallas kernels, group_sum(): pl.pallas_call(functools.partial(sum_kernel, mode, n, SUM_CUTS), out_shap...  43.3 us
    pallas_call x1, Pallas kernels, return_grads(): pl.pallas_call(functools.partial(return_kernel, n), out_shape=jax.ShapeDt...  31.7 us
    pallas_call x1, Pallas kernels, share_keys(): pl.pallas_call(functools.partial(share_kernel, n), out_shape=jax.ShapeDty...  23.1 us
    optimization_barrier x1, local copies, waits for them, and re-layouts, together(): return lax.optimization_barrier(values)  18 us
    pallas_call x1, Pallas kernels, attend_back(): pl.pallas_call(functools.partial(attend_back_kernel, heads), out_shape=(j...  16.4 us
    pallas_call x1, Pallas kernels, attend(): pl.pallas_call(functools.partial(attend_kernel, heads), out_shape=(jax.Sh...  13.2 us
  transfers between devices with their start and end apart: 6, of which 1 were waited for; matrix products, arithmetic and copies ran while one was open for 22% of the time, Pallas kernels for 69%

profile of v6, /device:TPU:0, one launch (start us, length us, event | category | flops | bytes accessed | tf_op | source)
XLA Modules:
  0.0 600.8 jit_solution(3159383390088899585)
XLA Ops:
  7.2 0.7 all-gather.11.cloned.1.call-update
  7.9 1.0 pad_maximum_fusion.15
  8.9 6.3 %all-gather.2 = bf16[4,1,1280]{2,1,0:T(2,128)(2,1)S(1)} all-gather(bf16[1,1,1280]{2,1,0:T(2,128)(2,1)S(1)} %reshape.299), channel_id=3, replica_groups=mesh['ctx'=8,'fsdp'=4] {'fsdp'}, dimensions={0}, use_global_device_ids=true | all-gather | bytes 12800 | tf_op jit(solution)/shard_map/all_gather | solution.py:862
  15.2 1.1 fusion.37
  16.3 1.4 fusion.36
  17.8 1.6 pad_maximum_fusion
  19.4 4.4 all-to-all-start
  23.9 18.0 %copy.118 = bf16[384,2,4480]{0,2,1:T(8,128)(2,1)} copy(bf16[384,2,4480]{2,1,0:T(2,128)(2,1)} %param.17) | data formatting | bytes 13762560 | tf_op jit(solution)/shard_map/optimization_barrier | solution.py:830
  41.9 6.5 %copy.161 = bf16[384,2,4,1120]{0,3,1,2:T(8,128)(2,1)} copy(bf16[384,2,4,1120]{0,3,2,1:T(8,128)(2,1)} %bitcast.148) | data formatting | bytes 13762560 | tf_op jit(solution)/shard_map/reshape | solution.py:894
  48.4 3.2 all-to-all-done
  51.6 5.5 all-to-all-start.1
  60.0 1.2 broadcast_multiply_fusion
  62.5 1.0 fusion.23
  63.6 0.7 copy-done.6
  64.2 1.0 pad_maximum_fusion.13
  65.2 5.4 project.1
  70.6 23.1 %share_keys.1 = bf16[8,2,256,256]{3,2,1,0:T(8,128)(2,1)} custom-call(bf16[2,256,256]{2,1,0:T(8,128)(2,1)} %bitcast.192), custom_call_target="tpu_custom_call" | custom-call | bytes 60000000 | tf_op jit(solution)/shard_map/share_keys/pallas_call | solution.py:489
  93.7 13.2 %attend.1 = (bf16[2,256,384]{2,1,0:T(8,128)(2,1)}, f32[2,1,768]{2,1,0:T(1,128)}) custom-call(s32[16]{0:T(128)} %pad_add_fusion.table, s32[2]{0:T(128)} %get-tuple-element.76.ids, bf16[2,256,384]{2,1,0:T(8,128)(2,1)} %bitcast.206, bf16[4096,256]{1,0:T(8,128)(2,1)} %bitcast.172), custom_call_target="tpu_custom_call" | custom-call | flops 1610612736 | bytes 2097152 | tf_op jit(solution)/shard_map/attend/pallas_call | solution.py:170
  106.9 3.5 convolution_convert_fusion.1
  110.4 43.3 %group_sum_attention.1 = (f32[2,64,1536]{2,1,0:T(8,128)}, bf16[2,4,64,1536]{3,2,1,0:T(8,128)(2,1)}) custom-call(bf16[2,4,64,1536]{3,2,1,0:T(8,128)(2,1)} %bitcast.157, bf16[2,64,1536]{2,1,0:T(8,128)(2,1)} %bitcast.163, f32[1,1536]{1,0:T(1,128)} %bitcast.195), custom_call_target="tpu_custom_call" | custom-call | flops 1966080 | bytes 60000000 | tf_op jit(solution)/shard_map/group_sum_attention/pallas_call | solution.py:406
  154.2 3.9 reshape_reshape.3
  158.2 4.7 fusion.4
  162.9 6.8 %fusion.7 = (bf16[1120,512]{1,0:T(8,128)(2,1)}, f32[512,1120,1]{0,1,2:T(8,128)}) fusion(f32[512,1120,1]{0,1,2:T(8,128)S(1)} %fusion.4, bf16[4,2,1120,384]{3,2,1,0:T(8,128)(2,1)} %all-to-all-done.1, bf16[512,4,384]{2,1,0:T(4,128)(2,1)S(1)} %copy-done.13), kind=kOutput, calls=%fused_computation.21 | convolution fusion | flops 1765048320 | bytes 10747904 | tf_op jit(solution)/shard_map/tsk,sfk->tf/dot_general | solution.py:937
  169.8 3.0 copy.126
  172.8 3.0 copy.124
  175.8 5.7 convolution_convert_fusion
  181.6 2.6 copy.129
  184.2 2.7 copy.130
  187.0 5.9 multiply_convert_fusion
  192.9 5.0 fusion.3
  198.0 4.2 add_convert_fusion
  202.2 1.2 copy.138
  203.4 1.7 reshape.274.refs_6_
  205.1 1.1 pad.16
  206.2 120.2 %ring_sum.2 = (bf16[4,48,1120]{2,1,0:T(8,128)(2,1)}, bf16[4,48,1120]{2,1,0:T(8,128)(2,1)}, bf16[1,144,1536]{2,1,0:T(8,128)(2,1)}, f32[2,64,1536]{2,1,0:T(8,128)}...) custom-call(bf16[8,192,512]{2,1,0:T(8,128)(2,1)} %bitcast.149, bf16[512,1120]{1,0:T(8,128)(2,1)} %copy-done.18, ...), custom_call_target="tpu_custom_call" | custom-call | bytes 200000000 | tf_op jit(solution)/shard_map/ring_sum/pallas_call | solution.py:674
  326.4 1.2 copy.142
  327.9 1.2 copy.141
  329.5 1.0 pad_maximum_fusion.4
  330.6 1.0 copy.139
  331.5 1.8 copy.127
  333.3 2.8 copy.128
  336.6 1.7 convolution_convert_fusion.2
  338.3 16.4 %attend_back.1 = (f32[2,256,384]{2,1,0:T(8,128)}, bf16[4096,256]{1,0:T(8,128)(2,1)}) custom-call(s32[16]{0:T(128)} %pad_add_fusion.table, s32[2]{0:T(128)} %get-tuple-element.76.ids, bf16[2,256,384]{2,1,0:T(8,128)(2,1)} %bitcast.207, bf16[4096,256]{1,0:T(8,128)(2,1)} %bitcast.173, bf16[2,256,384]{2,1,0:T(8,128)(2,1)} %get-tuple-element.45.o_ref, ...), custom_call_target="tpu_custom_call" | custom-call | flops 4026531840 | bytes 4194304 | tf_op jit(solution)/shard_map/attend_back/pallas_call | solution.py:191
  354.7 31.7 %return_grads.1 = f32[2,256,256]{2,1,0:T(8,128)} custom-call(bf16[8,2,256,256]{3,2,1,0:T(8,128)(2,1)} %bitcast.170), custom_call_target="tpu_custom_call" | custom-call | bytes 80000000 | tf_op jit(solution)/shard_map/return_grads/pallas_call | solution.py:541
  386.4 1.1 fusion.38
  387.5 1.1 pad_maximum_fusion.2
  388.6 1.6 reshape.280
  390.2 1.1 multiply_add_fusion
  394.2 1.0 fusion.17.refs_1_
  395.2 4.4 fusion.35
  399.7 0.9 copy.140
  400.5 92.6 %ring_sum.3 = (bf16[4,48,640]{2,1,0:T(8,128)(2,1)}, bf16[1,48,1536]{2,1,0:T(8,128)(2,1)}, bf16[4,16,256]{2,1,0:T(8,128)(2,1)}, f32[2,64,1536]{2,1,0:T(8,128)}, f32[1,1536]{1,0:T(1,128)}) custom-call(bf16[8,192,512]{2,1,0:T(8,128)(2,1)} %bitcast.160, bf16[512,640]{1,0:T(8,128)(2,1)} %copy-done.5, bf16[8,48,512]{2,1,0:T(8,128)(2,1)} %bitcast.185, ...), custom_call_target="tpu_custom_call" | custom-call | bytes 200000000 | tf_op jit(solution)/shard_map/ring_sum/pallas_call | solution.py:674
  493.2 0.8 reduce
  494.0 0.9 slice_bitcast_fusion.8
  495.0 0.9 bitcast_dynamic-update-slice_fusion
  496.0 0.7 copy-done.21
  496.7 68.9 %ring_gather.1 = (bf16[8,48,3840]{2,1,0:T(8,128)(2,1)}, bf16[8,144,1536]{2,1,0:T(8,128)(2,1)}) custom-call(bf16[48,3840]{1,0:T(8,128)(2,1)} %copy-done.21, bf16[144,1536]{1,0:T(8,128)(2,1)} %bitcast.189), custom_call_target="tpu_custom_call" | custom-call | bytes 120000000 | tf_op jit(solution)/shard_map/ring_gather/pallas_call | solution.py:741
  565.6 0.8 slice_convert_fusion.3
  567.5 3.4 slice_convert_fusion.1
  571.0 3.1 slice_convert_fusion.2
  574.1 3.8 slice_convert_fusion
  578.0 1.8 fusion.22
  579.8 12.0 %weave.1 = f32[384,2,4480]{2,1,0:T(2,128)} custom-call(bf16[2,384,4480]{2,1,0:T(8,128)(2,1)} %all-gather.9.cloned.1.call-done.planes), custom_call_target="tpu_custom_call" | custom-call | bytes 20643840 | tf_op jit(solution)/shard_map/weave/pallas_call | solution.py:763
  591.8 2.1 copy.183
  (120 shorter events, 9.7 us)
Async XLA Ops:
  7.2 168.6 %copy-start = (bf16[1120,1536]{1,0:T(8,128)(2,1)S(1)}, bf16[1120,1536]{1,0:T(8,128)(2,1)}, u32[]{:S(2)}) copy-start(bf16[1120,1536]{1,0:T(8,128)(2,1)} %param.18) | copy-start | bytes 10321924
  7.2 44.4 %all-gather.11.cloned.1.call-start = ((), (), s32[]{:S(2)}) async-start(), calls=%async_computation.6 | async-start | bytes 1966080 | tf_op jit(solution)/shard_map/all_gather | solution.py:867
  19.4 32.2 %all-to-all-start = ((bf16[4,384,640]{2,1,0:T(8,128)(2,1)}), bf16[4,384,640]{2,1,0:T(8,128)(2,1)}, u32[]{:S(2)}, u32[]{:S(2)}) async-start(bf16[4,384,640]{2,1,0:T(8,128)(2,1)} %pad_maximum_fusion), calls=%async_computation | async-start | bytes 3932160 | tf_op jit(solution)/shard_map/all_to_all | solution.py:826
  51.6 5.6 copy-start.23
  51.6 106.5 %all-to-all-start.1 = ((bf16[4,2,1120,384]{3,2,1,0:T(8,128)(2,1)}), bf16[4,2,1120,384]{3,2,1,0:T(8,128)(2,1)}, u32[]{:S(2)}, u32[]{:S(2)}) async-start(bf16[4,2,1120,384]{3,2,1,0:T(8,128)(2,1)} %bitcast.147), calls=%async_computation.1 | async-start | bytes 13762560 | tf_op jit(solution)/shard_map/all_to_all | solution.py:826
  57.1 129.8 %all-gather.7.cloned.1.call-start = ((), (), s32[]{:S(2)}) async-start(), calls=%async_computation.4 | async-start | bytes 1966080 | tf_op jit(solution)/shard_map/all_gather | solution.py:933
  63.5 0.7 copy-start.6
  63.6 1.7 copy-start.8
  153.7 424.3 %reduce-scatter.2.cloned.1.call-start = ((), (), s32[]{:S(2)}) async-start(), calls=%async_computation.3 | async-start | bytes 1966080 | tf_op jit(solution)/shard_map/reduce_scatter | solution.py:916
  158.1 4.7 copy-start.13
  162.9 6.9 %copy-start.11 = (f32[512,1120,1]{0,1,2:T(8,128)}, f32[512,1120,1]{0,1,2:T(8,128)S(1)}, u32[]{:S(2)}) copy-start(f32[512,1120,1]{0,1,2:T(8,128)S(1)} %fusion.4) | copy-start | bytes 6881284
  181.6 398.2 %all-gather.9.cloned.1.call-start = ((), (), s32[]{:S(2)}) async-start(), calls=%async_computation.5 | async-start | bytes 7741440 | tf_op jit(solution)/shard_map/all_gather | solution.py:994
  192.9 5.1 copy-start.18
  192.9 5.1 copy-start.17
  203.4 1.7 copy-start.19
  327.9 2.6 copy-start.14
  329.2 2.4 copy-start.12
  333.3 2.9 copy-start.2
  333.3 3.3 copy-start.15
  333.3 3.3 copy-start.16
  354.7 32.8 %copy-start.20 = (f32[2,256,384]{2,1,0:T(8,128)S(1)}, f32[2,256,384]{2,1,0:T(8,128)}, u32[]{:S(2)}) copy-start(f32[2,256,384]{2,1,0:T(8,128)} %get-tuple-element.54) | copy-start | bytes 2359300
  387.5 4.5 copy-start.10
  387.5 2.7 copy-start.7
  387.5 2.7 copy-start.9
  391.9 2.2 copy-start.22
  395.2 4.4 copy-start.5
  496.0 0.7 copy-start.21
  571.0 3.1 copy-start.3
  574.1 3.9 copy-start.4
  579.8 14.1 %copy-start.1 = (bf16[1120,1536]{1,0:T(8,128)(2,1)S(1)}, bf16[1120,1536]{1,0:T(8,128)(2,1)}, u32[]{:S(2)}) copy-start(bf16[1120,1536]{1,0:T(8,128)(2,1)} %param.18) | copy-start | bytes 10321924
Sparse Core Ops, SparseCore 0:
  9.6 25.7 all-gather.10
  153.8 19.6 all-gather.6
  181.7 28.0 reduce-scatter.1
  330.7 139.1 all-gather.8

commit v7 on v6

--- a/solution.py
+++ b/solution.py
@@ -625,7 +625,7 @@
 
     hop = 1
     if mode:
-        for _ in range(min(4, n - 3)):
+        for _ in range(min(4 if mode == "mlp" else 2, n - 3)):
             one_hop(jnp.int32(hop), 0)
             hop += 1
             next(beside, None)

time: 609 us -> 609 us (level)
  no operation moved by 1% of the time
where the time goes in v7:
time: 609 us; the launch traced here: 601 us
  Pallas kernels  427 us (70%)
  local copies, waits for them, and re-layouts  69.3 us (11%)
  matrix products  42.1 us (7%)
  other arithmetic  26.5 us (4%)
  between operations  15.5 us (3%)
  starting transfers between devices  10.6 us (2%)
  blocking collectives  6.27 us (1%)
    pallas_call x2, Pallas kernels, ring_sum(): pl.pallas_call(functools.partial(ring_sum_kernel, n, members, plan, swaps...  213 us
    pallas_call x1, Pallas kernels, ring_gather(): pl.pallas_call(functools.partial(ring_gather_kernel, n, count), out_shape...  68.9 us
    pallas_call x1, Pallas kernels, group_sum(): pl.pallas_call(functools.partial(sum_kernel, mode, n, SUM_CUTS), out_shap...  43.3 us
    pallas_call x1, Pallas kernels, return_grads(): pl.pallas_call(functools.partial(return_kernel, n), out_shape=jax.ShapeDt...  31.7 us
    pallas_call x1, Pallas kernels, share_keys(): pl.pallas_call(functools.partial(share_kernel, n), out_shape=jax.ShapeDty...  23.1 us
    optimization_barrier x1, local copies, waits for them, and re-layouts, together(): return lax.optimization_barrier(values)  18 us
    pallas_call x1, Pallas kernels, attend_back(): pl.pallas_call(functools.partial(attend_back_kernel, heads), out_shape=(j...  16.4 us
    pallas_call x1, Pallas kernels, attend(): pl.pallas_call(functools.partial(attend_kernel, heads), out_shape=(jax.Sh...  13.2 us
  transfers between devices with their start and end apart: 6, of which 1 were waited for; matrix products, arithmetic and copies ran while one was open for 22% of the time, Pallas kernels for 69%

profile of v7, /device:TPU:0, one launch (start us, length us, event | category | flops | bytes accessed | tf_op | source)
XLA Modules:
  0.0 600.8 jit_solution(6954027996250554808)
XLA Ops:
  7.2 0.7 all-gather.11.cloned.1.call-update
  7.9 1.0 pad_maximum_fusion.15
  8.9 6.3 %all-gather.2 = bf16[4,1,1280]{2,1,0:T(2,128)(2,1)S(1)} all-gather(bf16[1,1,1280]{2,1,0:T(2,128)(2,1)S(1)} %reshape.299), channel_id=3, replica_groups=mesh['ctx'=8,'fsdp'=4] {'fsdp'}, dimensions={0}, use_global_device_ids=true | all-gather | bytes 12800 | tf_op jit(solution)/shard_map/all_gather | solution.py:862
  15.2 1.1 fusion.37
  16.3 1.4 fusion.36
  17.8 1.6 pad_maximum_fusion
  19.4 4.4 all-to-all-start
  23.9 18.0 %copy.118 = bf16[384,2,4480]{0,2,1:T(8,128)(2,1)} copy(bf16[384,2,4480]{2,1,0:T(2,128)(2,1)} %param.17) | data formatting | bytes 13762560 | tf_op jit(solution)/shard_map/optimization_barrier | solution.py:830
  41.9 6.5 %copy.161 = bf16[384,2,4,1120]{0,3,1,2:T(8,128)(2,1)} copy(bf16[384,2,4,1120]{0,3,2,1:T(8,128)(2,1)} %bitcast.148) | data formatting | bytes 13762560 | tf_op jit(solution)/shard_map/reshape | solution.py:894
  48.4 3.2 all-to-all-done
  51.6 5.5 all-to-all-start.1
  60.0 1.2 broadcast_multiply_fusion
  62.5 1.0 fusion.23
  63.6 0.7 copy-done.6
  64.2 1.0 pad_maximum_fusion.13
  65.2 5.4 project.1
  70.6 23.1 %share_keys.1 = bf16[8,2,256,256]{3,2,1,0:T(8,128)(2,1)} custom-call(bf16[2,256,256]{2,1,0:T(8,128)(2,1)} %bitcast.192), custom_call_target="tpu_custom_call" | custom-call | bytes 60000000 | tf_op jit(solution)/shard_map/share_keys/pallas_call | solution.py:489
  93.7 13.2 %attend.1 = (bf16[2,256,384]{2,1,0:T(8,128)(2,1)}, f32[2,1,768]{2,1,0:T(1,128)}) custom-call(s32[16]{0:T(128)} %pad_add_fusion.table, s32[2]{0:T(128)} %get-tuple-element.76.ids, bf16[2,256,384]{2,1,0:T(8,128)(2,1)} %bitcast.206, bf16[4096,256]{1,0:T(8,128)(2,1)} %bitcast.172), custom_call_target="tpu_custom_call" | custom-call | flops 1610612736 | bytes 2097152 | tf_op jit(solution)/shard_map/attend/pallas_call | solution.py:170
  106.9 3.5 convolution_convert_fusion.1
  110.4 43.3 %group_sum_attention.1 = (f32[2,64,1536]{2,1,0:T(8,128)}, bf16[2,4,64,1536]{3,2,1,0:T(8,128)(2,1)}) custom-call(bf16[2,4,64,1536]{3,2,1,0:T(8,128)(2,1)} %bitcast.157, bf16[2,64,1536]{2,1,0:T(8,128)(2,1)} %bitcast.163, f32[1,1536]{1,0:T(1,128)} %bitcast.195), custom_call_target="tpu_custom_call" | custom-call | flops 1966080 | bytes 60000000 | tf_op jit(solution)/shard_map/group_sum_attention/pallas_call | solution.py:406
  154.2 3.9 reshape_reshape.3
  158.2 4.7 fusion.4
  162.9 6.8 %fusion.7 = (bf16[1120,512]{1,0:T(8,128)(2,1)}, f32[512,1120,1]{0,1,2:T(8,128)}) fusion(f32[512,1120,1]{0,1,2:T(8,128)S(1)} %fusion.4, bf16[4,2,1120,384]{3,2,1,0:T(8,128)(2,1)} %all-to-all-done.1, bf16[512,4,384]{2,1,0:T(4,128)(2,1)S(1)} %copy-done.13), kind=kOutput, calls=%fused_computation.21 | convolution fusion | flops 1765048320 | bytes 10747904 | tf_op jit(solution)/shard_map/tsk,sfk->tf/dot_general | solution.py:937
  169.8 3.0 copy.126
  172.8 3.0 copy.124
  175.8 5.7 convolution_convert_fusion
  181.6 2.6 copy.129
  184.2 2.7 copy.130
  187.0 5.9 multiply_convert_fusion
  192.9 5.0 fusion.3
  198.0 4.2 add_convert_fusion
  202.2 1.2 copy.138
  203.4 1.7 reshape.274.refs_6_
  205.1 1.1 pad.16
  206.2 120.2 %ring_sum.2 = (bf16[4,48,1120]{2,1,0:T(8,128)(2,1)}, bf16[4,48,1120]{2,1,0:T(8,128)(2,1)}, bf16[1,144,1536]{2,1,0:T(8,128)(2,1)}, f32[2,64,1536]{2,1,0:T(8,128)}...) custom-call(bf16[8,192,512]{2,1,0:T(8,128)(2,1)} %bitcast.149, bf16[512,1120]{1,0:T(8,128)(2,1)} %copy-done.18, ...), custom_call_target="tpu_custom_call" | custom-call | bytes 200000000 | tf_op jit(solution)/shard_map/ring_sum/pallas_call | solution.py:674
  326.4 1.2 copy.142
  327.9 1.2 copy.141
  329.5 1.0 pad_maximum_fusion.4
  330.6 1.0 copy.139
  331.5 1.8 copy.127
  333.3 2.8 copy.128
  336.6 1.7 convolution_convert_fusion.2
  338.3 16.4 %attend_back.1 = (f32[2,256,384]{2,1,0:T(8,128)}, bf16[4096,256]{1,0:T(8,128)(2,1)}) custom-call(s32[16]{0:T(128)} %pad_add_fusion.table, s32[2]{0:T(128)} %get-tuple-element.76.ids, bf16[2,256,384]{2,1,0:T(8,128)(2,1)} %bitcast.207, bf16[4096,256]{1,0:T(8,128)(2,1)} %bitcast.173, bf16[2,256,384]{2,1,0:T(8,128)(2,1)} %get-tuple-element.45.o_ref, ...), custom_call_target="tpu_custom_call" | custom-call | flops 4026531840 | bytes 4194304 | tf_op jit(solution)/shard_map/attend_back/pallas_call | solution.py:191
  354.7 31.7 %return_grads.1 = f32[2,256,256]{2,1,0:T(8,128)} custom-call(bf16[8,2,256,256]{3,2,1,0:T(8,128)(2,1)} %bitcast.170), custom_call_target="tpu_custom_call" | custom-call | bytes 80000000 | tf_op jit(solution)/shard_map/return_grads/pallas_call | solution.py:541
  386.4 1.1 fusion.38
  387.5 1.1 pad_maximum_fusion.2
  388.6 1.6 reshape.280
  390.2 1.1 multiply_add_fusion
  394.2 1.0 fusion.17.refs_1_
  395.2 4.4 fusion.35
  399.7 0.9 copy.140
  400.5 92.6 %ring_sum.3 = (bf16[4,48,640]{2,1,0:T(8,128)(2,1)}, bf16[1,48,1536]{2,1,0:T(8,128)(2,1)}, bf16[4,16,256]{2,1,0:T(8,128)(2,1)}, f32[2,64,1536]{2,1,0:T(8,128)}, f32[1,1536]{1,0:T(1,128)}) custom-call(bf16[8,192,512]{2,1,0:T(8,128)(2,1)} %bitcast.160, bf16[512,640]{1,0:T(8,128)(2,1)} %copy-done.5, bf16[8,48,512]{2,1,0:T(8,128)(2,1)} %bitcast.185, ...), custom_call_target="tpu_custom_call" | custom-call | bytes 200000000 | tf_op jit(solution)/shard_map/ring_sum/pallas_call | solution.py:674
  493.2 0.8 reduce
  494.0 0.9 slice_bitcast_fusion.8
  495.0 0.9 bitcast_dynamic-update-slice_fusion
  496.0 0.7 copy-done.21
  496.7 68.9 %ring_gather.1 = (bf16[8,48,3840]{2,1,0:T(8,128)(2,1)}, bf16[8,144,1536]{2,1,0:T(8,128)(2,1)}) custom-call(bf16[48,3840]{1,0:T(8,128)(2,1)} %copy-done.21, bf16[144,1536]{1,0:T(8,128)(2,1)} %bitcast.189), custom_call_target="tpu_custom_call" | custom-call | bytes 120000000 | tf_op jit(solution)/shard_map/ring_gather/pallas_call | solution.py:741
  565.6 0.8 slice_convert_fusion.3
  567.5 3.4 slice_convert_fusion.1
  571.0 3.1 slice_convert_fusion.2
  574.1 3.8 slice_convert_fusion
  578.0 1.8 fusion.22
  579.8 12.0 %weave.1 = f32[384,2,4480]{2,1,0:T(2,128)} custom-call(bf16[2,384,4480]{2,1,0:T(8,128)(2,1)} %all-gather.9.cloned.1.call-done.planes), custom_call_target="tpu_custom_call" | custom-call | bytes 20643840 | tf_op jit(solution)/shard_map/weave/pallas_call | solution.py:763
  591.8 2.1 copy.183
  (120 shorter events, 9.7 us)
Async XLA Ops:
  7.2 168.6 %copy-start = (bf16[1120,1536]{1,0:T(8,128)(2,1)S(1)}, bf16[1120,1536]{1,0:T(8,128)(2,1)}, u32[]{:S(2)}) copy-start(bf16[1120,1536]{1,0:T(8,128)(2,1)} %param.18) | copy-start | bytes 10321924
  7.2 44.4 %all-gather.11.cloned.1.call-start = ((), (), s32[]{:S(2)}) async-start(), calls=%async_computation.6 | async-start | bytes 1966080 | tf_op jit(solution)/shard_map/all_gather | solution.py:867
  19.4 32.2 %all-to-all-start = ((bf16[4,384,640]{2,1,0:T(8,128)(2,1)}), bf16[4,384,640]{2,1,0:T(8,128)(2,1)}, u32[]{:S(2)}, u32[]{:S(2)}) async-start(bf16[4,384,640]{2,1,0:T(8,128)(2,1)} %pad_maximum_fusion), calls=%async_computation | async-start | bytes 3932160 | tf_op jit(solution)/shard_map/all_to_all | solution.py:826
  51.6 5.6 copy-start.23
  51.6 106.5 %all-to-all-start.1 = ((bf16[4,2,1120,384]{3,2,1,0:T(8,128)(2,1)}), bf16[4,2,1120,384]{3,2,1,0:T(8,128)(2,1)}, u32[]{:S(2)}, u32[]{:S(2)}) async-start(bf16[4,2,1120,384]{3,2,1,0:T(8,128)(2,1)} %bitcast.147), calls=%async_computation.1 | async-start | bytes 13762560 | tf_op jit(solution)/shard_map/all_to_all | solution.py:826
  57.1 129.8 %all-gather.7.cloned.1.call-start = ((), (), s32[]{:S(2)}) async-start(), calls=%async_computation.4 | async-start | bytes 1966080 | tf_op jit(solution)/shard_map/all_gather | solution.py:933
  63.5 0.7 copy-start.6
  63.6 1.7 copy-start.8
  153.7 424.3 %reduce-scatter.2.cloned.1.call-start = ((), (), s32[]{:S(2)}) async-start(), calls=%async_computation.3 | async-start | bytes 1966080 | tf_op jit(solution)/shard_map/reduce_scatter | solution.py:916
  158.1 4.7 copy-start.13
  162.9 6.9 %copy-start.11 = (f32[512,1120,1]{0,1,2:T(8,128)}, f32[512,1120,1]{0,1,2:T(8,128)S(1)}, u32[]{:S(2)}) copy-start(f32[512,1120,1]{0,1,2:T(8,128)S(1)} %fusion.4) | copy-start | bytes 6881284
  181.6 398.2 %all-gather.9.cloned.1.call-start = ((), (), s32[]{:S(2)}) async-start(), calls=%async_computation.5 | async-start | bytes 7741440 | tf_op jit(solution)/shard_map/all_gather | solution.py:994
  192.9 5.1 copy-start.18
  192.9 5.1 copy-start.17
  203.4 1.7 copy-start.19
  327.9 2.6 copy-start.14
  329.2 2.4 copy-start.12
  333.3 2.9 copy-start.2
  333.3 3.3 copy-start.15
  333.3 3.3 copy-start.16
  354.7 32.8 %copy-start.20 = (f32[2,256,384]{2,1,0:T(8,128)S(1)}, f32[2,256,384]{2,1,0:T(8,128)}, u32[]{:S(2)}) copy-start(f32[2,256,384]{2,1,0:T(8,128)} %get-tuple-element.54) | copy-start | bytes 2359300
  387.5 4.5 copy-start.10
  387.5 2.7 copy-start.7
  387.5 2.7 copy-start.9
  391.9 2.2 copy-start.22
  395.2 4.4 copy-start.5
  496.0 0.7 copy-start.21
  571.0 3.1 copy-start.3
  574.1 3.9 copy-start.4
  579.8 14.1 %copy-start.1 = (bf16[1120,1536]{1,0:T(8,128)(2,1)S(1)}, bf16[1120,1536]{1,0:T(8,128)(2,1)}, u32[]{:S(2)}) copy-start(bf16[1120,1536]{1,0:T(8,128)(2,1)} %param.18) | copy-start | bytes 10321924
Sparse Core Ops, SparseCore 0:
  9.6 25.7 all-gather.10
  153.8 19.6 all-gather.6
  181.7 28.0 reduce-scatter.1
  330.7 139.1 all-gather.8
